TPU v7x, 32 devices: a whole 2x2x4 slice. The times are simulated.
32 devices in a mesh: dp: 8 (over z, core), tensor: 4 (over y, x).
Axes of the slice: x: 2, y: 2, z: 4, core: 2. Of those that a mesh axis runs over, the one named last changes fastest.
Arguments:
- token_ids: int32 [8, 1024], P('dp', 'tensor'), may hold values from 0 to 30527
- lengths: int32 [8], P('dp'), may hold values from 256 to 1024, as said below
- teacher_bins: int32 [8], P('dp'), may hold values from 0 to 127
- embed_table: bfloat16 [30528, 1024], P('tensor'), may hold values from -6 to 6
- query_key_value_matrix: bfloat16 [1024, 3, 1024], P('dp', None, 'tensor'), may hold values from -2 to 2
- output_matrix: bfloat16 [1024, 1024], P('tensor', 'dp'), may hold values from -0.1875 to 0.1875
- up_matrix: bfloat16 [1024, 4096], P('dp', 'tensor'), may hold values from -0.1875 to 0.1875
- down_matrix: bfloat16 [4096, 1024], P('tensor', 'dp'), may hold values from -0.09375 to 0.09375
- w_head: bfloat16 [1024, 128], P('dp'), may hold values from -64 to 64
Outputs:
- loss: float32 [], replicated
- query_key_value_gradient: float32 [1024, 3, 1024], P('dp', None, 'tensor')
- output_weight_gradient: float32 [1024, 1024], P('tensor', 'dp')
- up_weight_gradient: float32 [1024, 4096], P('dp', 'tensor')
- down_weight_gradient: float32 [4096, 1024], P('tensor', 'dp')
- grad_head: float32 [1024, 128], P('dp')
Inputs may be any that keep to these rules, and one draw needn't show every extreme that they name: lengths[0] is 1024.
All inputs are finite; a program needn't handle non-finite values.
Results may differ from a plain program's by a relative error of at most 0.02.
Values may be sent and summed in bfloat16 or wider, within the bound.
A program may use at most 128 MiB of HBM per device.

v0:
```python
import functools

import jax
import jax.numpy as jnp
from jax import lax
from jax.experimental import pallas as pl
from jax.experimental.pallas import tpu as pltpu
from jax.sharding import PartitionSpec as P

HEAD_WIDTH = 64
EPS = 1e-05
BF = jnp.bfloat16
F32 = jnp.float32
MESH = pl.DeviceIdType.MESH
VMEM = pltpu.VMEM
BIG = 60 * 1024 * 1024


def normalize(values):
    mean = jnp.mean(values, axis=-1, keepdims=True)
    centered = values - mean
    return centered * lax.rsqrt(jnp.mean(centered * centered, axis=-1, keepdims=True) + EPS)


def vmem_spec():
    return pl.BlockSpec(memory_space=pltpu.VMEM)


def greet(axis, count):
    me = lax.axis_index(axis)
    barrier = pltpu.get_barrier_semaphore()
    for step in range(1, count):
        pl.semaphore_signal(
            barrier, inc=1, device_id={axis: lax.rem(me + step, count)}, device_id_type=MESH
        )
    pl.semaphore_wait(barrier, count - 1)
    return me


def gather_body(axis, count, x_ref, out_ref, send_sem, recv_sem):
    me = greet(axis, count)
    copies = []
    for step in range(1, count):
        copy = pltpu.make_async_remote_copy(
            src_ref=x_ref,
            dst_ref=out_ref.at[me],
            send_sem=send_sem.at[step - 1],
            recv_sem=recv_sem.at[step - 1],
            device_id={axis: lax.rem(me + step, count)},
            device_id_type=MESH,
        )
        copy.start()
        copies.append(copy)
    out_ref[me] = x_ref[...]
    for copy in copies:
        copy.wait()


def relay_gather(axis, me, src, out, send_sem, recv_sem):
    across = me + 1 - 2 * lax.rem(me, 2)
    over = lax.rem(me + 2, 4)
    half = src.shape[0] // 2
    low, high = pl.ds(0, half), pl.ds(half, half)

    def copy(index, src_part, block, part, device):
        return pltpu.make_async_remote_copy(
            src_ref=src_part,
            dst_ref=out.at[block, part],
            send_sem=send_sem.at[index],
            recv_sem=recv_sem.at[index],
            device_id={axis: device},
            device_id_type=MESH,
        )

    first_a = copy(0, src.at[low], me, low, across)
    first_b = copy(1, src.at[high], me, high, over)
    second_a = copy(2, src.at[high], me, high, across)
    second_b = copy(3, src.at[low], me, low, over)
    for one in (first_a, first_b, second_a, second_b):
        one.start()
    first_a.wait_recv()
    pass_b = copy(4, out.at[across, low], across, low, over)
    pass_b.start()
    first_b.wait_recv()
    pass_a = copy(5, out.at[over, high], over, high, across)
    pass_a.start()
    second_a.wait_recv()
    second_b.wait_recv()
    pass_b.wait_recv()
    pass_a.wait_recv()
    for one in (first_a, first_b, second_a, second_b, pass_b, pass_a):
        one.wait_send()


def relay_body(axis, x_ref, out_ref, send_sem, recv_sem):
    me = greet(axis, 4)
    relay_gather(axis, me, x_ref, out_ref, send_sem, recv_sem)
    out_ref[me] = x_ref[...]


def gather_blocks(x, axis, count, ident):
    if count != 4:
        return gather_all(x, axis, count, ident)
    return pl.pallas_call(
        functools.partial(relay_body, axis),
        out_shape=jax.ShapeDtypeStruct((count,) + x.shape, x.dtype),
        in_specs=[vmem_spec()],
        out_specs=vmem_spec(),
        scratch_shapes=[pltpu.SemaphoreType.DMA((6,)), pltpu.SemaphoreType.DMA((6,))],
        compiler_params=pltpu.CompilerParams(collective_id=ident, has_side_effects=True),
        name="gather_blocks",
    )(x)


def gather_all(x, axis, count, ident):
    return pl.pallas_call(
        functools.partial(gather_body, axis, count),
        out_shape=jax.ShapeDtypeStruct((count,) + x.shape, x.dtype),
        in_specs=[vmem_spec()],
        out_specs=vmem_spec(),
        scratch_shapes=[
            pltpu.SemaphoreType.DMA((count - 1,)),
            pltpu.SemaphoreType.DMA((count - 1,)),
        ],
        compiler_params=pltpu.CompilerParams(collective_id=ident, has_side_effects=True),
        name="gather_all",
    )(x)


def scatter_copies(axis, count, me, x_ref, held, send_sem, recv_sem):
    copies = []
    for step in range(1, count):
        peer = lax.rem(me + step, count)
        copies.append(
            pltpu.make_async_remote_copy(
                src_ref=x_ref.at[peer],
                dst_ref=held.at[step - 1],
                send_sem=send_sem.at[step - 1],
                recv_sem=recv_sem.at[step - 1],
                device_id={axis: peer},
                device_id_type=MESH,
            )
        )
    return copies


def scatter_start(*args):
    for copy in scatter_copies(*args):
        copy.start()


def scatter_finish(axis, count, me, x_ref, held, send_sem, recv_sem, put):
    for copy in scatter_copies(axis, count, me, x_ref, held, send_sem, recv_sem):
        copy.wait()

    def body(at):
        total = x_ref[me, at].astype(F32)
        for step in range(1, count):
            total = total + held[step - 1, at].astype(F32)
        put(at, total)

    add_tiles(x_ref.shape[1], 32, body)


def add_tiles(rows, tile, body):
    def step(index, carry):
        body(pl.ds(pl.multiple_of(index * tile, tile), tile))
        return carry

    lax.fori_loop(0, rows // tile, step, 0)


class GroupSum:
    def __init__(self, x_ref, out_ref, pair, mine, far, sems):
        self.x, self.out, self.pair, self.mine, self.far = x_ref, out_ref, pair, mine, far
        self.sems = sems
        self.groups = x_ref.shape[0]
        self.chips = self.groups // 2
        self.rows = x_ref.shape[1]
        me = lax.axis_index("dp")
        self.core = lax.rem(me, 2)
        self.chip = me // 2
        self.near = self.chip * 2 + 1 - self.core

    @staticmethod
    def scratch(shape, dtype):
        groups, rows, columns = shape
        chips = groups // 2
        return [
            VMEM((chips, rows, columns), dtype),
            VMEM((chips, rows, columns), dtype),
            VMEM((chips - 1, rows, columns), dtype),
            pltpu.SemaphoreType.DMA((chips,)),
            pltpu.SemaphoreType.DMA((chips,)),
            pltpu.SemaphoreType.DMA((6 if chips == 4 else chips - 1,)),
            pltpu.SemaphoreType.DMA((6 if chips == 4 else chips - 1,)),
        ]

    def signal(self, barrier):
        pl.semaphore_signal(
            barrier, inc=1, device_id={"dp": self.near}, device_id_type=MESH
        )
        for step in range(1, self.chips):
            pl.semaphore_signal(
                barrier, inc=1, device_id={"dp": self.owner(step)}, device_id_type=MESH
            )
        return self.chips

    def owner(self, step):
        return lax.rem(self.chip + step, self.chips) * 2 + self.core

    def pair_copies(self):
        copies = []
        for chip in range(self.chips):
            copies.append(
                pltpu.make_async_remote_copy(
                    src_ref=self.x.at[chip * 2 + 1 - self.core],
                    dst_ref=self.pair.at[chip],
                    send_sem=self.sems[0].at[chip],
                    recv_sem=self.sems[1].at[chip],
                    device_id={"dp": self.near},
                    device_id_type=MESH,
                )
            )
        return copies

    def far_copies(self):
        copies = []
        for step in range(1, self.chips):
            copies.append(
                pltpu.make_async_remote_copy(
                    src_ref=self.mine.at[lax.rem(self.chip + step, self.chips)],
                    dst_ref=self.far.at[step - 1],
                    send_sem=self.sems[2].at[step - 1],
                    recv_sem=self.sems[3].at[step - 1],
                    device_id={"dp": self.owner(step)},
                    device_id_type=MESH,
                )
            )
        return copies

    def ring_copies(self):
        right, left = lax.rem(self.chip + 1, 4), lax.rem(self.chip + 3, 4)
        opposite = lax.rem(self.chip + 2, 4)
        half = self.rows // 2
        low, high = pl.ds(0, half), pl.ds(half, half)

        def copy(index, block, part, slot, chip):
            return pltpu.make_async_remote_copy(
                src_ref=self.mine.at[block, part],
                dst_ref=self.far.at[slot, part],
                send_sem=self.sems[2].at[index],
                recv_sem=self.sems[3].at[index],
                device_id={"dp": chip * 2 + self.core},
                device_id_type=MESH,
            )

        return (
            copy(0, opposite, low, 2, right),
            copy(1, opposite, high, 2, left),
            copy(2, right, high, 0, right),
            copy(3, left, low, 1, left),
            copy(4, right, low, 0, right),
            copy(5, left, high, 1, left),
        )

    def relay(self):
        if self.chips != 4:
            return
        copies = self.ring_copies()
        half = self.rows // 2
        for index, step, base in ((0, 1, 0), (1, 3, half)):
            copies[index].wait_recv()
            block = lax.rem(self.chip + step, 4)

            def body(at, block=block, base=base):
                here = pl.ds(base + at.start, at.size)
                self.mine[block, here] = (
                    self.mine[block, here].astype(F32) + self.far[2, here].astype(F32)
                ).astype(self.mine.dtype)

            add_tiles(half, 32, body)
            copies[index + 4].start()

    def start(self):
        for copy in self.pair_copies():
            copy.start()

    def middle(self):
        for copy in self.pair_copies():
            copy.wait()

        for chip in range(self.chips):

            def body(at, chip=chip):
                self.mine[chip, at] = (
                    self.x[chip * 2 + self.core, at].astype(F32)
                    + self.pair[chip, at].astype(F32)
                ).astype(self.mine.dtype)

            add_tiles(self.rows, 32, body)
        copies = self.ring_copies()[:4] if self.chips == 4 else self.far_copies()
        for copy in copies:
            copy.start()

    def finish(self):
        if self.chips == 4:
            copies = self.ring_copies()
            for copy in copies[2:]:
                copy.wait()
            for copy in copies[:2]:
                copy.wait_send()
        else:
            for copy in self.far_copies():
                copy.wait()

        def body(at):
            total = self.mine[self.chip, at].astype(F32)
            for step in range(2 if self.chips == 4 else self.chips - 1):
                total = total + self.far[step, at].astype(F32)
            self.out[at] = total

        add_tiles(self.rows, 32, body)


def scatter_and_group_body(
    count, x_ref, up_ref, small_ref, out_ref, up_out, small_out, held, send_sem, recv_sem, *rest
):
    up = GroupSum(up_ref, up_out, rest[0], rest[1], rest[2], rest[3:7])
    small_send, small_recv = rest[7:]
    groups = small_out.shape[0]
    group = lax.axis_index("dp")
    barrier = pltpu.get_barrier_semaphore()
    me = lax.axis_index("tensor")
    for step in range(1, count):
        pl.semaphore_signal(
            barrier, inc=1, device_id={"tensor": lax.rem(me + step, count)}, device_id_type=MESH
        )
    for step in range(1, groups):
        pl.semaphore_signal(
            barrier, inc=1, device_id={"dp": lax.rem(group + step, groups)}, device_id_type=MESH
        )
    pl.semaphore_wait(barrier, count + groups - 2)
    smalls = []
    for step in range(1, groups):
        smalls.append(
            pltpu.make_async_remote_copy(
                src_ref=small_ref,
                dst_ref=small_out.at[group],
                send_sem=small_send.at[step - 1],
                recv_sem=small_recv.at[step - 1],
                device_id={"dp": lax.rem(group + step, groups)},
                device_id_type=MESH,
            )
        )

    def put(at, total):
        out_ref[at] = total.astype(out_ref.dtype)

    up.start()
    scatter_start("tensor", count, me, x_ref, held, send_sem, recv_sem)
    up.middle()
    for copy in smalls:
        copy.start()
    small_out[group] = small_ref[...]
    up.relay()
    scatter_finish("tensor", count, me, x_ref, held, send_sem, recv_sem, put)
    up.finish()
    for copy in smalls:
        copy.wait()


def scatter_and_group(x, up, small, count, ident):
    return pl.pallas_call(
        functools.partial(scatter_and_group_body, count),
        out_shape=(
            jax.ShapeDtypeStruct(x.shape[1:], x.dtype),
            jax.ShapeDtypeStruct(up.shape[1:], F32),
            jax.ShapeDtypeStruct(up.shape[:1] + small.shape, F32),
        ),
        in_specs=[vmem_spec()] * 3,
        out_specs=(vmem_spec(),) * 3,
        scratch_shapes=[
            VMEM((count - 1,) + x.shape[1:], x.dtype),
            pltpu.SemaphoreType.DMA((count - 1,)),
            pltpu.SemaphoreType.DMA((count - 1,)),
        ]
        + GroupSum.scratch(up.shape, up.dtype)
        + [pltpu.SemaphoreType.DMA((up.shape[0] - 1,))] * 2,
        compiler_params=pltpu.CompilerParams(
            collective_id=ident, has_side_effects=True, vmem_limit_bytes=BIG
        ),
        name="scatter_and_group",
    )(x, up, small)


def group_sum_body(number, *refs):
    xs, outs, rest = refs[:number], refs[number : 2 * number], refs[2 * number :]
    sums = [
        GroupSum(x, out, *rest[7 * i : 7 * i + 3], rest[7 * i + 3 : 7 * i + 7])
        for i, (x, out) in enumerate(zip(xs, outs))
    ]
    barrier = pltpu.get_barrier_semaphore()
    pl.semaphore_wait(barrier, sums[0].signal(barrier))
    for one in sums:
        one.start()
    for one in sums:
        one.middle()
    for one in sums:
        one.relay()
    for one in sums:
        one.finish()


def group_sum(arrays, ident):
    number = len(arrays)
    scratch = []
    for array in arrays:
        scratch += GroupSum.scratch(array.shape, array.dtype)
    return pl.pallas_call(
        functools.partial(group_sum_body, number),
        out_shape=tuple(jax.ShapeDtypeStruct(a.shape[1:], F32) for a in arrays),
        in_specs=[vmem_spec()] * number,
        out_specs=(vmem_spec(),) * number,
        scratch_shapes=scratch,
        compiler_params=pltpu.CompilerParams(
            collective_id=ident, has_side_effects=True, vmem_limit_bytes=BIG
        ),
        name="group_sum",
    )(*arrays)


def sum_all_body(axis, count, x_ref, out_ref, held, send_sem, recv_sem, send_two, recv_two):
    me = greet(axis, count)

    def put(at, total):
        out_ref[me, at] = total.astype(out_ref.dtype)

    scatter_start(axis, count, me, x_ref, held, send_sem, recv_sem)
    scatter_finish(axis, count, me, x_ref, held, send_sem, recv_sem, put)
    if count == 4:
        relay_gather(axis, me, out_ref.at[me], out_ref, send_two, recv_two)
        return
    copies = []
    for step in range(1, count):
        copy = pltpu.make_async_remote_copy(
            src_ref=out_ref.at[me],
            dst_ref=out_ref.at[me],
            send_sem=send_two.at[step - 1],
            recv_sem=recv_two.at[step - 1],
            device_id={axis: lax.rem(me + step, count)},
            device_id_type=MESH,
        )
        copy.start()
        copies.append(copy)
    for copy in copies:
        copy.wait()


def sum_all(x, axis, count, ident):
    return pl.pallas_call(
        functools.partial(sum_all_body, axis, count),
        out_shape=jax.ShapeDtypeStruct(x.shape, x.dtype),
        in_specs=[vmem_spec()],
        out_specs=vmem_spec(),
        scratch_shapes=[VMEM((count - 1,) + x.shape[1:], x.dtype)]
        + [pltpu.SemaphoreType.DMA((count - 1,))] * 2
        + [pltpu.SemaphoreType.DMA((6 if count == 4 else count - 1,))] * 2,
        compiler_params=pltpu.CompilerParams(collective_id=ident, has_side_effects=True),
        name="sum_all",
    )(x)


def contract(left, right, dims):
    return lax.dot_general(left, right, ((dims[:1], dims[1:]), ((), ())), preferred_element_type=F32)


def masked_scores(keys, query, length):
    scores = contract(keys, query, (0, 0))
    position = lax.broadcasted_iota(jnp.int32, scores.shape, 0)
    return jnp.where(position < length, scores, -1e30)


def attend_body(chunk, length_ref, qkv_ref, out_ref, lse_ref):
    length = length_ref[0]
    keys, vals = qkv_ref[1], qkv_ref[2]
    scale = HEAD_WIDTH ** (-0.5)
    for at in range(0, qkv_ref.shape[2], chunk):
        query = (qkv_ref[0, :, at : at + chunk].astype(F32) * scale).astype(BF)
        scores = masked_scores(keys, query, length)
        top = jnp.max(scores, axis=0, keepdims=True)
        expo = jnp.exp(scores - top)
        total = jnp.sum(expo, axis=0, keepdims=True)
        mixed = contract(vals, expo.astype(BF), (1, 0))
        out_ref[:, at : at + chunk] = (mixed * (1.0 / total)).astype(BF)
        lse_ref[0, :, at : at + chunk] = top + jnp.log(total)


def attend(qkv, lengths, chunk):
    _, width, length = qkv.shape
    heads = width // HEAD_WIDTH
    return pl.pallas_call(
        functools.partial(attend_body, chunk),
        grid=(heads,),
        out_shape=(
            jax.ShapeDtypeStruct((width, length), BF),
            jax.ShapeDtypeStruct((heads, 1, length), F32),
        ),
        in_specs=[
            pl.BlockSpec(memory_space=pltpu.SMEM),
            pl.BlockSpec((3, HEAD_WIDTH, length), lambda h: (0, h, 0)),
        ],
        out_specs=(
            pl.BlockSpec((HEAD_WIDTH, length), lambda h: (h, 0)),
            pl.BlockSpec((1, 1, length), lambda h: (h, 0, 0)),
        ),
        cost_estimate=pl.CostEstimate(
            flops=4 * width * length * length,
            bytes_accessed=8 * width * length,
            transcendentals=heads * length * length,
        ),
        compiler_params=pltpu.CompilerParams(vmem_limit_bytes=BIG),
        name="attend",
    )(lengths, qkv)


def attend_back_body(
    chunk, ranks, length_ref, qkv_ref, lse_ref, grad_ref, x_ref, out_ref, x_out, held, send_sem, recv_sem
):
    me = lax.axis_index("tensor")
    args = ("tensor", ranks, me, x_ref, held, send_sem, recv_sem)

    @pl.when(pl.program_id(0) == 0)
    def _():
        greet("tensor", ranks)
        scatter_start(*args)

    attend_back_head(chunk, length_ref, qkv_ref, lse_ref, grad_ref, out_ref)

    @pl.when(pl.program_id(0) == pl.num_programs(0) - 1)
    def _():
        piece = x_out.shape[2]

        def put(at, total):
            for group in range(x_out.shape[0]):
                x_out[group, at] = total[:, group * piece : (group + 1) * piece].astype(BF)

        scatter_finish(*args, put)


def attend_back_head(chunk, length_ref, qkv_ref, lse_ref, grad_ref, out_ref):
    length = length_ref[0]
    keys, vals = qkv_ref[1], qkv_ref[2]
    scale = HEAD_WIDTH ** (-0.5)
    span = qkv_ref.shape[2]
    g_keys = jnp.zeros((HEAD_WIDTH, span), F32)
    g_vals = jnp.zeros((HEAD_WIDTH, span), F32)
    for at in range(0, span, chunk):
        here = slice(at, at + chunk)
        query = (qkv_ref[0, :, here].astype(F32) * scale).astype(BF)
        grad = grad_ref[:, here]
        probs = jnp.exp(masked_scores(keys, query, length) - lse_ref[0, :, here])
        g_probs = contract(vals, grad, (0, 0))
        weighted = probs * g_probs
        inner = jnp.sum(weighted, axis=0, keepdims=True)
        g_scores = (weighted - probs * inner).astype(BF)
        out_ref[0, :, here] = (contract(keys, g_scores, (1, 0)) * scale).astype(BF)
        g_keys += contract(query, g_scores, (1, 1))
        g_vals += contract(grad, probs.astype(BF), (1, 1))
    out_ref[1] = g_keys.astype(BF)
    out_ref[2] = g_vals.astype(BF)


def attend_back(qkv, lengths, lse, grad, x, groups, chunk, ident):
    _, width, length = qkv.shape
    heads = width // HEAD_WIDTH
    return pl.pallas_call(
        functools.partial(attend_back_body, chunk, x.shape[0]),
        grid=(heads,),
        out_shape=(
            jax.ShapeDtypeStruct(qkv.shape, BF),
            jax.ShapeDtypeStruct((groups, x.shape[1], x.shape[2] // groups), BF),
        ),
        in_specs=[
            pl.BlockSpec(memory_space=pltpu.SMEM),
            pl.BlockSpec((3, HEAD_WIDTH, length), lambda h: (0, h, 0)),
            pl.BlockSpec((1, 1, length), lambda h: (h, 0, 0)),
            pl.BlockSpec((HEAD_WIDTH, length), lambda h: (h, 0)),
            vmem_spec(),
        ],
        out_specs=(
            pl.BlockSpec((3, HEAD_WIDTH, length), lambda h: (0, h, 0)),
            vmem_spec(),
        ),
        scratch_shapes=[
            VMEM((x.shape[0] - 1,) + x.shape[1:], x.dtype),
            pltpu.SemaphoreType.DMA((x.shape[0] - 1,)),
            pltpu.SemaphoreType.DMA((x.shape[0] - 1,)),
        ],
        cost_estimate=pl.CostEstimate(
            flops=10 * width * length * length,
            bytes_accessed=14 * width * length,
            transcendentals=heads * length * length,
        ),
        compiler_params=pltpu.CompilerParams(
            collective_id=ident, has_side_effects=True, vmem_limit_bytes=BIG
        ),
        name="attend_back",
    )(lengths, qkv, lse, grad, x)


def hidden_body(length_ref, normed_ref, up_ref, slope_ref, sum_ref):
    pre = jnp.dot(normed_ref[...], up_ref[...], preferred_element_type=F32)
    live = lax.broadcasted_iota(jnp.int32, pre.shape, 0) < length_ref[0]
    square = pre * pre
    bend = jnp.tanh(0.7978845608028654 * (pre * (1.0 + 0.044715 * square)))
    half = 0.5 * (1.0 + bend)
    act = (pre * half).astype(BF).astype(F32)
    sum_ref[...] = jnp.sum(jnp.where(live, act, 0.0), axis=0, keepdims=True)
    inner = 0.7978845608028654 * (1.0 + 3 * 0.044715 * square)
    slope = half + 0.5 * pre * (1.0 - bend * bend) * inner
    slope_ref[...] = jnp.where(live, slope, 0.0).astype(BF)


def hidden(normed, up, lengths, chunk):
    length, width = normed.shape
    units = up.shape[1]
    return pl.pallas_call(
        hidden_body,
        grid=(units // chunk,),
        out_shape=(
            jax.ShapeDtypeStruct((length, units), BF),
            jax.ShapeDtypeStruct((1, units), F32),
        ),
        in_specs=[
            pl.BlockSpec(memory_space=pltpu.SMEM),
            pl.BlockSpec((length, width), lambda f: (0, 0)),
            pl.BlockSpec((width, chunk), lambda f: (0, f)),
        ],
        out_specs=(
            pl.BlockSpec((length, chunk), lambda f: (0, f)),
            pl.BlockSpec((1, chunk), lambda f: (0, f)),
        ),
        cost_estimate=pl.CostEstimate(
            flops=2 * length * width * units,
            bytes_accessed=6 * length * units,
            transcendentals=length * units,
        ),
        compiler_params=pltpu.CompilerParams(vmem_limit_bytes=BIG),
        name="hidden",
    )(lengths, normed, up)


def per_device(
    token_ids,
    lengths,
    teacher_bins,
    embed_table,
    query_key_value_matrix,
    output_matrix,
    up_matrix,
    down_matrix,
    w_head,
):
    ranks = lax.axis_size("tensor")
    groups = lax.axis_size("dp")
    rank = lax.axis_index("tensor")
    group = lax.axis_index("dp")
    assert token_ids.shape[0] == 1
    local_len = token_ids.shape[1]
    span = local_len * ranks
    vocab_local, width = embed_table.shape
    d_local, _, e_local = query_key_value_matrix.shape
    f_local = up_matrix.shape[1]
    bins = w_head.shape[1]
    exact = lax.Precision.HIGHEST

    qkv_full = lax.all_gather(
        query_key_value_matrix.reshape(d_local, 3 * e_local), "dp", axis=0, tiled=True
    )
    out_parts = lax.all_gather(output_matrix, ("tensor", "dp"), axis=0, tiled=False)
    out_full = (
        out_parts.reshape(ranks, groups, e_local, d_local)
        .transpose(0, 2, 1, 3)
        .reshape(ranks * e_local, width)
    )
    up_full = lax.all_gather(up_matrix, "dp", axis=0, tiled=True)
    low = lax.all_gather(
        jnp.concatenate([down_matrix, w_head.reshape(bins, d_local)], axis=0), "dp", axis=0, tiled=False
    )
    down_full = low[:, :f_local]
    head_wide = low[:, f_local:].reshape(width, bins).astype(F32)

    all_ids = gather_all(token_ids, "tensor", ranks, 1).reshape(ranks, local_len)
    shifted = all_ids - rank * vocab_local
    inside = (shifted >= 0) & (shifted < vocab_local)
    rows = jnp.take(embed_table, jnp.clip(shifted, 0, vocab_local - 1), axis=0)
    first = sum_all(
        jnp.where(inside[..., None], rows, jnp.zeros((), BF)), "tensor", ranks, 2
    ).reshape(span, width)
    normed_one = normalize(first.astype(F32)).astype(BF)
    qkv = (
        lax.dot_general(qkv_full, normed_one, (((0,), (1,)), ((), ())), preferred_element_type=F32)
        .astype(BF)
        .reshape(3, e_local, span)
    )
    chunk = min(256, span)
    context, lse = attend(qkv, lengths, chunk)
    context_all = gather_blocks(context, "tensor", ranks, 3).reshape(ranks * e_local, span)
    attn = lax.dot_general(
        context_all, out_full, (((0,), (0,)), ((), ())), preferred_element_type=F32
    )
    second = (first.astype(F32) + attn).astype(BF)
    normed_f, norm_back = jax.vjp(normalize, second.astype(F32))
    normed_two = normed_f.astype(BF)
    slope, hidden_sum = hidden(normed_two, up_full, lengths, min(256, f_local))

    live = (jnp.arange(span, dtype=jnp.int32) < lengths[0]).astype(F32)
    count = lengths.astype(F32)[:, None]
    ffn_part = jnp.einsum(
        "of,jfd->ojd", hidden_sum, down_full.astype(F32), precision=exact
    ).reshape(1, width)
    ffn_all = gather_all(ffn_part, "tensor", ranks, 4)
    second_sum = jnp.sum(second.astype(F32) * live[:, None], axis=0, keepdims=True)
    pooled = (second_sum + jnp.sum(ffn_all, axis=0)) / count
    final, final_back = jax.vjp(normalize, pooled)
    logits = jnp.dot(final, head_wide, precision=exact)
    top = jnp.max(logits, axis=-1, keepdims=True)
    total_exp = jnp.log(jnp.sum(jnp.exp(logits - top), axis=-1, keepdims=True)) + top
    labels = (teacher_bins[:, None] == jnp.arange(bins, dtype=jnp.int32)[None, :]).astype(F32)
    loss_here = total_exp - jnp.sum(logits * labels, axis=-1, keepdims=True)
    g_logits = (jnp.exp(logits - total_exp) - labels) / groups
    g_final = jnp.dot(g_logits, head_wide.T, precision=exact)
    per_token = final_back(g_final)[0] / count
    rounded = per_token.astype(BF).astype(F32)
    g_hidden = jnp.einsum(
        "ojd,jfd->of",
        rounded.reshape(1, groups, d_local),
        down_full.astype(F32),
        precision=exact,
    )

    packed = jnp.concatenate(
        [hidden_sum, rounded, final, g_logits, jnp.broadcast_to(loss_here, (1, 128))], axis=1
    )

    over_seqs = (((0,), (0,)), ((), ()))
    up_base = lax.dot_general(normed_two, slope, over_seqs, preferred_element_type=F32)
    up_term = (up_base * g_hidden).astype(BF).reshape(groups, d_local, f_local)
    g_pre = (slope.astype(F32) * g_hidden).astype(BF)
    g_normed = lax.dot_general(
        g_pre, up_full, (((1,), (1,)), ((), ())), preferred_element_type=F32
    )
    g_second = (
        norm_back(g_normed)[0] + live[:, None] * (per_token / ranks)
    ).astype(BF)
    spread = lax.dot_general(
        out_full, g_second, (((1,), (1,)), ((), ())), preferred_element_type=F32
    ).astype(BF)
    g_context, up_weight_gradient, every = scatter_and_group(
        spread.reshape(ranks, e_local, span), up_term, packed, ranks, 6
    )
    every = every[:, 0]
    hidden_every = every[:, :f_local]
    rounded_every = every[:, f_local : f_local + width]
    final_every = every[:, f_local + width : f_local + 2 * width]
    rest = every[:, f_local + 2 * width :]
    loss = jnp.sum(rest[:, bins]) / groups
    mine = group * d_local
    down_weight_gradient = lax.dot_general(
        hidden_every,
        lax.dynamic_slice_in_dim(rounded_every, mine, d_local, axis=1),
        over_seqs,
        precision=exact,
    )
    grad_head = lax.dot_general(
        lax.dynamic_slice_in_dim(final_every, mine, d_local, axis=1),
        rest[:, :bins],
        over_seqs,
        precision=exact,
    )

    out_term = (
        jnp.dot(context_all, g_second, preferred_element_type=F32)
        .astype(BF)
        .reshape(ranks, e_local, width)
    )
    g_qkv, out_mine = attend_back(qkv, lengths, lse, g_context, out_term, groups, chunk, 7)
    qkv_term = lax.dot_general(
        normed_one,
        g_qkv.reshape(3 * e_local, span),
        (((0,), (1,)), ((), ())),
        preferred_element_type=F32,
    )
    qkv_gradient, output_weight_gradient = group_sum(
        [qkv_term.astype(BF).reshape(groups, d_local, 3 * e_local), out_mine], 8
    )
    query_key_value_gradient = qkv_gradient.reshape(d_local, 3, e_local)
    return (
        loss,
        query_key_value_gradient,
        output_weight_gradient,
        up_weight_gradient,
        down_weight_gradient,
        grad_head,
    )


def remote(src, dst, sems, index, device):
    return pltpu.make_async_remote_copy(
        src_ref=src,
        dst_ref=dst,
        send_sem=sems[0].at[index],
        recv_sem=sems[1].at[index],
        device_id=device,
        device_id_type=MESH,
    )


class Place:
    def __init__(self):
        self.rank = lax.axis_index("tensor")
        self.across = self.rank + 1 - 2 * lax.rem(self.rank, 2)
        self.over = lax.rem(self.rank + 2, 4)
        self.diag = 3 - self.rank
        self.group = lax.axis_index("dp")
        self.core = lax.rem(self.group, 2)
        self.chip = self.group // 2
        self.near = self.chip * 2 + 1 - self.core

    def turn(self, step):
        return lax.rem(self.chip + step, 4)

    def same(self, chip):
        return chip * 2 + self.core

    def greet(self, tensor, dp, everyone=False):
        barrier = pltpu.get_barrier_semaphore()
        peers = []
        if tensor:
            peers += [{"tensor": one} for one in (self.across, self.over, self.diag)]
        if everyone:
            peers += [{"dp": lax.rem(self.group + step, 8)} for step in range(1, 8)]
        elif dp:
            peers += [
                {"dp": self.near},
                {"dp": self.same(self.turn(1))},
                {"dp": self.same(self.turn(3))},
            ]
        for peer in peers:
            pl.semaphore_signal(barrier, inc=1, device_id=peer, device_id_type=MESH)
        pl.semaphore_wait(barrier, len(peers))


class RingGather:
    def __init__(self, at, src, own, slot, sems):
        self.at, self.src, self.own, self.slot = at, src, own, slot
        self.sems, self.local = sems[:2], sems[2]

    @staticmethod
    def scratch():
        return [
            pltpu.SemaphoreType.DMA((10,)),
            pltpu.SemaphoreType.DMA((10,)),
            pltpu.SemaphoreType.DMA((1,)),
        ]

    def copies(self):
        at = self.at
        right, left, far = at.turn(1), at.turn(3), at.turn(2)
        me, to_right, to_left = at.group, {"dp": at.same(right)}, {"dp": at.same(left)}
        near = {"dp": at.near}

        def held(index, chip, half, device):
            ref = self.slot(at.same(chip), half)
            return remote(ref, ref, self.sems, index, device)

        def first(index, half, device):
            return remote(self.own(half), self.slot(me, half), self.sems, index, device)

        return (
            first(0, 0, to_right),
            first(1, 1, to_left),
            first(2, 1, to_right),
            first(3, 0, to_left),
            held(4, left, 0, to_right),
            held(5, right, 1, to_left),
            remote(self.src, self.slot(me, None), self.sems, 6, near),
            held(7, left, None, near),
            held(8, right, None, near),
            held(9, far, None, near),
        )

    def keep(self):
        return pltpu.make_async_copy(self.src, self.slot(self.at.group, None), self.local.at[0])

    def start(self):
        copies = self.copies()
        for index in (0, 1, 2, 3, 6):
            copies[index].start()
        self.keep().start()

    def relay(self):
        copies = self.copies()
        copies[0].wait_recv()
        copies[4].start()
        copies[1].wait_recv()
        copies[5].start()

    def spread(self):
        copies = self.copies()
        copies[2].wait_recv()
        copies[7].start()
        copies[3].wait_recv()
        copies[8].start()
        copies[4].wait_recv()
        copies[5].wait_recv()
        copies[9].start()

    def finish(self):
        copies = self.copies()
        for index in (6, 7, 8, 9):
            copies[index].wait_recv()
        for copy in copies:
            copy.wait_send()
        self.keep().wait()


def rows_of(ref, block, half, size, axis=0):
    lead = (slice(None),) * axis
    if half is None:
        return ref.at[lead + (pl.ds(pl.multiple_of(block * size, size), size),)]
    part = size // 2
    return ref.at[lead + (pl.ds(pl.multiple_of(block * size + half * part, part), part),)]


def half_rows(ref, half, axis=0):
    part = ref.shape[axis] // 2
    return ref.at[(slice(None),) * axis + (pl.ds(half * part, part),)]


def ids_body(ids_ref, out_ref, ids_all, out_all, send, recv):
    at = Place()
    at.greet(True, False)
    copies = []
    for index, peer in enumerate((at.across, at.over, at.diag)):
        copies.append(
            remote(ids_ref, ids_all.at[at.rank], (send, recv), index, {"tensor": peer})
        )
    for index, peer in enumerate((at.across, at.over, at.diag)):
        copies.append(
            remote(out_ref, out_all.at[at.rank], (send, recv), 3 + index, {"tensor": peer})
        )
    for copy in copies:
        copy.start()
    ids_all[at.rank] = ids_ref[...]
    out_all[at.rank] = out_ref[...]
    for copy in copies:
        copy.wait()


def share_ids(ids, out, ident):
    return pl.pallas_call(
        ids_body,
        out_shape=(
            jax.ShapeDtypeStruct((4,) + ids.shape, ids.dtype),
            jax.ShapeDtypeStruct((4,) + out.shape, out.dtype),
        ),
        in_specs=[vmem_spec()] * 2,
        out_specs=(vmem_spec(),) * 2,
        scratch_shapes=[pltpu.SemaphoreType.DMA((6,))] * 2,
        compiler_params=pltpu.CompilerParams(collective_id=ident, has_side_effects=True),
        name="share_ids",
    )(ids, out)


def any_spec():
    return pl.BlockSpec(memory_space=pl.ANY)


class Stream:
    def __init__(self, at, x_ref, acc, held, last, whole, sems, index, rows, x_first):
        self.at, self.x, self.acc, self.held, self.last, self.whole = at, x_ref, acc, held, last, whole
        self.sems, self.index, self.rows = sems, index * 6, rows
        self.one, self.two = (at.across, at.over) if x_first else (at.over, at.across)

    def copies(self):
        at, rows, base, sems = self.at, self.rows, self.index, self.sems
        one, two = {"tensor": self.one}, {"tensor": self.two}
        return (
            remote(self.x.at[at.diag, rows], self.held.at[1, rows], sems, base, one),
            remote(self.x.at[self.one, rows], self.held.at[0, rows], sems, base + 1, one),
            remote(self.acc.at[rows], self.last.at[rows], sems, base + 2, two),
            remote(self.whole.at[at.rank, rows], self.whole.at[at.rank, rows], sems, base + 3, two),
            remote(self.whole.at[at.rank, rows], self.whole.at[at.rank, rows], sems, base + 4, one),
            remote(self.whole.at[self.two, rows], self.whole.at[self.two, rows], sems, base + 5, one),
        )

    def start(self):
        copies = self.copies()
        copies[0].start()
        copies[1].start()

    def second(self):
        copies = self.copies()
        copies[0].wait_recv()

        def body(at):
            here = pl.ds(self.rows.start + at.start, at.size)
            self.acc[here] = self.x[self.two, here] + self.held[1, here]

        add_tiles(self.rows.size, 32, body)
        copies[2].start()

    def third(self):
        copies = self.copies()
        copies[1].wait_recv()
        copies[2].wait_recv()

        def body(at):
            here = pl.ds(self.rows.start + at.start, at.size)
            self.whole[self.at.rank, here] = (
                self.x[self.at.rank, here] + self.held[0, here] + self.last[here]
            )

        add_tiles(self.rows.size, 32, body)
        copies[3].start()
        copies[4].start()

    def relay(self):
        copies = self.copies()
        copies[3].wait_recv()
        copies[5].start()

    def beside(self):
        self.copies()[4].wait_recv()

    def opposite(self):
        self.copies()[5].wait_recv()

    def finish(self):
        for copy in self.copies():
            copy.wait_send()


def embed_body(
    x_ref, w_ref, up_ref, first_out, normed_out, qkv_ref, up_out,
    acc, held, last, whole, normed, w_full, w_turn, send, recv, saved, *rest,
):
    at = Place()
    at.greet(True, True)
    d_local = w_ref.shape[1]
    local = x_ref.shape[1]
    weights = RingGather(
        at, w_ref, lambda half: half_rows(w_ref, half, 1),
        lambda block, half: rows_of(w_full, block, half, d_local, 1), rest[:3],
    )
    ups = RingGather(
        at, up_ref, lambda half: half_rows(up_ref, half),
        lambda block, half: rows_of(up_out, block, half, d_local), rest[3:],
    )
    weights.start()
    part = local // 4
    streams = [
        Stream(
            at, x_ref, acc, held, last, whole, (send, recv), index,
            pl.ds((index % 2) * (local // 2) + (index // 2) * part, part), index % 2 == 0,
        )
        for index in range(4)
    ]
    for one in streams:
        one.start()
    for one in streams:
        one.second()
    weights.relay()
    ups.start()
    for one in streams:
        one.third()
    weights.spread()
    weights.finish()
    for index in range(3):
        w_turn[index] = w_full[index].T

    def project(block, slot):
        def tile(here):
            normed[block, here] = normalize(whole[block, here].astype(F32)).astype(BF)

        add_tiles(local, 32, tile)
        base = pl.multiple_of(block * local, local)

        def matrix(index, carry):
            qkv_ref[index, :, pl.ds(base, local)] = contract(
                w_turn[index], normed[block], (1, 1)
            ).astype(BF)
            return carry

        lax.fori_loop(0, 3, matrix, 0)
        pltpu.make_async_copy(whole.at[block], first_out.at[block], saved.at[slot, 0]).start()
        pltpu.make_async_copy(normed.at[block], normed_out.at[block], saved.at[slot, 1]).start()

    for one in streams[:2]:
        one.relay()
    project(at.rank, 0)
    for one in streams[2:]:
        one.relay()
    ups.relay()
    for one in streams:
        one.beside()
    project(at.across, 1)
    project(at.over, 2)
    ups.spread()
    for one in streams:
        one.opposite()
    project(at.diag, 3)
    ups.finish()
    for one in streams:
        one.finish()
    for slot, block in enumerate((at.rank, at.across, at.over, at.diag)):
        pltpu.make_async_copy(whole.at[block], first_out.at[block], saved.at[slot, 0]).wait()
        pltpu.make_async_copy(normed.at[block], normed_out.at[block], saved.at[slot, 1]).wait()


def embed(x, w, up, ident):
    ranks, local, width = x.shape
    kinds, d_local, e_local = w.shape
    f_local = up.shape[1]
    return pl.pallas_call(
        embed_body,
        out_shape=(
            jax.ShapeDtypeStruct(x.shape, BF),
            jax.ShapeDtypeStruct(x.shape, BF),
            jax.ShapeDtypeStruct((kinds, e_local, ranks * local), BF),
            jax.ShapeDtypeStruct((width, f_local), BF),
        ),
        in_specs=[vmem_spec()] * 3,
        out_specs=(any_spec(), any_spec(), vmem_spec(), any_spec()),
        scratch_shapes=[
            VMEM((local, width), BF),
            VMEM((2, local, width), BF),
            VMEM((local, width), BF),
            VMEM(x.shape, BF),
            VMEM(x.shape, BF),
            VMEM((kinds, width, e_local), BF),
            VMEM((kinds, e_local, width), BF),
            pltpu.SemaphoreType.DMA((24,)),
            pltpu.SemaphoreType.DMA((24,)),
            pltpu.SemaphoreType.DMA((4, 2)),
        ]
        + RingGather.scratch()
        + RingGather.scratch(),
        compiler_params=pltpu.CompilerParams(
            collective_id=ident, has_side_effects=True, vmem_limit_bytes=BIG
        ),
        name="embed",
    )(x, w, up)


def attend_send_body(
    chunk, length_ref, qkv_ref, col_ref, ctx_out, lse_ref, out_full, ctx_ref, saved, send, recv, *rest
):
    at = Place()
    head = pl.program_id(0)
    last = pl.num_programs(0) - 1
    size = HEAD_WIDTH // 2
    d_local = col_ref.shape[1]
    e_rows = col_ref.shape[0]

    def columns(block, half):
        lanes = pl.ds(pl.multiple_of(block * d_local, d_local), d_local)
        if half is None:
            return out_full.at[:, lanes]
        return out_full.at[pl.ds(half * (e_rows // 2), e_rows // 2), lanes]

    outs = RingGather(at, col_ref, lambda half: half_rows(col_ref, half), columns, rest)

    def copies(one):
        def copy(index, block, half, peer):
            ref = ctx_ref.at[block, pl.ds(pl.multiple_of(one * HEAD_WIDTH + half * size, size), size)]
            return pltpu.make_async_remote_copy(
                src_ref=ref,
                dst_ref=ref,
                send_sem=send.at[one, index],
                recv_sem=recv.at[one, index],
                device_id={"tensor": peer},
                device_id_type=MESH,
            )

        return (
            copy(0, at.rank, 0, at.across),
            copy(1, at.rank, 1, at.over),
            copy(2, at.rank, 1, at.across),
            copy(3, at.rank, 0, at.over),
            copy(4, at.across, 0, at.over),
            copy(5, at.over, 1, at.across),
        )

    def relay(one):
        group = copies(one)
        group[0].wait_recv()
        group[4].start()
        group[1].wait_recv()
        group[5].start()

    @pl.when(head == 0)
    def _():
        at.greet(True, True)
        outs.start()

    length = length_ref[0]
    keys, vals = qkv_ref[1], qkv_ref[2]
    scale = HEAD_WIDTH ** (-0.5)
    for start in range(0, qkv_ref.shape[2], chunk):
        here = slice(start, start + chunk)
        query = (qkv_ref[0, :, here].astype(F32) * scale).astype(BF)
        scores = masked_scores(keys, query, length)
        top = jnp.max(scores, axis=0, keepdims=True)
        expo = jnp.exp(scores - top)
        total = jnp.sum(expo, axis=0, keepdims=True)
        mixed = contract(vals, expo.astype(BF), (1, 0))
        ctx_ref[at.rank, pl.ds(pl.multiple_of(head * HEAD_WIDTH, HEAD_WIDTH), HEAD_WIDTH), here] = (
            mixed * (1.0 / total)
        ).astype(BF)
        lse_ref[0, :, here] = top + jnp.log(total)

    @pl.when(head > 0)
    def _():
        relay(head - 1)

    for copy in copies(head)[:4]:
        copy.start()

    @pl.when(head == 1)
    def _():
        outs.relay()

    @pl.when(head == last)
    def _():
        relay(last)
        outs.spread()

        def save(one):
            here = pl.ds(pl.multiple_of(one * HEAD_WIDTH, HEAD_WIDTH), HEAD_WIDTH)
            return pltpu.make_async_copy(ctx_ref.at[:, here], ctx_out.at[:, here], saved.at[one])

        def drain(one, carry):
            group = copies(one)
            for copy in group[2:]:
                copy.wait_recv()
            for copy in group:
                copy.wait_send()
            save(one).start()
            return carry

        lax.fori_loop(0, last + 1, drain, 0)
        outs.finish()

        def store(one, carry):
            save(one).wait()
            return carry

        lax.fori_loop(0, last + 1, store, 0)


def attend_send(qkv, lengths, column, chunk, ident):
    _, width, length = qkv.shape
    heads = width // HEAD_WIDTH
    assert heads > 1
    return pl.pallas_call(
        functools.partial(attend_send_body, chunk),
        grid=(heads,),
        out_shape=(
            jax.ShapeDtypeStruct((4, width, length), BF),
            jax.ShapeDtypeStruct((heads, 1, length), F32),
            jax.ShapeDtypeStruct((column.shape[0], 8 * column.shape[1]), BF),
        ),
        in_specs=[
            pl.BlockSpec(memory_space=pltpu.SMEM),
            pl.BlockSpec((3, HEAD_WIDTH, length), lambda h: (0, h, 0)),
            vmem_spec(),
        ],
        out_specs=(
            any_spec(),
            pl.BlockSpec((1, 1, length), lambda h: (h, 0, 0)),
            any_spec(),
        ),
        scratch_shapes=[VMEM((4, width, length), BF), pltpu.SemaphoreType.DMA((heads,))]
        + [pltpu.SemaphoreType.DMA((heads, 6))] * 2
        + RingGather.scratch(),
        compiler_params=pltpu.CompilerParams(
            collective_id=ident, has_side_effects=True, vmem_limit_bytes=BIG
        ),
        name="attend_send",
    )(lengths, qkv, column)


def exact_dot(row, matrix, dims):
    high = row.astype(BF).astype(F32)
    middle = (row - high).astype(BF).astype(F32)
    low = row - high - middle
    shape = (8, row.shape[1])
    index = lax.broadcasted_iota(jnp.int32, shape, 0)
    stacked = jnp.where(
        index == 0, jnp.broadcast_to(high, shape),
        jnp.where(
            index == 1, jnp.broadcast_to(middle, shape),
            jnp.where(index == 2, jnp.broadcast_to(low, shape), 0.0),
        ),
    ).astype(BF)
    return jnp.sum(contract(stacked, matrix, dims), axis=0, keepdims=True)


def classify_body(
    length_ref, bin_ref, normed_ref, up_ref, base_ref, down_ref, head_ref,
    slope_ref, small_ref, hidden_ref, token_ref,
    sums, down_full, head_full, parts, send, recv, *rest,
):
    at = Place()
    step = pl.program_id(0)
    last = pl.num_programs(0) - 1
    units, width = down_full.shape
    chunk = up_ref.shape[1]
    d_local = down_ref.shape[1]
    bins = head_ref.shape[1]

    def columns(block, half):
        lanes = pl.ds(pl.multiple_of(block * d_local, d_local), d_local)
        if half is None:
            return down_full.at[:, lanes]
        return down_full.at[pl.ds(half * (units // 2), units // 2), lanes]

    downs = RingGather(at, down_ref, lambda half: half_rows(down_ref, half), columns, rest[:3])
    heads = RingGather(
        at, head_ref, lambda half: half_rows(head_ref, half),
        lambda block, half: rows_of(head_full, block, half, d_local), rest[3:],
    )

    @pl.when(step == 0)
    def _():
        at.greet(True, True)
        downs.start()
        heads.start()

    pre = jnp.dot(normed_ref[...], up_ref[...], preferred_element_type=F32)
    live = lax.broadcasted_iota(jnp.int32, pre.shape, 0) < length_ref[0]
    square = pre * pre
    bend = jnp.tanh(0.7978845608028654 * (pre * (1.0 + 0.044715 * square)))
    half = 0.5 * (1.0 + bend)
    act = (pre * half).astype(BF).astype(F32)
    sums[:, pl.ds(pl.multiple_of(step * chunk, chunk), chunk)] = jnp.sum(
        jnp.where(live, act, 0.0), axis=0, keepdims=True
    )
    inner = 0.7978845608028654 * (1.0 + 3 * 0.044715 * square)
    slope = half + 0.5 * pre * (1.0 - bend * bend) * inner
    slope_ref[...] = jnp.where(live, slope, 0.0).astype(BF)

    @pl.when(step == last)
    def _():
        downs.relay()
        heads.relay()
        downs.spread()
        heads.spread()
        downs.finish()
        heads.finish()
        hidden_sum = sums[...]
        parts[at.rank] = exact_dot(hidden_sum, down_full[...], (1, 0))
        copies = [
            remote(parts.at[at.rank], parts.at[at.rank], (send, recv), index, {"tensor": peer})
            for index, peer in enumerate((at.across, at.over, at.diag))
        ]
        for copy in copies:
            copy.start()
        for copy in copies:
            copy.wait()
        count = jnp.full((1, 1), length_ref[0], jnp.int32).astype(F32)
        total = base_ref[...]
        for index in range(4):
            total = total + parts[index]
        pooled = total / count
        mean = jnp.mean(pooled, axis=-1, keepdims=True)
        centered = pooled - mean
        scale = lax.rsqrt(jnp.mean(centered * centered, axis=-1, keepdims=True) + EPS)
        final = centered * scale
        logits = exact_dot(final, head_full[...], (1, 0))
        top = jnp.max(logits, axis=-1, keepdims=True)
        total_exp = jnp.log(jnp.sum(jnp.exp(logits - top), axis=-1, keepdims=True)) + top
        labels = (lax.broadcasted_iota(jnp.int32, logits.shape, 1) == bin_ref[0]).astype(F32)
        loss = total_exp - jnp.sum(logits * labels, axis=-1, keepdims=True)
        g_logits = (jnp.exp(logits - total_exp) - labels) / 8.0
        g_final = exact_dot(g_logits, head_full[...], (1, 1))
        g_pooled = scale * (
            g_final
            - jnp.mean(g_final, axis=-1, keepdims=True)
            - final * jnp.mean(g_final * final, axis=-1, keepdims=True)
        )
        per_token = g_pooled / count
        rounded = per_token.astype(BF)
        token_ref[...] = per_token
        hidden_ref[...] = contract(
            jnp.broadcast_to(rounded.astype(F32), (8, width)).astype(BF), down_full[...], (1, 1)
        )[:1]
        small_ref[:, :units] = hidden_sum
        small_ref[:, units : units + width] = rounded.astype(F32)
        small_ref[:, units + width : units + 2 * width] = final
        small_ref[:, units + 2 * width : units + 2 * width + bins] = g_logits
        small_ref[:, units + 2 * width + bins :] = jnp.broadcast_to(loss, (1, 128))


def classify(normed, up, base, down, head, lengths, bins_at, chunk, ident):
    length, width = normed.shape
    units = up.shape[1]
    bins = head.shape[1]
    return pl.pallas_call(
        classify_body,
        grid=(units // chunk,),
        out_shape=(
            jax.ShapeDtypeStruct((length, units), BF),
            jax.ShapeDtypeStruct((1, units + 2 * width + bins + 128), F32),
            jax.ShapeDtypeStruct((1, units), F32),
            jax.ShapeDtypeStruct((1, width), F32),
        ),
        in_specs=[
            pl.BlockSpec(memory_space=pltpu.SMEM),
            pl.BlockSpec(memory_space=pltpu.SMEM),
            vmem_spec(),
            pl.BlockSpec((width, chunk), lambda f: (0, f)),
            vmem_spec(),
            vmem_spec(),
            vmem_spec(),
        ],
        out_specs=(
            pl.BlockSpec((length, chunk), lambda f: (0, f)),
            vmem_spec(),
            vmem_spec(),
            vmem_spec(),
        ),
        scratch_shapes=[
            VMEM((1, units), F32),
            VMEM((units, width), BF),
            VMEM((width, bins), BF),
            VMEM((4, 1, width), F32),
            pltpu.SemaphoreType.DMA((3,)),
            pltpu.SemaphoreType.DMA((3,)),
        ]
        + RingGather.scratch()
        + RingGather.scratch(),
        compiler_params=pltpu.CompilerParams(
            collective_id=ident, has_side_effects=True, vmem_limit_bytes=BIG
        ),
        name="classify",
    )(lengths, bins_at, normed, up, base, down, head)


def per_device_block(
    token_ids,
    lengths,
    teacher_bins,
    embed_table,
    query_key_value_matrix,
    output_matrix,
    up_matrix,
    down_matrix,
    w_head,
):
    ranks = lax.axis_size("tensor")
    groups = lax.axis_size("dp")
    rank = lax.axis_index("tensor")
    group = lax.axis_index("dp")
    assert token_ids.shape[0] == 1
    local_len = token_ids.shape[1]
    span = local_len * ranks
    vocab_local, width = embed_table.shape
    d_local, _, e_local = query_key_value_matrix.shape
    f_local = up_matrix.shape[1]
    bins = w_head.shape[1]
    exact = lax.Precision.HIGHEST

    all_ids, out_columns = share_ids(token_ids, output_matrix, 11)
    all_ids = all_ids.reshape(ranks, local_len)
    shifted = all_ids - rank * vocab_local
    inside = (shifted >= 0) & (shifted < vocab_local)
    rows = jnp.take(embed_table, jnp.clip(shifted, 0, vocab_local - 1), axis=0)
    first, normed_one, qkv, up_full = embed(
        jnp.where(inside[..., None], rows, jnp.zeros((), BF)),
        query_key_value_matrix.transpose(1, 0, 2),
        up_matrix,
        12,
    )
    first = first.reshape(span, width)
    normed_one = normed_one.reshape(span, width)
    chunk = min(256, span)
    context, lse, out_full = attend_send(
        qkv, lengths, out_columns.reshape(ranks * e_local, d_local), chunk, 13
    )
    context_all = context.reshape(ranks * e_local, span)
    attn = lax.dot_general(
        context_all, out_full, (((0,), (0,)), ((), ())), preferred_element_type=F32
    )
    second = (first.astype(F32) + attn).astype(BF)
    normed_f, norm_back = jax.vjp(normalize, second.astype(F32))
    normed_two = normed_f.astype(BF)
    live = (jnp.arange(span, dtype=jnp.int32) < lengths[0]).astype(F32)
    second_sum = jnp.sum(second.astype(F32) * live[:, None], axis=0, keepdims=True)
    slope, packed, g_hidden, per_token = classify(
        normed_two, up_full, second_sum, down_matrix, w_head, lengths, teacher_bins,
        min(256, f_local), 14,
    )

    over_seqs = (((0,), (0,)), ((), ()))
    up_base = lax.dot_general(normed_two, slope, over_seqs, preferred_element_type=F32)
    up_term = (up_base * g_hidden).astype(BF).reshape(groups, d_local, f_local)
    g_pre = (slope.astype(F32) * g_hidden).astype(BF)
    g_normed = lax.dot_general(
        g_pre, up_full, (((1,), (1,)), ((), ())), preferred_element_type=F32
    )
    g_second = (
        norm_back(g_normed)[0] + live[:, None] * (per_token / ranks)
    ).astype(BF)
    spread = lax.dot_general(
        out_full, g_second, (((1,), (1,)), ((), ())), preferred_element_type=F32
    ).astype(BF)
    g_context, up_weight_gradient, every = scatter_and_group(
        spread.reshape(ranks, e_local, span), up_term, packed, ranks, 6
    )
    every = every[:, 0]
    hidden_every = every[:, :f_local]
    rounded_every = every[:, f_local : f_local + width]
    final_every = every[:, f_local + width : f_local + 2 * width]
    rest = every[:, f_local + 2 * width :]
    loss = jnp.sum(rest[:, bins]) / groups
    mine = group * d_local
    down_weight_gradient = lax.dot_general(
        hidden_every,
        lax.dynamic_slice_in_dim(rounded_every, mine, d_local, axis=1),
        over_seqs,
        precision=exact,
    )
    grad_head = lax.dot_general(
        lax.dynamic_slice_in_dim(final_every, mine, d_local, axis=1),
        rest[:, :bins],
        over_seqs,
        precision=exact,
    )

    out_term = (
        jnp.dot(context_all, g_second, preferred_element_type=F32)
        .astype(BF)
        .reshape(ranks, e_local, width)
    )
    g_qkv, out_mine = attend_back(qkv, lengths, lse, g_context, out_term, groups, chunk, 7)
    qkv_term = lax.dot_general(
        normed_one,
        g_qkv.reshape(3 * e_local, span),
        (((0,), (1,)), ((), ())),
        preferred_element_type=F32,
    )
    qkv_gradient, output_weight_gradient = group_sum(
        [qkv_term.astype(BF).reshape(groups, d_local, 3 * e_local), out_mine], 8
    )
    query_key_value_gradient = qkv_gradient.reshape(d_local, 3, e_local)
    return (
        loss,
        query_key_value_gradient,
        output_weight_gradient,
        up_weight_gradient,
        down_weight_gradient,
        grad_head,
    )


def solution(mesh):
    placed = (
        P("dp", "tensor"),
        P("dp"),
        P("dp"),
        P("tensor", None),
        P("dp", None, "tensor"),
        P("tensor", "dp"),
        P("dp", "tensor"),
        P("tensor", "dp"),
        P("dp", None),
    )
    return jax.shard_map(
        per_device_block if (mesh.shape["tensor"], mesh.shape["dp"]) == (4, 8) else per_device,
        mesh=mesh,
        in_specs=placed,
        out_specs=(
            P(),
            P("dp", None, "tensor"),
            P("tensor", "dp"),
            P("dp", "tensor"),
            P("tensor", "dp"),
            P("dp", None),
        ),
        check_vma=False,
    )
```

profile of v0, /device:TPU:0, one launch (start us, length us, event | category | flops | bytes accessed | tf_op | source)
XLA Modules:
  0.0 263.7 jit_solution(7391314771845603762)
XLA Ops:
  1.9 9.4 %share_ids.1 = (s32[4,1,256]{2,1,0:T(1,128)}, bf16[4,256,128]{2,1,0:T(8,128)(2,1)}) custom-call(s32[1,256]{1,0:T(1,128)} %ids_ref.1, bf16[256,128]{1,0:T(8,128)(2,1)} %out_ref.1), custom_call_target="tpu_custom_call" | custom-call | tf_op jit(solution)/shard_map/share_ids/pallas_call | solution.py:963
  12.8 12.6 %gather_fusion = bf16[1024,1024]{1,0:T(8,128)(2,1)S(1)} fusion(bf16[7632,1024]{1,0:T(8,128)(2,1)} %param.12, s32[1024]{0:T(1024)S(1)} %broadcast_clamp_fusion), kind=kCustom, calls=%fused_computation | custom fusion | bytes 4198400 | tf_op jit(solution)/shard_map/jit(_take)/gather | solution.py:1481
  25.4 1.6 select_select_fusion.x_ref
  27.0 47.0 %embed.1 = (bf16[4,256,1024]{2,1,0:T(8,128)(2,1)}, bf16[4,256,1024]{2,1,0:T(8,128)(2,1)}, bf16[3,256,1024]{2,1,0:T(8,128)(2,1)}, bf16[1024,1024]{1,0:T(8,128)(2,1)}) custom-call(bf16[4,256,1024]{2,1,0:T(8,128)(2,1)} %select_select_fusion.x_ref, bf16[3,128,256]{2,1,0:T(8,128)(2,1)} %bitcast.51, bf16[128,1024]{1,0:T(8,128)(2,1)} %up_ref.1), custom_call_target="tpu_custom_call" | custom-call | tf_op jit(solution)/shard_map/embed/pallas_call | solution.py:1127
  74.1 29.4 %attend_send.1 = (bf16[4,256,1024]{2,1,0:T(8,128)(2,1)}, f32[4,1,1024]{2,1,0:T(1,128)}, bf16[1024,1024]{1,0:T(8,128)(2,1)}) custom-call(s32[1]{0:T(128)} %copy.38.length_ref, bf16[3,256,1024]{2,1,0:T(8,128)(2,1)} %get-tuple-element.27.qkv_ref, bf16[1024,128]{1,0:T(8,128)(2,1)} %bitcast.50), custom_call_target="tpu_custom_call" | custom-call | tf_op jit(solution)/shard_map/attend_send/pallas_call | solution.py:1268
  103.5 5.5 %convert_reduce_fusion = (f32[1024]{0:T(1024)S(1)}, bf16[1024,1024]{1,0:T(8,128)(2,1)S(1)}) fusion(bf16[1024,1024]{1,0:T(8,128)(2,1)} %bitcast.58, bf16[1024,1024]{1,0:T(8,128)(2,1)} %get-tuple-element.29, bf16[4,256,1024]{2,1,0:T(8,128)(2,1)} %get-tuple-element.30), kind=kOutput, calls=%fused_computation.4 | convolution fusion | flops 2152725504 | bytes 8392704 | tf_op jit(solution)/shard_map/dot_general | solution.py:1495
  109.0 1.7 fusion.7
  110.7 1.9 fusion.5.normed_ref
  112.6 32.9 %classify.1 = (bf16[1024,1024]{1,0:T(8,128)(2,1)}, f32[1,3328]{1,0:T(1,128)}, f32[1,1024]{1,0:T(1,128)}, f32[1,1024]{1,0:T(1,128)}) custom-call(s32[1]{0:T(128)} %copy.38.length_ref, s32[1]{0:T(128)S(6)} %copy.39.bin_ref, bf16[1024,1024]{1,0:T(8,128)(2,1)} %fusion.5.normed_ref, bf16[1024,1024]{1,0:T(8,128)(2,1)} %get-tuple-element.32.up_ref, ...), custom_call_target="tpu_custom_call" | custom-call | tf_op jit(solution)/shard_map/classify/pallas_call | solution.py:1412
  145.5 6.1 %multiply_convert_fusion = bf16[1024,1024]{1,0:T(8,128)(2,1)} fusion(bf16[1024,1024]{1,0:T(8,128)(2,1)} %fusion.5.normed_ref, bf16[1024,1024]{1,0:T(8,128)(2,1)} %get-tuple-element.33, f32[1024]{0:T(1024)} %bitcast.60), kind=kOutput, calls=%fused_computation.15 | convolution fusion | flops 2149580800 | bytes 6295552 | tf_op jit(solution)/shard_map/dot_general | solution.py:1509
  151.7 2.5 fusion.6
  154.2 1.7 fusion.21
  155.9 3.8 %convolution_convert_fusion = bf16[1024,1024]{1,0:T(8,128)(2,1)} fusion(bf16[1024,1024]{1,0:T(8,128)(2,1)S(1)} %bitcast.59, f32[1024,1024]{1,0:T(8,128)S(1)} %get-tuple-element.61, f32[1024]{0:T(1024)S(1)} %bitcast.54, f32[1024]{0:T(1024)S(1)} %negate_multiply_fusion, f32[1024]{0:T(1024)S(1)} %fusion.17), kind=kOutput, calls=%fused_computation.21 | convolution fusion | flops 2152726528 | bytes 8400896 | tf_op jit(solution)/shard_map/dot_general | solution.py:1545
  159.7 3.8 %convolution_convert_fusion.1 = bf16[1024,1024]{1,0:T(8,128)(2,1)} fusion(bf16[1024,1024]{1,0:T(8,128)(2,1)S(1)} %copy-done.5, f32[1024,1024]{1,0:T(8,128)S(1)} %get-tuple-element.61, f32[1024]{0:T(1024)S(1)} %bitcast.55, f32[1024]{0:T(1024)S(1)} %negate_multiply_fusion, f32[1024]{0:T(1024)S(1)} %fusion.17), kind=kOutput, calls=%fused_computation.22 | convolution fusion | flops 2152726528 | bytes 8400896 | tf_op jit(solution)/shard_map/dot_general | solution.py:1518
  163.6 30.4 %scatter_and_group.1 = (bf16[256,1024]{1,0:T(8,128)(2,1)}, f32[128,1024]{1,0:T(8,128)}, f32[8,1,3328]{2,1,0:T(1,128)}) custom-call(bf16[4,256,1024]{2,1,0:T(8,128)(2,1)} %bitcast.43, bf16[8,128,1024]{2,1,0:T(8,128)(2,1)} %bitcast.42, f32[1,3328]{1,0:T(1,128)} %get-tuple-element.36.small_ref), custom_call_target="tpu_custom_call" | custom-call | tf_op jit(solution)/shard_map/scatter_and_group/pallas_call | solution.py:374
  194.0 0.9 copy.34
  196.2 29.0 %attend_back.1 = (bf16[3,256,1024]{2,1,0:T(8,128)(2,1)}, bf16[8,256,128]{2,1,0:T(8,128)(2,1)}) custom-call(s32[1]{0:T(128)} %copy.38.length_ref, bf16[3,256,1024]{2,1,0:T(8,128)(2,1)} %get-tuple-element.27.qkv_ref, f32[4,1,1024]{2,1,0:T(1,128)} %get-tuple-element.39.lse_ref, bf16[256,1024]{1,0:T(8,128)(2,1)} %get-tuple-element.40.grad_ref, ...), custom_call_target="tpu_custom_call" | custom-call | flops 2684354560 | bytes 3670016 | tf_op jit(solution)/shard_map/attend_back/pallas_call | solution.py:577
  225.2 4.5 %convolution_convert_fusion.2 = bf16[1024,768]{1,0:T(8,128)(2,1)} fusion(bf16[1024,1024]{1,0:T(8,128)(2,1)S(1)} %bitcast.57, bf16[768,1024]{1,0:T(8,128)(2,1)} %bitcast.63), kind=kOutput, calls=%fused_computation.23 | convolution fusion | flops 1611399168 | bytes 5242880 | tf_op jit(solution)/shard_map/dot_general | solution.py:1550
  229.6 26.6 %group_sum.1 = (f32[128,768]{1,0:T(8,128)}, f32[256,128]{1,0:T(8,128)}) custom-call(bf16[8,128,768]{2,1,0:T(8,128)(2,1)} %bitcast.45, bf16[8,256,128]{2,1,0:T(8,128)(2,1)} %get-tuple-element.42.refs_1_), custom_call_target="tpu_custom_call" | custom-call | tf_op jit(solution)/shard_map/group_sum/pallas_call | solution.py:420
  256.2 1.2 copy.22
  257.4 0.9 copy.23
  258.4 0.9 fusion.13
  259.3 1.8 fusion.11
  261.7 0.8 copy.41
  (32 shorter events, 2.7 us)
Async XLA Ops:
  145.5 6.1 %copy-start = (bf16[1024,1024]{1,0:T(8,128)(2,1)S(1)}, bf16[1024,1024]{1,0:T(8,128)(2,1)}, u32[]{:S(2)}) copy-start(bf16[1024,1024]{1,0:T(8,128)(2,1)} %get-tuple-element.32.up_ref) | copy-start | bytes 6291460
  145.5 6.1 %copy-start.7 = (bf16[1024,1024]{1,0:T(8,128)(2,1)S(1)}, bf16[1024,1024]{1,0:T(8,128)(2,1)}, u32[]{:S(2)}) copy-start(bf16[1024,1024]{1,0:T(8,128)(2,1)} %get-tuple-element.33) | copy-start | bytes 6291460
  145.5 6.1 %copy-start.8 = (f32[1,1024]{1,0:T(1,128)S(1)}, f32[1,1024]{1,0:T(1,128)}, u32[]{:S(2)}) copy-start(f32[1,1024]{1,0:T(1,128)} %get-tuple-element.34) | copy-start | bytes 12292
  154.2 1.7 copy-start.3
  154.2 1.7 copy-start.6
  155.9 3.8 %copy-start.5 = (bf16[1024,1024]{1,0:T(8,128)(2,1)S(1)}, bf16[1024,1024]{1,0:T(8,128)(2,1)}, u32[]{:S(2)}) copy-start(bf16[1024,1024]{1,0:T(8,128)(2,1)} %get-tuple-element.29) | copy-start | bytes 6291460
  196.2 29.0 %copy-start.4 = (bf16[4,256,1024]{2,1,0:T(8,128)(2,1)S(1)}, bf16[4,256,1024]{2,1,0:T(8,128)(2,1)}, u32[]{:S(2)}) copy-start(bf16[4,256,1024]{2,1,0:T(8,128)(2,1)} %get-tuple-element.38) | copy-start | bytes 6291460
  229.6 32.1 %copy-start.1 = (f32[128,1024]{1,0:T(8,128)S(1)}, f32[128,1024]{1,0:T(8,128)}, u32[]{:S(2)}) copy-start(f32[128,1024]{1,0:T(8,128)} %get-tuple-element.79) | copy-start | bytes 1572868
  256.2 4.8 %copy-start.2 = (f32[256,128]{1,0:T(8,128)S(1)}, f32[256,128]{1,0:T(8,128)}, u32[]{:S(2)}) copy-start(f32[256,128]{1,0:T(8,128)} %get-tuple-element.78) | copy-start | bytes 393220
where the time goes:
time: 264 us
  Pallas kernels  205 us (78%)
  matrix products  28.9 us (11%)
  local copies, waits for them, and re-layouts  17.1 us (6%)
  other arithmetic  8.89 us (3%)
  between operations  3.95 us (1%)
    pallas_call x1, Pallas kernels, embed(): pl.pallas_call(embed_body, out_shape=(jax.ShapeDtypeStruct(x.shape, BF),...  47 us
    pallas_call x1, Pallas kernels, classify(): pl.pallas_call(classify_body, grid=(units // chunk,), out_shape=(jax.Shap...  32.9 us
    pallas_call x1, Pallas kernels, scatter_and_group(): pl.pallas_call(functools.partial(scatter_and_group_body, count), out_shap...  30.4 us
    pallas_call x1, Pallas kernels, attend_send(): pl.pallas_call(functools.partial(attend_send_body, chunk), grid=(heads,),...  29.4 us
    pallas_call x1, Pallas kernels, attend_back(): pl.pallas_call(functools.partial(attend_back_body, chunk, x.shape[0]), gr...  29 us
    pallas_call x1, Pallas kernels, group_sum(): pl.pallas_call(functools.partial(group_sum_body, number), out_shape=tuple...  26.6 us
    gather x1, local copies, waits for them, and re-layouts, per_device_block(): rows = jnp.take(embed_table, jnp.clip(shifted, 0, vocab_local - 1), axis=0)  12.6 us
    pallas_call x1, Pallas kernels, share_ids(): pl.pallas_call(ids_body, out_shape=(jax.ShapeDtypeStruct((4,) + ids.shape...  9.43 us

commit v1 on v0

--- a/solution.py
+++ b/solution.py
@@ -1450,6 +1450,383 @@
     )(lengths, bins_at, normed, up, base, down, head)
 
 
+class Fold:
+    def __init__(self, at, src, held, acc, last, sems, base, rows, x_first):
+        self.at, self.src, self.held, self.acc, self.last = at, src, held, acc, last
+        self.sems, self.base, self.rows = sems, base, rows
+        self.one, self.two = (at.across, at.over) if x_first else (at.over, at.across)
+
+    def copies(self):
+        rows, base, sems = self.rows, self.base, self.sems
+        one, two = {"tensor": self.one}, {"tensor": self.two}
+        return (
+            remote(self.src.at[self.at.diag, rows], self.held.at[1, rows], sems, base, one),
+            remote(self.src.at[self.one, rows], self.held.at[0, rows], sems, base + 1, one),
+            remote(self.acc.at[rows], self.last.at[rows], sems, base + 2, two),
+        )
+
+    def start(self):
+        copies = self.copies()
+        copies[0].start()
+        copies[1].start()
+
+    def tiles(self, body):
+        def step(at):
+            body(pl.ds(pl.multiple_of(self.rows.start + at.start, 32), at.size))
+
+        add_tiles(self.rows.size, 32, step)
+
+    def second(self):
+        copies = self.copies()
+        copies[0].wait_recv()
+
+        def body(here):
+            self.acc[here] = (
+                self.src[self.two, here].astype(F32) + self.held[1, here].astype(F32)
+            ).astype(BF)
+
+        self.tiles(body)
+        copies[2].start()
+
+    def third(self, put):
+        copies = self.copies()
+        copies[1].wait_recv()
+        copies[2].wait_recv()
+
+        def body(here):
+            put(
+                here,
+                self.src[self.at.rank, here].astype(F32)
+                + self.held[0, here].astype(F32)
+                + self.last[here].astype(F32),
+            )
+
+        self.tiles(body)
+
+    def finish(self):
+        for copy in self.copies():
+            copy.wait_send()
+
+
+class DirectSum(GroupSum):
+    def __init__(self, x_ref, pair, mine, far, sems, tile):
+        super().__init__(x_ref, None, pair, mine, far, sems)
+        self.tile = tile
+
+    def middle(self):
+        for copy in self.pair_copies():
+            copy.wait()
+        for chip in range(self.chips):
+
+            def body(at, chip=chip):
+                self.mine[chip, at] = (
+                    self.x[chip * 2 + self.core, at].astype(F32)
+                    + self.pair[chip, at].astype(F32)
+                ).astype(BF)
+
+            add_tiles(self.rows, self.tile, body)
+        for copy in self.far_copies():
+            copy.start()
+
+    def finish(self, put):
+        for copy in self.far_copies():
+            copy.wait()
+
+        def body(at):
+            total = self.mine[self.chip, at].astype(F32)
+            for step in range(self.chips - 1):
+                total = total + self.far[step, at].astype(F32)
+            put(at, total)
+
+        add_tiles(self.rows, self.tile, body)
+
+
+def backward_body(
+    chunk, length_ref, qkv_ref, lse_ref, small_ref, g_second_in, out_in, up_in, ctx_in, normed_in,
+    qkv_out, out_out, up_out, small_out,
+    g_second, outs, up_term, ctx, normed, loads,
+    spread, g_ctx, s_held, s_acc, s_last, s_send, s_recv,
+    out_term, o_held, o_acc, o_last, o_send, o_recv,
+    out_mine, o_pair, o_own, o_far, o_sem0, o_sem1, o_sem2, o_sem3,
+    u_pair, u_own, u_far, u_sem0, u_sem1, u_sem2, u_sem3,
+    g_qkv, q_term, q_pair, q_own, q_far, q_sem0, q_sem1, q_sem2, q_sem3,
+    smalls, m_send, m_recv,
+):
+    at = Place()
+    head = pl.program_id(0)
+    heads = lse_ref.shape[0] * q_term.shape[0]
+    end = heads - 1
+    e_local = g_ctx.shape[0]
+    d_local = q_term.shape[3]
+    groups = q_term.shape[1]
+    half = HEAD_WIDTH // 2
+    length = length_ref[0]
+    scale = HEAD_WIDTH ** (-0.5)
+    span = qkv_ref.shape[2]
+
+    def load(index):
+        pairs = (
+            (g_second_in, g_second), (out_in, outs), (up_in, up_term), (ctx_in, ctx), (normed_in, normed)
+        )
+        return pltpu.make_async_copy(*pairs[index], loads.at[index])
+
+    def folds(one):
+        return [
+            Fold(
+                at, spread, s_held, s_acc, s_last, (s_send, s_recv), one * 6 + part * 3,
+                pl.ds(pl.multiple_of(one * HEAD_WIDTH + part * half, half), half), part == 0,
+            )
+            for part in range(2)
+        ]
+
+    out_folds = [
+        Fold(
+            at, out_term, o_held, o_acc, o_last, (o_send, o_recv), part * 3,
+            pl.ds(part * (e_local // 2), e_local // 2), part == 0,
+        )
+        for part in range(2)
+    ]
+    up_sum = GroupSum(up_term, up_out, u_pair, u_own, u_far, (u_sem0, u_sem1, u_sem2, u_sem3))
+    out_sum = DirectSum(out_mine, o_pair, o_own, o_far, (o_sem0, o_sem1, o_sem2, o_sem3), 64)
+
+    def qkv_sum(one):
+        return DirectSum(
+            q_term.at[one], q_pair.at[one], q_own.at[one], q_far.at[one],
+            (q_sem0.at[one], q_sem1.at[one], q_sem2.at[one], q_sem3.at[one]), q_term.shape[2],
+        )
+
+    def small_copies():
+        return [
+            remote(
+                small_ref, smalls.at[at.group], (m_send, m_recv), step - 1,
+                {"dp": lax.rem(at.group + step, groups)},
+            )
+            for step in range(1, groups)
+        ]
+
+    def put_context(here, total):
+        g_ctx[here] = total.astype(BF)
+
+    def put_out(here, total):
+        for group in range(groups):
+            out_mine[group, here] = total[:, group * d_local : (group + 1) * d_local].astype(BF)
+
+    @pl.when(head == 0)
+    def _():
+        for index in range(5):
+            load(index).start()
+        at.greet(True, True, True)
+        load(2).wait()
+        up_sum.start()
+        for copy in small_copies():
+            copy.start()
+        smalls[at.group] = small_ref[...]
+        load(0).wait()
+        load(1).wait()
+
+        def spread_head(one, carry):
+            left = jnp.concatenate(
+                [
+                    outs[pl.ds(pl.multiple_of(part * e_local + one * HEAD_WIDTH, HEAD_WIDTH), HEAD_WIDTH)]
+                    for part in range(4)
+                ],
+                axis=0,
+            )
+            result = contract(left, g_second[...], (1, 1)).astype(BF)
+            for part in range(4):
+                spread[part, pl.ds(pl.multiple_of(one * HEAD_WIDTH, HEAD_WIDTH), HEAD_WIDTH)] = result[
+                    part * HEAD_WIDTH : (part + 1) * HEAD_WIDTH
+                ]
+            for fold in folds(one):
+                fold.start()
+            return carry
+
+        lax.fori_loop(0, 2, spread_head, 0)
+        up_sum.middle()
+        for fold in folds(0):
+            fold.second()
+        lax.fori_loop(2, heads, spread_head, 0)
+        for fold in folds(1):
+            fold.second()
+        load(3).wait()
+
+        def out_block(one, carry):
+            rows = pl.ds(pl.multiple_of(one * e_local, e_local), e_local)
+            out_term[one] = jnp.dot(
+                ctx[rows], g_second[...], preferred_element_type=F32
+            ).astype(BF)
+            return carry
+
+        lax.fori_loop(0, 4, out_block, 0)
+        load(4).wait()
+
+    for fold in folds(head):
+        fold.third(put_context)
+
+    keys, vals = qkv_ref[1], qkv_ref[2]
+    g_keys = jnp.zeros((HEAD_WIDTH, span), F32)
+    g_vals = jnp.zeros((HEAD_WIDTH, span), F32)
+    mine = pl.ds(pl.multiple_of(head * HEAD_WIDTH, HEAD_WIDTH), HEAD_WIDTH)
+    for index, start in enumerate(range(0, span, chunk)):
+        here = slice(start, start + chunk)
+        query = (qkv_ref[0, :, here].astype(F32) * scale).astype(BF)
+        grad = g_ctx[mine, here]
+        probs = jnp.exp(masked_scores(keys, query, length) - lse_ref[0, :, here])
+        g_probs = contract(vals, grad, (0, 0))
+        weighted = probs * g_probs
+        inner = jnp.sum(weighted, axis=0, keepdims=True)
+        g_scores = (weighted - probs * inner).astype(BF)
+        g_qkv[:HEAD_WIDTH, here] = (contract(keys, g_scores, (1, 0)) * scale).astype(BF)
+        g_keys += contract(query, g_scores, (1, 1))
+        g_vals += contract(grad, probs.astype(BF), (1, 1))
+        if index == 1:
+
+            @pl.when((head > 0) & (head < end))
+            def _():
+                qkv_sum(head - 1).middle()
+
+            @pl.when(head == end)
+            def _():
+                for fold in out_folds:
+                    fold.third(put_out)
+                out_sum.start()
+                qkv_sum(head - 1).middle()
+
+            @pl.when(head == end - 1)
+            def _():
+                for fold in out_folds:
+                    fold.second()
+
+    g_qkv[HEAD_WIDTH : 2 * HEAD_WIDTH] = g_keys.astype(BF)
+    g_qkv[2 * HEAD_WIDTH :] = g_vals.astype(BF)
+    result = jnp.dot(g_qkv[...], normed[...], preferred_element_type=F32)
+    for group in range(groups):
+        q_term[head, group] = result[:, group * d_local : (group + 1) * d_local].astype(BF)
+    qkv_sum(head).start()
+
+    @pl.when(head == 0)
+    def _():
+        def second(one, carry):
+            for fold in folds(one):
+                fold.second()
+            return carry
+
+        lax.fori_loop(2, heads, second, 0)
+        for fold in out_folds:
+            fold.start()
+        up_sum.relay()
+
+    @pl.when(head == end)
+    def _():
+        out_sum.middle()
+        qkv_sum(head).middle()
+        up_sum.finish()
+        for copy in small_copies():
+            copy.wait()
+        small_out[...] = smalls[...]
+
+        def drain(one, carry):
+            for fold in folds(one):
+                fold.finish()
+            return carry
+
+        lax.fori_loop(0, heads, drain, 0)
+        for fold in out_folds:
+            fold.finish()
+
+        def put_final(here, total):
+            out_out[here] = total
+
+        out_sum.finish(put_final)
+
+        def store(one, carry):
+            def put(here, total):
+                for kind in range(3):
+                    qkv_out[kind, pl.ds(pl.multiple_of(one * HEAD_WIDTH, HEAD_WIDTH), HEAD_WIDTH)] = total[
+                        kind * HEAD_WIDTH : (kind + 1) * HEAD_WIDTH
+                    ]
+
+            qkv_sum(one).finish(put)
+            return carry
+
+        lax.fori_loop(0, heads, store, 0)
+
+
+def backward(qkv, lengths, lse, small, g_second, out_full, up_term, context, normed, chunk, ident):
+    _, width, length = qkv.shape
+    heads = width // HEAD_WIDTH
+    groups, d_local, f_local = up_term.shape
+    full = out_full.shape[1]
+    rows = 3 * HEAD_WIDTH
+    dma = pltpu.SemaphoreType.DMA
+    return pl.pallas_call(
+        functools.partial(backward_body, chunk),
+        grid=(heads,),
+        out_shape=(
+            jax.ShapeDtypeStruct((3, width, d_local), F32),
+            jax.ShapeDtypeStruct((width, d_local), F32),
+            jax.ShapeDtypeStruct((d_local, f_local), F32),
+            jax.ShapeDtypeStruct((groups,) + small.shape, F32),
+        ),
+        in_specs=[
+            pl.BlockSpec(memory_space=pltpu.SMEM),
+            pl.BlockSpec((3, HEAD_WIDTH, length), lambda h: (0, h, 0)),
+            pl.BlockSpec((1, 1, length), lambda h: (h, 0, 0)),
+            vmem_spec(),
+        ]
+        + [any_spec()] * 5,
+        out_specs=(vmem_spec(),) * 4,
+        scratch_shapes=[
+            VMEM(g_second.shape, BF),
+            VMEM(out_full.shape, BF),
+            VMEM(up_term.shape, BF),
+            VMEM(context.shape, BF),
+            VMEM(normed.shape, BF),
+            dma((5,)),
+            VMEM((4, width, length), BF),
+            VMEM((width, length), BF),
+            VMEM((2, width, length), BF),
+            VMEM((width, length), BF),
+            VMEM((width, length), BF),
+            dma((heads * 6,)),
+            dma((heads * 6,)),
+            VMEM((4, width, full), BF),
+            VMEM((2, width, full), BF),
+            VMEM((width, full), BF),
+            VMEM((width, full), BF),
+            dma((6,)),
+            dma((6,)),
+            VMEM((groups, width, d_local), BF),
+            VMEM((4, width, d_local), BF),
+            VMEM((4, width, d_local), BF),
+            VMEM((3, width, d_local), BF),
+            dma((4,)),
+            dma((4,)),
+            dma((3,)),
+            dma((3,)),
+        ]
+        + GroupSum.scratch(up_term.shape, BF)
+        + [
+            VMEM((rows, length), BF),
+            VMEM((heads, groups, rows, d_local), BF),
+            VMEM((heads, 4, rows, d_local), BF),
+            VMEM((heads, 4, rows, d_local), BF),
+            VMEM((heads, 3, rows, d_local), BF),
+            dma((heads, 4)),
+            dma((heads, 4)),
+            dma((heads, 3)),
+            dma((heads, 3)),
+            VMEM((groups,) + small.shape, F32),
+            dma((groups - 1,)),
+            dma((groups - 1,)),
+        ],
+        compiler_params=pltpu.CompilerParams(
+            collective_id=ident, has_side_effects=True, vmem_limit_bytes=BIG
+        ),
+        name="backward",
+    )(lengths, qkv, lse, small, g_second, out_full, up_term, context, normed)
+
+
 def per_device_block(
     token_ids,
     lengths,
@@ -1515,11 +1892,8 @@
     g_second = (
         norm_back(g_normed)[0] + live[:, None] * (per_token / ranks)
     ).astype(BF)
-    spread = lax.dot_general(
-        out_full, g_second, (((1,), (1,)), ((), ())), preferred_element_type=F32
-    ).astype(BF)
-    g_context, up_weight_gradient, every = scatter_and_group(
-        spread.reshape(ranks, e_local, span), up_term, packed, ranks, 6
+    qkv_gradient, output_weight_gradient, up_weight_gradient, every = backward(
+        qkv, lengths, lse, packed, g_second, out_full, up_term, context_all, normed_one, chunk, 15
     )
     every = every[:, 0]
     hidden_every = every[:, :f_local]
@@ -1541,22 +1915,7 @@
         precision=exact,
     )
 
-    out_term = (
-        jnp.dot(context_all, g_second, preferred_element_type=F32)
-        .astype(BF)
-        .reshape(ranks, e_local, width)
-    )
-    g_qkv, out_mine = attend_back(qkv, lengths, lse, g_context, out_term, groups, chunk, 7)
-    qkv_term = lax.dot_general(
-        normed_one,
-        g_qkv.reshape(3 * e_local, span),
-        (((0,), (1,)), ((), ())),
-        preferred_element_type=F32,
-    )
-    qkv_gradient, output_weight_gradient = group_sum(
-        [qkv_term.astype(BF).reshape(groups, d_local, 3 * e_local), out_mine], 8
-    )
-    query_key_value_gradient = qkv_gradient.reshape(d_local, 3, e_local)
+    query_key_value_gradient = qkv_gradient.transpose(2, 0, 1)
     return (
         loss,
         query_key_value_gradient,

time: 264 us -> 225 us (0.85)
  Pallas kernels: 205 us -> 176 us
  matrix products: 28.9 us -> 16.8 us
    pallas_call x3 -> x1, Pallas kernels: 86 us -> 56.8 us  [backward(): pl.pallas_call(functools.partial(backward_body, chunk), grid=(heads,), ou...]
    dot_general x3 -> x0, matrix products: 12.1 us -> none  [the longest x1 4.45 us: per_device_block(): lax.dot_general(normed_one, g_qkv.reshape(3 * e_local, span), (((0,), (1,...]
where the time goes in v1:
time: 225 us
  Pallas kernels  176 us (78%)
  local copies, waits for them, and re-layouts  17.9 us (8%)
  matrix products  16.8 us (7%)
  other arithmetic  10.8 us (5%)
  between operations  3.89 us (2%)
    pallas_call x1, Pallas kernels, backward(): pl.pallas_call(functools.partial(backward_body, chunk), grid=(heads,), ou...  56.8 us
    pallas_call x1, Pallas kernels, embed(): pl.pallas_call(embed_body, out_shape=(jax.ShapeDtypeStruct(x.shape, BF),...  47.1 us
    pallas_call x1, Pallas kernels, classify(): pl.pallas_call(classify_body, grid=(units // chunk,), out_shape=(jax.Shap...  32.8 us
    pallas_call x1, Pallas kernels, attend_send(): pl.pallas_call(functools.partial(attend_send_body, chunk), grid=(heads,),...  29.5 us
    gather x1, local copies, waits for them, and re-layouts, per_device_block(): rows = jnp.take(embed_table, jnp.clip(shifted, 0, vocab_local - 1), axis=0)  12.6 us
    pallas_call x1, Pallas kernels, share_ids(): pl.pallas_call(ids_body, out_shape=(jax.ShapeDtypeStruct((4,) + ids.shape...  9.44 us
    dot_general x1, matrix products, per_device_block(): lax.dot_general(normed_two, slope, over_seqs, preferred_element_type=F32)  6.11 us
    dot_general x1, matrix products, per_device_block(): lax.dot_general(context_all, out_full, (((0,), (0,)), ((), ())), preferre...  5.49 us

profile of v1, /device:TPU:0, one launch (start us, length us, event | category | flops | bytes accessed | tf_op | source)
XLA Modules:
  0.0 224.9 jit_solution(864521992808284275)
XLA Ops:
  1.9 9.4 %share_ids.1 = (s32[4,1,256]{2,1,0:T(1,128)}, bf16[4,256,128]{2,1,0:T(8,128)(2,1)}) custom-call(s32[1,256]{1,0:T(1,128)} %ids_ref.1, bf16[256,128]{1,0:T(8,128)(2,1)} %out_ref.1), custom_call_target="tpu_custom_call" | custom-call | tf_op jit(solution)/shard_map/share_ids/pallas_call | solution.py:963
  11.4 0.7 compare_and_fusion
  12.1 0.7 compare_select_fusion
  12.8 12.6 %gather_fusion = bf16[1024,1024]{1,0:T(8,128)(2,1)S(1)} fusion(bf16[7632,1024]{1,0:T(8,128)(2,1)} %param.12, s32[1024]{0:T(1024)S(1)} %broadcast_clamp_fusion), kind=kCustom, calls=%fused_computation | custom fusion | bytes 4198400 | tf_op jit(solution)/shard_map/jit(_take)/gather | solution.py:1858
  25.4 1.6 select_select_fusion.x_ref
  27.0 47.1 %embed.1 = (bf16[4,256,1024]{2,1,0:T(8,128)(2,1)}, bf16[4,256,1024]{2,1,0:T(8,128)(2,1)}, bf16[3,256,1024]{2,1,0:T(8,128)(2,1)}, bf16[1024,1024]{1,0:T(8,128)(2,1)}) custom-call(bf16[4,256,1024]{2,1,0:T(8,128)(2,1)} %select_select_fusion.x_ref, bf16[3,128,256]{2,1,0:T(8,128)(2,1)} %bitcast.44, bf16[128,1024]{1,0:T(8,128)(2,1)} %up_ref.1), custom_call_target="tpu_custom_call" | custom-call | tf_op jit(solution)/shard_map/embed/pallas_call | solution.py:1127
  74.1 29.5 %attend_send.1 = (bf16[4,256,1024]{2,1,0:T(8,128)(2,1)}, f32[4,1,1024]{2,1,0:T(1,128)}, bf16[1024,1024]{1,0:T(8,128)(2,1)}) custom-call(s32[1]{0:T(128)} %copy.37.length_ref, bf16[3,256,1024]{2,1,0:T(8,128)(2,1)} %get-tuple-element.24.qkv_ref, bf16[1024,128]{1,0:T(8,128)(2,1)} %bitcast.43), custom_call_target="tpu_custom_call" | custom-call | tf_op jit(solution)/shard_map/attend_send/pallas_call | solution.py:1268
  103.7 5.5 %convert_reduce_fusion = (f32[1024]{0:T(1024)S(1)}, bf16[1024,1024]{1,0:T(8,128)(2,1)S(1)}) fusion(bf16[1024,1024]{1,0:T(8,128)(2,1)} %bitcast.35, bf16[1024,1024]{1,0:T(8,128)(2,1)} %get-tuple-element.29.out_in, bf16[4,256,1024]{2,1,0:T(8,128)(2,1)} %get-tuple-element.27), kind=kOutput, calls=%fused_computation.4 | convolution fusion | flops 2152725504 | bytes 8392704 | tf_op jit(solution)/shard_map/dot_general | solution.py:1872
  109.2 1.7 fusion.7
  110.9 1.9 fusion.5.normed_ref
  112.8 32.8 %classify.1 = (bf16[1024,1024]{1,0:T(8,128)(2,1)}, f32[1,3328]{1,0:T(1,128)}, f32[1,1024]{1,0:T(1,128)}, f32[1,1024]{1,0:T(1,128)}) custom-call(s32[1]{0:T(128)} %copy.37.length_ref, s32[1]{0:T(128)S(6)} %copy.38.bin_ref, bf16[1024,1024]{1,0:T(8,128)(2,1)} %fusion.5.normed_ref, bf16[1024,1024]{1,0:T(8,128)(2,1)} %get-tuple-element.30.up_ref, ...), custom_call_target="tpu_custom_call" | custom-call | tf_op jit(solution)/shard_map/classify/pallas_call | solution.py:1412
  145.6 6.1 %multiply_convert_fusion = bf16[1024,1024]{1,0:T(8,128)(2,1)} fusion(bf16[1024,1024]{1,0:T(8,128)(2,1)} %fusion.5.normed_ref, bf16[1024,1024]{1,0:T(8,128)(2,1)} %get-tuple-element.32, f32[1024]{0:T(1024)} %bitcast.49), kind=kOutput, calls=%fused_computation.15 | convolution fusion | flops 2149580800 | bytes 6295552 | tf_op jit(solution)/shard_map/dot_general | solution.py:1886
  151.7 0.0 copy-done.4
  151.7 2.5 %fusion.6 = (f32[1024]{0:T(1024)S(1)}, f32[1024,1024]{1,0:T(8,128)S(1)}) fusion(bf16[1024,1024]{1,0:T(8,128)(2,1)S(1)} %get-tuple-element.61, f32[1024]{0:T(1024)S(1)} %broadcast_multiply_fusion.1, bf16[1024,1024]{1,0:T(8,128)(2,1)S(1)} %copy-done, bf16[1024,1024]{1,0:T(8,128)(2,1)S(1)} %copy-done.3, f32[1024]{0:T(1024)S(1)} %bitcast.50), kind=kOutput, calls=%fused_computation.11 | convolution fusion | flops 2154822656 | bytes 10498048 | tf_op jit(solution)/shard_map/dot_general | solution.py:1889
  154.2 1.6 fusion.21
  155.9 2.0 add_convert_fusion.g_second_in
  157.8 56.8 %backward.1 = (f32[3,256,128]{2,1,0:T(8,128)}, f32[256,128]{1,0:T(8,128)}, f32[128,1024]{1,0:T(8,128)}, f32[8,1,3328]{2,1,0:T(1,128)}) custom-call(s32[1]{0:T(128)} %copy.37.length_ref, bf16[3,256,1024]{2,1,0:T(8,128)(2,1)} %get-tuple-element.24.qkv_ref, f32[4,1,1024]{2,1,0:T(1,128)} %get-tuple-element.26.lse_ref, f32[1,3328]{1,0:T(1,128)} %get-tuple-element.31.small_ref, ...), custom_call_target="tpu_custom_call" | custom-call | tf_op jit(solution)/shard_map/backward/pallas_call | solution.py:1762
  214.6 1.0 copy.33
  215.6 0.6 slice_reduce_fusion
  216.8 1.9 copy.22
  218.7 0.9 fusion.13
  219.6 1.8 fusion.11
  221.4 1.6 copy.39
  223.0 0.8 copy.40
  (19 shorter events, 0.1 us)
Async XLA Ops:
  145.6 6.1 %copy-start = (bf16[1024,1024]{1,0:T(8,128)(2,1)S(1)}, bf16[1024,1024]{1,0:T(8,128)(2,1)}, u32[]{:S(2)}) copy-start(bf16[1024,1024]{1,0:T(8,128)(2,1)} %get-tuple-element.30.up_ref) | copy-start | bytes 6291460
  145.6 6.1 %copy-start.3 = (bf16[1024,1024]{1,0:T(8,128)(2,1)S(1)}, bf16[1024,1024]{1,0:T(8,128)(2,1)}, u32[]{:S(2)}) copy-start(bf16[1024,1024]{1,0:T(8,128)(2,1)} %get-tuple-element.32) | copy-start | bytes 6291460
  145.6 6.1 %copy-start.4 = (f32[1,1024]{1,0:T(1,128)S(1)}, f32[1,1024]{1,0:T(1,128)}, u32[]{:S(2)}) copy-start(f32[1,1024]{1,0:T(1,128)} %get-tuple-element.33) | copy-start | bytes 12292
  154.2 1.6 copy-start.2
  214.6 8.4 %copy-start.1 = (f32[128,1024]{1,0:T(8,128)S(1)}, f32[128,1024]{1,0:T(8,128)}, u32[]{:S(2)}) copy-start(f32[128,1024]{1,0:T(8,128)} %get-tuple-element.73) | copy-start | bytes 1572868

commit v2 on v1

--- a/solution.py
+++ b/solution.py
@@ -834,22 +834,23 @@
     def same(self, chip):
         return chip * 2 + self.core
 
-    def greet(self, tensor, dp, everyone=False):
+    def peers(self, everyone=False):
+        peers = [{"tensor": one} for one in (self.across, self.over, self.diag)]
+        if everyone:
+            return peers + [{"dp": lax.rem(self.group + step, 8)} for step in range(1, 8)]
+        return peers + [
+            {"dp": self.near},
+            {"dp": self.same(self.turn(1))},
+            {"dp": self.same(self.turn(3))},
+        ]
+
+    def signal(self, peers):
         barrier = pltpu.get_barrier_semaphore()
-        peers = []
-        if tensor:
-            peers += [{"tensor": one} for one in (self.across, self.over, self.diag)]
-        if everyone:
-            peers += [{"dp": lax.rem(self.group + step, 8)} for step in range(1, 8)]
-        elif dp:
-            peers += [
-                {"dp": self.near},
-                {"dp": self.same(self.turn(1))},
-                {"dp": self.same(self.turn(3))},
-            ]
         for peer in peers:
             pl.semaphore_signal(barrier, inc=1, device_id=peer, device_id_type=MESH)
-        pl.semaphore_wait(barrier, len(peers))
+
+    def ready(self, peers):
+        pl.semaphore_wait(pltpu.get_barrier_semaphore(), len(peers))
 
 
 class RingGather:
@@ -925,6 +926,52 @@
             copy.wait_send()
         self.keep().wait()
 
+    def near(self):
+        copies = self.copies()
+        for index in (0, 2):
+            copies[index].wait_recv()
+        copies[7].start()
+        for index in (1, 3):
+            copies[index].wait_recv()
+        copies[8].start()
+
+    def close_near(self):
+        copies = self.copies()
+        for index in (6, 7, 8):
+            copies[index].wait_recv()
+        for index in (0, 1, 2, 3, 6, 7, 8):
+            copies[index].wait_send()
+        self.keep().wait()
+
+    def pass_on(self):
+        copies = self.copies()
+        copies[4].start()
+        copies[5].start()
+
+    def far(self):
+        copies = self.copies()
+        copies[4].wait_recv()
+        copies[5].wait_recv()
+        copies[9].start()
+
+    def close_far(self):
+        copies = self.copies()
+        copies[9].wait_recv()
+        for index in (4, 5, 9):
+            copies[index].wait_send()
+
+
+def columns_of(ref, size):
+    rows = ref.shape[0]
+
+    def slot(block, half):
+        lanes = pl.ds(pl.multiple_of(block * size, size), size)
+        if half is None:
+            return ref.at[:, lanes]
+        return ref.at[pl.ds(half * (rows // 2), rows // 2), lanes]
+
+    return slot
+
 
 def rows_of(ref, block, half, size, axis=0):
     lead = (slice(None),) * axis
@@ -939,39 +986,32 @@
     return ref.at[(slice(None),) * axis + (pl.ds(half * part, part),)]
 
 
-def ids_body(ids_ref, out_ref, ids_all, out_all, send, recv):
+def ids_body(ids_ref, ids_all, send, recv):
     at = Place()
-    at.greet(True, False)
-    copies = []
-    for index, peer in enumerate((at.across, at.over, at.diag)):
-        copies.append(
-            remote(ids_ref, ids_all.at[at.rank], (send, recv), index, {"tensor": peer})
-        )
-    for index, peer in enumerate((at.across, at.over, at.diag)):
-        copies.append(
-            remote(out_ref, out_all.at[at.rank], (send, recv), 3 + index, {"tensor": peer})
-        )
+    peers = at.peers()[:3]
+    at.signal(peers)
+    ids_all[at.rank] = ids_ref[...]
+    at.ready(peers)
+    copies = [
+        remote(ids_ref, ids_all.at[at.rank], (send, recv), index, peer)
+        for index, peer in enumerate(peers)
+    ]
     for copy in copies:
         copy.start()
-    ids_all[at.rank] = ids_ref[...]
-    out_all[at.rank] = out_ref[...]
     for copy in copies:
         copy.wait()
 
 
-def share_ids(ids, out, ident):
+def share_ids(ids, ident):
     return pl.pallas_call(
         ids_body,
-        out_shape=(
-            jax.ShapeDtypeStruct((4,) + ids.shape, ids.dtype),
-            jax.ShapeDtypeStruct((4,) + out.shape, out.dtype),
-        ),
-        in_specs=[vmem_spec()] * 2,
-        out_specs=(vmem_spec(),) * 2,
-        scratch_shapes=[pltpu.SemaphoreType.DMA((6,))] * 2,
+        out_shape=jax.ShapeDtypeStruct((4,) + ids.shape, ids.dtype),
+        in_specs=[vmem_spec()],
+        out_specs=vmem_spec(),
+        scratch_shapes=[pltpu.SemaphoreType.DMA((3,))] * 2,
         compiler_params=pltpu.CompilerParams(collective_id=ident, has_side_effects=True),
         name="share_ids",
-    )(ids, out)
+    )(ids)
 
 
 def any_spec():
@@ -1043,23 +1083,52 @@
             copy.wait_send()
 
 
-def embed_body(
-    x_ref, w_ref, up_ref, first_out, normed_out, qkv_ref, up_out,
-    acc, held, last, whole, normed, w_full, w_turn, send, recv, saved, *rest,
+def front_body(
+    chunk, length_ref, x_in, w_ref, up_ref, down_ref, head_ref, out_ref,
+    first_out, normed_out, qkv_out, ctx_out, lse_ref, up_out, out_full, down_out, head_out,
+    x_ref, acc, held, last, whole, normed, qkv_ref, w_full, w_turn, ctx_ref, cols,
+    load, saved, send, recv, col_send, col_recv, ctx_send, ctx_recv, ctx_saved, *rest,
 ):
     at = Place()
-    at.greet(True, True)
+    peers = at.peers()
+    at.signal(peers)
+    entry = pltpu.make_async_copy(x_in, x_ref, load.at[0])
+    entry.start()
     d_local = w_ref.shape[1]
     local = x_ref.shape[1]
+    e_local = w_ref.shape[2]
+    span = qkv_ref.shape[2]
+    heads = lse_ref.shape[0]
+    size = HEAD_WIDTH // 2
     weights = RingGather(
         at, w_ref, lambda half: half_rows(w_ref, half, 1),
         lambda block, half: rows_of(w_full, block, half, d_local, 1), rest[:3],
     )
     ups = RingGather(
         at, up_ref, lambda half: half_rows(up_ref, half),
-        lambda block, half: rows_of(up_out, block, half, d_local), rest[3:],
-    )
+        lambda block, half: rows_of(up_out, block, half, d_local), rest[3:6],
+    )
+    tops = RingGather(
+        at, head_ref, lambda half: half_rows(head_ref, half),
+        lambda block, half: rows_of(head_out, block, half, d_local), rest[6:9],
+    )
+    downs = RingGather(
+        at, down_ref, lambda half: half_rows(down_ref, half), columns_of(down_out, d_local), rest[9:12]
+    )
+    outs = RingGather(
+        at, cols, lambda half: half_rows(cols, half), columns_of(out_full, d_local), rest[12:15]
+    )
+    mine = pl.ds(pl.multiple_of(at.rank * e_local, e_local), e_local)
+    own_columns = pltpu.make_async_copy(out_ref, cols.at[mine], load.at[1])
+    own_columns.start()
+    column_copies = [
+        remote(out_ref, cols.at[mine], (col_send, col_recv), index, peer)
+        for index, peer in enumerate(peers[:3])
+    ]
+
+    at.ready(peers)
     weights.start()
+    entry.wait()
     part = local // 4
     streams = [
         Stream(
@@ -1074,12 +1143,25 @@
         one.second()
     weights.relay()
     ups.start()
+    tops.start()
     for one in streams:
         one.third()
+    for copy in column_copies:
+        copy.start()
     weights.spread()
     weights.finish()
     for index in range(3):
         w_turn[index] = w_full[index].T
+
+    def saves(slot, block):
+        base = pl.multiple_of(block * local, local)
+        return (
+            pltpu.make_async_copy(whole.at[block], first_out.at[block], saved.at[slot, 0]),
+            pltpu.make_async_copy(normed.at[block], normed_out.at[block], saved.at[slot, 1]),
+            pltpu.make_async_copy(
+                qkv_ref.at[:, :, pl.ds(base, local)], qkv_out.at[:, :, pl.ds(base, local)], saved.at[slot, 2]
+            ),
+        )
 
     def project(block, slot):
         def tile(here):
@@ -1095,8 +1177,8 @@
             return carry
 
         lax.fori_loop(0, 3, matrix, 0)
-        pltpu.make_async_copy(whole.at[block], first_out.at[block], saved.at[slot, 0]).start()
-        pltpu.make_async_copy(normed.at[block], normed_out.at[block], saved.at[slot, 1]).start()
+        for copy in saves(slot, block):
+            copy.start()
 
     for one in streams[:2]:
         one.relay()
@@ -1104,74 +1186,19 @@
     for one in streams[2:]:
         one.relay()
     ups.relay()
+    tops.relay()
+    downs.start()
     for one in streams:
         one.beside()
     project(at.across, 1)
     project(at.over, 2)
-    ups.spread()
     for one in streams:
         one.opposite()
     project(at.diag, 3)
-    ups.finish()
-    for one in streams:
-        one.finish()
-    for slot, block in enumerate((at.rank, at.across, at.over, at.diag)):
-        pltpu.make_async_copy(whole.at[block], first_out.at[block], saved.at[slot, 0]).wait()
-        pltpu.make_async_copy(normed.at[block], normed_out.at[block], saved.at[slot, 1]).wait()
-
-
-def embed(x, w, up, ident):
-    ranks, local, width = x.shape
-    kinds, d_local, e_local = w.shape
-    f_local = up.shape[1]
-    return pl.pallas_call(
-        embed_body,
-        out_shape=(
-            jax.ShapeDtypeStruct(x.shape, BF),
-            jax.ShapeDtypeStruct(x.shape, BF),
-            jax.ShapeDtypeStruct((kinds, e_local, ranks * local), BF),
-            jax.ShapeDtypeStruct((width, f_local), BF),
-        ),
-        in_specs=[vmem_spec()] * 3,
-        out_specs=(any_spec(), any_spec(), vmem_spec(), any_spec()),
-        scratch_shapes=[
-            VMEM((local, width), BF),
-            VMEM((2, local, width), BF),
-            VMEM((local, width), BF),
-            VMEM(x.shape, BF),
-            VMEM(x.shape, BF),
-            VMEM((kinds, width, e_local), BF),
-            VMEM((kinds, e_local, width), BF),
-            pltpu.SemaphoreType.DMA((24,)),
-            pltpu.SemaphoreType.DMA((24,)),
-            pltpu.SemaphoreType.DMA((4, 2)),
-        ]
-        + RingGather.scratch()
-        + RingGather.scratch(),
-        compiler_params=pltpu.CompilerParams(
-            collective_id=ident, has_side_effects=True, vmem_limit_bytes=BIG
-        ),
-        name="embed",
-    )(x, w, up)
-
-
-def attend_send_body(
-    chunk, length_ref, qkv_ref, col_ref, ctx_out, lse_ref, out_full, ctx_ref, saved, send, recv, *rest
-):
-    at = Place()
-    head = pl.program_id(0)
-    last = pl.num_programs(0) - 1
-    size = HEAD_WIDTH // 2
-    d_local = col_ref.shape[1]
-    e_rows = col_ref.shape[0]
-
-    def columns(block, half):
-        lanes = pl.ds(pl.multiple_of(block * d_local, d_local), d_local)
-        if half is None:
-            return out_full.at[:, lanes]
-        return out_full.at[pl.ds(half * (e_rows // 2), e_rows // 2), lanes]
-
-    outs = RingGather(at, col_ref, lambda half: half_rows(col_ref, half), columns, rest)
+    own_columns.wait()
+    for copy in column_copies:
+        copy.wait()
+    outs.start()
 
     def copies(one):
         def copy(index, block, half, peer):
@@ -1179,8 +1206,8 @@
             return pltpu.make_async_remote_copy(
                 src_ref=ref,
                 dst_ref=ref,
-                send_sem=send.at[one, index],
-                recv_sem=recv.at[one, index],
+                send_sem=ctx_send.at[one, index],
+                recv_sem=ctx_recv.at[one, index],
                 device_id={"tensor": peer},
                 device_id_type=MESH,
             )
@@ -1201,96 +1228,128 @@
         group[1].wait_recv()
         group[5].start()
 
-    @pl.when(head == 0)
-    def _():
-        at.greet(True, True)
-        outs.start()
+    def save(one):
+        here = pl.ds(pl.multiple_of(one * HEAD_WIDTH, HEAD_WIDTH), HEAD_WIDTH)
+        return pltpu.make_async_copy(ctx_ref.at[:, here], ctx_out.at[:, here], ctx_saved.at[one])
 
     length = length_ref[0]
-    keys, vals = qkv_ref[1], qkv_ref[2]
     scale = HEAD_WIDTH ** (-0.5)
-    for start in range(0, qkv_ref.shape[2], chunk):
-        here = slice(start, start + chunk)
-        query = (qkv_ref[0, :, here].astype(F32) * scale).astype(BF)
-        scores = masked_scores(keys, query, length)
-        top = jnp.max(scores, axis=0, keepdims=True)
-        expo = jnp.exp(scores - top)
-        total = jnp.sum(expo, axis=0, keepdims=True)
-        mixed = contract(vals, expo.astype(BF), (1, 0))
-        ctx_ref[at.rank, pl.ds(pl.multiple_of(head * HEAD_WIDTH, HEAD_WIDTH), HEAD_WIDTH), here] = (
-            mixed * (1.0 / total)
-        ).astype(BF)
-        lse_ref[0, :, here] = top + jnp.log(total)
-
-    @pl.when(head > 0)
-    def _():
-        relay(head - 1)
-
-    for copy in copies(head)[:4]:
-        copy.start()
-
-    @pl.when(head == 1)
-    def _():
-        outs.relay()
-
-    @pl.when(head == last)
-    def _():
-        relay(last)
-        outs.spread()
-
-        def save(one):
-            here = pl.ds(pl.multiple_of(one * HEAD_WIDTH, HEAD_WIDTH), HEAD_WIDTH)
-            return pltpu.make_async_copy(ctx_ref.at[:, here], ctx_out.at[:, here], saved.at[one])
-
-        def drain(one, carry):
-            group = copies(one)
-            for copy in group[2:]:
-                copy.wait_recv()
-            for copy in group:
-                copy.wait_send()
-            save(one).start()
-            return carry
-
-        lax.fori_loop(0, last + 1, drain, 0)
-        outs.finish()
-
-        def store(one, carry):
-            save(one).wait()
-            return carry
-
-        lax.fori_loop(0, last + 1, store, 0)
-
-
-def attend_send(qkv, lengths, column, chunk, ident):
-    _, width, length = qkv.shape
-    heads = width // HEAD_WIDTH
+
+    def attend_head(head, carry):
+        lines = pl.ds(pl.multiple_of(head * HEAD_WIDTH, HEAD_WIDTH), HEAD_WIDTH)
+        keys, vals = qkv_ref[1, lines], qkv_ref[2, lines]
+        for start in range(0, span, chunk):
+            here = slice(start, start + chunk)
+            query = (qkv_ref[0, lines, here].astype(F32) * scale).astype(BF)
+            scores = masked_scores(keys, query, length)
+            top = jnp.max(scores, axis=0, keepdims=True)
+            expo = jnp.exp(scores - top)
+            total = jnp.sum(expo, axis=0, keepdims=True)
+            mixed = contract(vals, expo.astype(BF), (1, 0))
+            ctx_ref[at.rank, lines, here] = (mixed * (1.0 / total)).astype(BF)
+            lse_ref[head, :, here] = top + jnp.log(total)
+
+        for copy in copies(head)[:4]:
+            copy.start()
+
+        @pl.when(head > 0)
+        def _():
+            relay(head - 1)
+
+        @pl.when(head == 0)
+        def _():
+            ups.spread()
+            tops.spread()
+
+        @pl.when(head == 1)
+        def _():
+            downs.near()
+
+        return carry
+
+    lax.fori_loop(0, heads, attend_head, 0)
+    outs.relay()
+    relay(heads - 1)
+    ups.finish()
+    tops.finish()
+    downs.close_near()
+    for one in streams:
+        one.finish()
+
+    def drain(one, carry):
+        group = copies(one)
+        for copy in group[2:]:
+            copy.wait_recv()
+        save(one).start()
+        for copy in group:
+            copy.wait_send()
+        return carry
+
+    lax.fori_loop(0, heads, drain, 0)
+    outs.spread()
+    for slot, block in enumerate((at.rank, at.across, at.over, at.diag)):
+        for copy in saves(slot, block):
+            copy.wait()
+
+    def store(one, carry):
+        save(one).wait()
+        return carry
+
+    lax.fori_loop(0, heads, store, 0)
+    outs.finish()
+
+
+def front(x, w, up, down, top, out, lengths, chunk, ident):
+    ranks, local, width = x.shape
+    kinds, d_local, e_local = w.shape
+    f_local = up.shape[1]
+    heads = e_local // HEAD_WIDTH
+    span = ranks * local
     assert heads > 1
+    dma = pltpu.SemaphoreType.DMA
     return pl.pallas_call(
-        functools.partial(attend_send_body, chunk),
-        grid=(heads,),
+        functools.partial(front_body, chunk),
         out_shape=(
-            jax.ShapeDtypeStruct((4, width, length), BF),
-            jax.ShapeDtypeStruct((heads, 1, length), F32),
-            jax.ShapeDtypeStruct((column.shape[0], 8 * column.shape[1]), BF),
-        ),
-        in_specs=[
-            pl.BlockSpec(memory_space=pltpu.SMEM),
-            pl.BlockSpec((3, HEAD_WIDTH, length), lambda h: (0, h, 0)),
-            vmem_spec(),
-        ],
-        out_specs=(
-            any_spec(),
-            pl.BlockSpec((1, 1, length), lambda h: (h, 0, 0)),
-            any_spec(),
-        ),
-        scratch_shapes=[VMEM((4, width, length), BF), pltpu.SemaphoreType.DMA((heads,))]
-        + [pltpu.SemaphoreType.DMA((heads, 6))] * 2
-        + RingGather.scratch(),
+            jax.ShapeDtypeStruct(x.shape, BF),
+            jax.ShapeDtypeStruct(x.shape, BF),
+            jax.ShapeDtypeStruct((kinds, e_local, span), BF),
+            jax.ShapeDtypeStruct((ranks, e_local, span), BF),
+            jax.ShapeDtypeStruct((heads, 1, span), F32),
+            jax.ShapeDtypeStruct((width, f_local), BF),
+            jax.ShapeDtypeStruct((ranks * e_local, width), BF),
+            jax.ShapeDtypeStruct((f_local, width), BF),
+            jax.ShapeDtypeStruct((width, top.shape[1]), BF),
+        ),
+        in_specs=[pl.BlockSpec(memory_space=pltpu.SMEM), any_spec()] + [vmem_spec()] * 5,
+        out_specs=(any_spec(),) * 4 + (vmem_spec(),) + (any_spec(),) * 4,
+        scratch_shapes=[
+            VMEM(x.shape, BF),
+            VMEM((local, width), BF),
+            VMEM((2, local, width), BF),
+            VMEM((local, width), BF),
+            VMEM(x.shape, BF),
+            VMEM(x.shape, BF),
+            VMEM((kinds, e_local, span), BF),
+            VMEM((kinds, width, e_local), BF),
+            VMEM((kinds, e_local, width), BF),
+            VMEM((ranks, e_local, span), BF),
+            VMEM((ranks * e_local, d_local), BF),
+            dma((2,)),
+            dma((4, 3)),
+            dma((24,)),
+            dma((24,)),
+            dma((3,)),
+            dma((3,)),
+            dma((heads, 6)),
+            dma((heads, 6)),
+            dma((heads,)),
+        ]
+        + RingGather.scratch() * 5,
         compiler_params=pltpu.CompilerParams(
             collective_id=ident, has_side_effects=True, vmem_limit_bytes=BIG
         ),
-        name="attend_send",
-    )(lengths, qkv, column)
+        name="front",
+    )(lengths, x, w, up, down, top, out)
 
 
 def exact_dot(row, matrix, dims):
@@ -1310,35 +1369,32 @@
 
 
 def classify_body(
-    length_ref, bin_ref, normed_ref, up_ref, base_ref, down_ref, head_ref,
+    length_ref, bin_ref, normed_ref, up_ref, base_ref, down_in, head_full,
     slope_ref, small_ref, hidden_ref, token_ref,
-    sums, down_full, head_full, parts, send, recv, *rest,
+    sums, down_full, parts, loads, send, recv, *rest,
 ):
     at = Place()
     step = pl.program_id(0)
     last = pl.num_programs(0) - 1
     units, width = down_full.shape
     chunk = up_ref.shape[1]
-    d_local = down_ref.shape[1]
-    bins = head_ref.shape[1]
-
-    def columns(block, half):
-        lanes = pl.ds(pl.multiple_of(block * d_local, d_local), d_local)
-        if half is None:
-            return down_full.at[:, lanes]
-        return down_full.at[pl.ds(half * (units // 2), units // 2), lanes]
-
-    downs = RingGather(at, down_ref, lambda half: half_rows(down_ref, half), columns, rest[:3])
-    heads = RingGather(
-        at, head_ref, lambda half: half_rows(head_ref, half),
-        lambda block, half: rows_of(head_full, block, half, d_local), rest[3:],
-    )
+    d_local = width // 8
+    bins = head_full.shape[1]
+    slot = columns_of(down_full, d_local)
+    source = columns_of(down_in, d_local)
+    downs = RingGather(at, slot(at.group, None), lambda half: slot(at.group, half), slot, rest)
+
+    def load(index):
+        block = (at.same(at.turn(1)), at.same(at.turn(3)), at.group)[index % 3]
+        if index > 2:
+            block = block + 1 - 2 * at.core
+        return pltpu.make_async_copy(source(block, None), slot(block, None), loads.at[index])
 
     @pl.when(step == 0)
     def _():
-        at.greet(True, True)
-        downs.start()
-        heads.start()
+        at.signal(at.peers())
+        for index in range(6):
+            load(index).start()
 
     pre = jnp.dot(normed_ref[...], up_ref[...], preferred_element_type=F32)
     live = lax.broadcasted_iota(jnp.int32, pre.shape, 0) < length_ref[0]
@@ -1353,14 +1409,19 @@
     slope = half + 0.5 * pre * (1.0 - bend * bend) * inner
     slope_ref[...] = jnp.where(live, slope, 0.0).astype(BF)
 
+    @pl.when(step == 0)
+    def _():
+        at.ready(at.peers())
+        load(0).wait()
+        load(1).wait()
+        downs.pass_on()
+
     @pl.when(step == last)
     def _():
-        downs.relay()
-        heads.relay()
-        downs.spread()
-        heads.spread()
-        downs.finish()
-        heads.finish()
+        downs.far()
+        for index in range(2, 6):
+            load(index).wait()
+        downs.close_far()
         hidden_sum = sums[...]
         parts[at.rank] = exact_dot(hidden_sum, down_full[...], (1, 0))
         copies = [
@@ -1424,7 +1485,7 @@
             vmem_spec(),
             pl.BlockSpec((width, chunk), lambda f: (0, f)),
             vmem_spec(),
-            vmem_spec(),
+            any_spec(),
             vmem_spec(),
         ],
         out_specs=(
@@ -1436,12 +1497,11 @@
         scratch_shapes=[
             VMEM((1, units), F32),
             VMEM((units, width), BF),
-            VMEM((width, bins), BF),
             VMEM((4, 1, width), F32),
+            pltpu.SemaphoreType.DMA((6,)),
             pltpu.SemaphoreType.DMA((3,)),
             pltpu.SemaphoreType.DMA((3,)),
         ]
-        + RingGather.scratch()
         + RingGather.scratch(),
         compiler_params=pltpu.CompilerParams(
             collective_id=ident, has_side_effects=True, vmem_limit_bytes=BIG
@@ -1538,7 +1598,7 @@
                 total = total + self.far[step, at].astype(F32)
             put(at, total)
 
-        add_tiles(self.rows, self.tile, body)
+        add_tiles(self.far.shape[1], self.tile, body)
 
 
 def backward_body(
@@ -1546,8 +1606,8 @@
     qkv_out, out_out, up_out, small_out,
     g_second, outs, up_term, ctx, normed, loads,
     spread, g_ctx, s_held, s_acc, s_last, s_send, s_recv,
-    out_term, o_held, o_acc, o_last, o_send, o_recv,
-    out_mine, o_pair, o_own, o_far, o_sem0, o_sem1, o_sem2, o_sem3,
+    out_term, o_pair, out_sum, o_held, o_acc, o_last, o_send, o_recv,
+    o_own, o_far, o_sem0, o_sem1, o_sem2, o_sem3,
     u_pair, u_own, u_far, u_sem0, u_sem1, u_sem2, u_sem3,
     g_qkv, q_term, q_pair, q_own, q_far, q_sem0, q_sem1, q_sem2, q_sem3,
     smalls, m_send, m_recv,
@@ -1581,13 +1641,13 @@
 
     out_folds = [
         Fold(
-            at, out_term, o_held, o_acc, o_last, (o_send, o_recv), part * 3,
+            at, out_sum, o_held, o_acc, o_last, (o_send, o_recv), part * 3,
             pl.ds(part * (e_local // 2), e_local // 2), part == 0,
         )
         for part in range(2)
     ]
     up_sum = GroupSum(up_term, up_out, u_pair, u_own, u_far, (u_sem0, u_sem1, u_sem2, u_sem3))
-    out_sum = DirectSum(out_mine, o_pair, o_own, o_far, (o_sem0, o_sem1, o_sem2, o_sem3), 64)
+    out_group = DirectSum(out_term, o_pair, o_own, o_far, (o_sem0, o_sem1, o_sem2, o_sem3), 64)
 
     def qkv_sum(one):
         return DirectSum(
@@ -1608,15 +1668,35 @@
         g_ctx[here] = total.astype(BF)
 
     def put_out(here, total):
-        for group in range(groups):
-            out_mine[group, here] = total[:, group * d_local : (group + 1) * d_local].astype(BF)
+        for chip in range(4):
+            o_own[chip, here] = total[:, chip * d_local : (chip + 1) * d_local].astype(BF)
+
+    def pair_out():
+        for copy in out_group.pair_copies():
+            copy.wait()
+
+        def block(one, carry):
+            for chip in range(4):
+
+                def body(rows):
+                    here = pl.ds(pl.multiple_of(one * e_local + rows.start, 64), rows.size)
+                    out_sum[one, rows, chip * d_local : (chip + 1) * d_local] = (
+                        out_term[chip * 2 + at.core, here].astype(F32)
+                        + o_pair[chip, here].astype(F32)
+                    ).astype(BF)
+
+                add_tiles(e_local, 64, body)
+            return carry
+
+        lax.fori_loop(0, 4, block, 0)
 
     @pl.when(head == 0)
     def _():
+        at.signal(at.peers(True))
         for index in range(5):
             load(index).start()
-        at.greet(True, True, True)
         load(2).wait()
+        at.ready(at.peers(True))
         up_sum.start()
         for copy in small_copies():
             copy.start()
@@ -1652,12 +1732,13 @@
 
         def out_block(one, carry):
             rows = pl.ds(pl.multiple_of(one * e_local, e_local), e_local)
-            out_term[one] = jnp.dot(
-                ctx[rows], g_second[...], preferred_element_type=F32
-            ).astype(BF)
+            result = jnp.dot(ctx[rows], g_second[...], preferred_element_type=F32)
+            for group in range(groups):
+                out_term[group, rows] = result[:, group * d_local : (group + 1) * d_local].astype(BF)
             return carry
 
         lax.fori_loop(0, 4, out_block, 0)
+        out_group.start()
         load(4).wait()
 
     for fold in folds(head):
@@ -1681,21 +1762,21 @@
         g_vals += contract(grad, probs.astype(BF), (1, 1))
         if index == 1:
 
-            @pl.when((head > 0) & (head < end))
+            @pl.when(head > 0)
             def _():
                 qkv_sum(head - 1).middle()
 
-            @pl.when(head == end)
+            @pl.when(head == 1)
+            def _():
+                for fold in out_folds:
+                    fold.second()
+
+            @pl.when(head == 2)
             def _():
                 for fold in out_folds:
                     fold.third(put_out)
-                out_sum.start()
-                qkv_sum(head - 1).middle()
-
-            @pl.when(head == end - 1)
-            def _():
-                for fold in out_folds:
-                    fold.second()
+                for copy in out_group.far_copies():
+                    copy.start()
 
     g_qkv[HEAD_WIDTH : 2 * HEAD_WIDTH] = g_keys.astype(BF)
     g_qkv[2 * HEAD_WIDTH :] = g_vals.astype(BF)
@@ -1712,13 +1793,13 @@
             return carry
 
         lax.fori_loop(2, heads, second, 0)
+        pair_out()
         for fold in out_folds:
             fold.start()
         up_sum.relay()
 
     @pl.when(head == end)
     def _():
-        out_sum.middle()
         qkv_sum(head).middle()
         up_sum.finish()
         for copy in small_copies():
@@ -1737,7 +1818,7 @@
         def put_final(here, total):
             out_out[here] = total
 
-        out_sum.finish(put_final)
+        out_group.finish(put_final)
 
         def store(one, carry):
             def put(here, total):
@@ -1790,14 +1871,14 @@
             VMEM((width, length), BF),
             dma((heads * 6,)),
             dma((heads * 6,)),
-            VMEM((4, width, full), BF),
-            VMEM((2, width, full), BF),
-            VMEM((width, full), BF),
-            VMEM((width, full), BF),
+            VMEM((groups, 4 * width, d_local), BF),
+            VMEM((4, 4 * width, d_local), BF),
+            VMEM((4, width, full // 2), BF),
+            VMEM((2, width, full // 2), BF),
+            VMEM((width, full // 2), BF),
+            VMEM((width, full // 2), BF),
             dma((6,)),
             dma((6,)),
-            VMEM((groups, width, d_local), BF),
-            VMEM((4, width, d_local), BF),
             VMEM((4, width, d_local), BF),
             VMEM((3, width, d_local), BF),
             dma((4,)),
@@ -1851,23 +1932,25 @@
     bins = w_head.shape[1]
     exact = lax.Precision.HIGHEST
 
-    all_ids, out_columns = share_ids(token_ids, output_matrix, 11)
+    all_ids = share_ids(token_ids, 11)
     all_ids = all_ids.reshape(ranks, local_len)
     shifted = all_ids - rank * vocab_local
     inside = (shifted >= 0) & (shifted < vocab_local)
     rows = jnp.take(embed_table, jnp.clip(shifted, 0, vocab_local - 1), axis=0)
-    first, normed_one, qkv, up_full = embed(
+    chunk = min(256, span)
+    first, normed_one, qkv, context, lse, up_full, out_full, down_part, head_full = front(
         jnp.where(inside[..., None], rows, jnp.zeros((), BF)),
         query_key_value_matrix.transpose(1, 0, 2),
         up_matrix,
+        down_matrix,
+        w_head,
+        output_matrix,
+        lengths,
+        chunk,
         12,
     )
     first = first.reshape(span, width)
     normed_one = normed_one.reshape(span, width)
-    chunk = min(256, span)
-    context, lse, out_full = attend_send(
-        qkv, lengths, out_columns.reshape(ranks * e_local, d_local), chunk, 13
-    )
     context_all = context.reshape(ranks * e_local, span)
     attn = lax.dot_general(
         context_all, out_full, (((0,), (0,)), ((), ())), preferred_element_type=F32
@@ -1878,7 +1961,7 @@
     live = (jnp.arange(span, dtype=jnp.int32) < lengths[0]).astype(F32)
     second_sum = jnp.sum(second.astype(F32) * live[:, None], axis=0, keepdims=True)
     slope, packed, g_hidden, per_token = classify(
-        normed_two, up_full, second_sum, down_matrix, w_head, lengths, teacher_bins,
+        normed_two, up_full, second_sum, down_part, head_full, lengths, teacher_bins,
         min(256, f_local), 14,
     )
 

time: 225 us -> 204 us (0.907)
  Pallas kernels: 176 us -> 154 us
    pallas_call x1, Pallas kernels: 32.8 us -> 19.3 us  [classify(): pl.pallas_call(classify_body, grid=(units // chunk,), out_shape=(jax.Shap...]
    pallas_call x3 -> x2, Pallas kernels: 86.1 us -> 80.7 us  [the longest x1 73.3 us: front(): pl.pallas_call(functools.partial(front_body, chunk), out_shape=(jax.Shape...]
    pallas_call x1, Pallas kernels: 56.8 us -> 54.5 us  [backward(): pl.pallas_call(functools.partial(backward_body, chunk), grid=(heads,), ou...]
where the time goes in v2:
time: 204 us
  Pallas kernels  154 us (75%)
  local copies, waits for them, and re-layouts  17.9 us (9%)
  matrix products  16.8 us (8%)
  other arithmetic  10.7 us (5%)
  between operations  3.88 us (2%)
    pallas_call x1, Pallas kernels, front(): pl.pallas_call(functools.partial(front_body, chunk), out_shape=(jax.Shape...  73.3 us
    pallas_call x1, Pallas kernels, backward(): pl.pallas_call(functools.partial(backward_body, chunk), grid=(heads,), ou...  54.5 us
    pallas_call x1, Pallas kernels, classify(): pl.pallas_call(classify_body, grid=(units // chunk,), out_shape=(jax.Shap...  19.3 us
    gather x1, local copies, waits for them, and re-layouts, per_device_block(): rows = jnp.take(embed_table, jnp.clip(shifted, 0, vocab_local - 1), axis=0)  12.6 us
    pallas_call x1, Pallas kernels, share_ids(): pl.pallas_call(ids_body, out_shape=jax.ShapeDtypeStruct((4,) + ids.shape,...  7.38 us
    dot_general x1, matrix products, per_device_block(): lax.dot_general(normed_two, slope, over_seqs, preferred_element_type=F32)  6.16 us
    dot_general x1, matrix products, per_device_block(): lax.dot_general(context_all, out_full, (((0,), (0,)), ((), ())), preferre...  5.49 us
    unnamed x15, local copies, waits for them, and re-layouts  5.26 us

profile of v2, /device:TPU:0, one launch (start us, length us, event | category | flops | bytes accessed | tf_op | source)
XLA Modules:
  0.0 203.7 jit_solution(11082630220705689811)
XLA Ops:
  1.9 7.4 %share_ids.1 = s32[4,1,256]{2,1,0:T(1,128)} custom-call(s32[1,256]{1,0:T(1,128)} %ids_ref.1), custom_call_target="tpu_custom_call" | custom-call | tf_op jit(solution)/shard_map/share_ids/pallas_call | solution.py:1006
  9.3 0.7 compare_and_fusion
  10.0 0.7 compare_select_fusion
  10.8 12.6 %gather_fusion = bf16[1024,1024]{1,0:T(8,128)(2,1)S(1)} fusion(bf16[7632,1024]{1,0:T(8,128)(2,1)} %param.12, s32[1024]{0:T(1024)S(1)} %broadcast_clamp_fusion), kind=kCustom, calls=%fused_computation | custom fusion | bytes 4198400 | tf_op jit(solution)/shard_map/jit(_take)/gather | solution.py:1939
  23.4 1.5 select_select_fusion.x_in
  24.9 73.3 %front.1 = (bf16[4,256,1024]{2,1,0:T(8,128)(2,1)}, bf16[4,256,1024]{2,1,0:T(8,128)(2,1)}, bf16[3,256,1024]{2,1,0:T(8,128)(2,1)}, bf16[4,256,1024]{2,1,0:T(8,128)...) custom-call(s32[1]{0:T(128)} %copy.37.length_ref, ...), custom_call_target="tpu_custom_call" | custom-call | tf_op jit(solution)/shard_map/front/pallas_call | solution.py:1310
  98.3 5.5 %convert_reduce_fusion = (f32[1024]{0:T(1024)S(1)}, bf16[1024,1024]{1,0:T(8,128)(2,1)S(1)}) fusion(bf16[1024,1024]{1,0:T(8,128)(2,1)} %bitcast.34, bf16[1024,1024]{1,0:T(8,128)(2,1)} %get-tuple-element.27.out_in, bf16[4,256,1024]{2,1,0:T(8,128)(2,1)} %get-tuple-element.25), kind=kOutput, calls=%fused_computation.4 | convolution fusion | flops 2152725504 | bytes 8392704 | tf_op jit(solution)/shard_map/dot_general | solution.py:1955
  103.8 1.7 fusion.7
  105.5 1.9 fusion.5.normed_ref
  107.4 19.3 %classify.1 = (bf16[1024,1024]{1,0:T(8,128)(2,1)}, f32[1,3328]{1,0:T(1,128)}, f32[1,1024]{1,0:T(1,128)}, f32[1,1024]{1,0:T(1,128)}) custom-call(s32[1]{0:T(128)} %copy.37.length_ref, s32[1]{0:T(128)S(6)} %copy.38.bin_ref, bf16[1024,1024]{1,0:T(8,128)(2,1)} %fusion.5.normed_ref, bf16[1024,1024]{1,0:T(8,128)(2,1)} %get-tuple-element.28.up_ref, ...), custom_call_target="tpu_custom_call" | custom-call | tf_op jit(solution)/shard_map/classify/pallas_call | solution.py:1473
  126.6 0.0 copy-start
  126.6 0.0 copy-start.3
  126.7 6.2 %multiply_convert_fusion = bf16[1024,1024]{1,0:T(8,128)(2,1)} fusion(bf16[1024,1024]{1,0:T(8,128)(2,1)} %fusion.5.normed_ref, bf16[1024,1024]{1,0:T(8,128)(2,1)} %get-tuple-element.32, f32[1024]{0:T(1024)} %bitcast.47), kind=kOutput, calls=%fused_computation.15 | convolution fusion | flops 2149580800 | bytes 6295552 | tf_op jit(solution)/shard_map/dot_general | solution.py:1969
  132.8 2.5 %fusion.6 = (f32[1024]{0:T(1024)S(1)}, f32[1024,1024]{1,0:T(8,128)S(1)}) fusion(bf16[1024,1024]{1,0:T(8,128)(2,1)S(1)} %get-tuple-element.61, f32[1024]{0:T(1024)S(1)} %broadcast_multiply_fusion.1, bf16[1024,1024]{1,0:T(8,128)(2,1)S(1)} %copy-done, bf16[1024,1024]{1,0:T(8,128)(2,1)S(1)} %copy-done.3, f32[1024]{0:T(1024)S(1)} %bitcast.48), kind=kOutput, calls=%fused_computation.11 | convolution fusion | flops 2154822656 | bytes 10498048 | tf_op jit(solution)/shard_map/dot_general | solution.py:1972
  135.3 1.6 fusion.21
  137.0 1.9 add_convert_fusion.g_second_in
  138.9 54.5 %backward.1 = (f32[3,256,128]{2,1,0:T(8,128)}, f32[256,128]{1,0:T(8,128)}, f32[128,1024]{1,0:T(8,128)}, f32[8,1,3328]{2,1,0:T(1,128)}) custom-call(s32[1]{0:T(128)} %copy.37.length_ref, bf16[3,256,1024]{2,1,0:T(8,128)(2,1)} %get-tuple-element.23.qkv_ref, f32[4,1,1024]{2,1,0:T(1,128)} %get-tuple-element.24.lse_ref, f32[1,3328]{1,0:T(1,128)} %get-tuple-element.31.small_ref, ...), custom_call_target="tpu_custom_call" | custom-call | tf_op jit(solution)/shard_map/backward/pallas_call | solution.py:1843
  193.4 1.0 copy.33
  194.3 0.6 slice_reduce_fusion
  195.6 1.9 copy.22
  197.5 0.9 fusion.13
  198.4 1.8 fusion.11
  200.2 1.6 copy.39
  201.8 0.8 copy.40
  (18 shorter events, 0.1 us)
Async XLA Ops:
  126.6 6.2 %copy-start = (bf16[1024,1024]{1,0:T(8,128)(2,1)S(1)}, bf16[1024,1024]{1,0:T(8,128)(2,1)}, u32[]{:S(2)}) copy-start(bf16[1024,1024]{1,0:T(8,128)(2,1)} %get-tuple-element.28.up_ref) | copy-start | bytes 6291460
  126.6 6.2 %copy-start.3 = (bf16[1024,1024]{1,0:T(8,128)(2,1)S(1)}, bf16[1024,1024]{1,0:T(8,128)(2,1)}, u32[]{:S(2)}) copy-start(bf16[1024,1024]{1,0:T(8,128)(2,1)} %get-tuple-element.32) | copy-start | bytes 6291460
  126.7 6.2 %copy-start.4 = (f32[1,1024]{1,0:T(1,128)S(1)}, f32[1,1024]{1,0:T(1,128)}, u32[]{:S(2)}) copy-start(f32[1,1024]{1,0:T(1,128)} %get-tuple-element.33) | copy-start | bytes 12292
  135.3 1.6 copy-start.2
  193.4 8.4 %copy-start.1 = (f32[128,1024]{1,0:T(8,128)S(1)}, f32[128,1024]{1,0:T(8,128)}, u32[]{:S(2)}) copy-start(f32[128,1024]{1,0:T(8,128)} %get-tuple-element.73) | copy-start | bytes 1572868

commit v3 on v2

--- a/solution.py
+++ b/solution.py
@@ -1368,148 +1368,6 @@
     return jnp.sum(contract(stacked, matrix, dims), axis=0, keepdims=True)
 
 
-def classify_body(
-    length_ref, bin_ref, normed_ref, up_ref, base_ref, down_in, head_full,
-    slope_ref, small_ref, hidden_ref, token_ref,
-    sums, down_full, parts, loads, send, recv, *rest,
-):
-    at = Place()
-    step = pl.program_id(0)
-    last = pl.num_programs(0) - 1
-    units, width = down_full.shape
-    chunk = up_ref.shape[1]
-    d_local = width // 8
-    bins = head_full.shape[1]
-    slot = columns_of(down_full, d_local)
-    source = columns_of(down_in, d_local)
-    downs = RingGather(at, slot(at.group, None), lambda half: slot(at.group, half), slot, rest)
-
-    def load(index):
-        block = (at.same(at.turn(1)), at.same(at.turn(3)), at.group)[index % 3]
-        if index > 2:
-            block = block + 1 - 2 * at.core
-        return pltpu.make_async_copy(source(block, None), slot(block, None), loads.at[index])
-
-    @pl.when(step == 0)
-    def _():
-        at.signal(at.peers())
-        for index in range(6):
-            load(index).start()
-
-    pre = jnp.dot(normed_ref[...], up_ref[...], preferred_element_type=F32)
-    live = lax.broadcasted_iota(jnp.int32, pre.shape, 0) < length_ref[0]
-    square = pre * pre
-    bend = jnp.tanh(0.7978845608028654 * (pre * (1.0 + 0.044715 * square)))
-    half = 0.5 * (1.0 + bend)
-    act = (pre * half).astype(BF).astype(F32)
-    sums[:, pl.ds(pl.multiple_of(step * chunk, chunk), chunk)] = jnp.sum(
-        jnp.where(live, act, 0.0), axis=0, keepdims=True
-    )
-    inner = 0.7978845608028654 * (1.0 + 3 * 0.044715 * square)
-    slope = half + 0.5 * pre * (1.0 - bend * bend) * inner
-    slope_ref[...] = jnp.where(live, slope, 0.0).astype(BF)
-
-    @pl.when(step == 0)
-    def _():
-        at.ready(at.peers())
-        load(0).wait()
-        load(1).wait()
-        downs.pass_on()
-
-    @pl.when(step == last)
-    def _():
-        downs.far()
-        for index in range(2, 6):
-            load(index).wait()
-        downs.close_far()
-        hidden_sum = sums[...]
-        parts[at.rank] = exact_dot(hidden_sum, down_full[...], (1, 0))
-        copies = [
-            remote(parts.at[at.rank], parts.at[at.rank], (send, recv), index, {"tensor": peer})
-            for index, peer in enumerate((at.across, at.over, at.diag))
-        ]
-        for copy in copies:
-            copy.start()
-        for copy in copies:
-            copy.wait()
-        count = jnp.full((1, 1), length_ref[0], jnp.int32).astype(F32)
-        total = base_ref[...]
-        for index in range(4):
-            total = total + parts[index]
-        pooled = total / count
-        mean = jnp.mean(pooled, axis=-1, keepdims=True)
-        centered = pooled - mean
-        scale = lax.rsqrt(jnp.mean(centered * centered, axis=-1, keepdims=True) + EPS)
-        final = centered * scale
-        logits = exact_dot(final, head_full[...], (1, 0))
-        top = jnp.max(logits, axis=-1, keepdims=True)
-        total_exp = jnp.log(jnp.sum(jnp.exp(logits - top), axis=-1, keepdims=True)) + top
-        labels = (lax.broadcasted_iota(jnp.int32, logits.shape, 1) == bin_ref[0]).astype(F32)
-        loss = total_exp - jnp.sum(logits * labels, axis=-1, keepdims=True)
-        g_logits = (jnp.exp(logits - total_exp) - labels) / 8.0
-        g_final = exact_dot(g_logits, head_full[...], (1, 1))
-        g_pooled = scale * (
-            g_final
-            - jnp.mean(g_final, axis=-1, keepdims=True)
-            - final * jnp.mean(g_final * final, axis=-1, keepdims=True)
-        )
-        per_token = g_pooled / count
-        rounded = per_token.astype(BF)
-        token_ref[...] = per_token
-        hidden_ref[...] = contract(
-            jnp.broadcast_to(rounded.astype(F32), (8, width)).astype(BF), down_full[...], (1, 1)
-        )[:1]
-        small_ref[:, :units] = hidden_sum
-        small_ref[:, units : units + width] = rounded.astype(F32)
-        small_ref[:, units + width : units + 2 * width] = final
-        small_ref[:, units + 2 * width : units + 2 * width + bins] = g_logits
-        small_ref[:, units + 2 * width + bins :] = jnp.broadcast_to(loss, (1, 128))
-
-
-def classify(normed, up, base, down, head, lengths, bins_at, chunk, ident):
-    length, width = normed.shape
-    units = up.shape[1]
-    bins = head.shape[1]
-    return pl.pallas_call(
-        classify_body,
-        grid=(units // chunk,),
-        out_shape=(
-            jax.ShapeDtypeStruct((length, units), BF),
-            jax.ShapeDtypeStruct((1, units + 2 * width + bins + 128), F32),
-            jax.ShapeDtypeStruct((1, units), F32),
-            jax.ShapeDtypeStruct((1, width), F32),
-        ),
-        in_specs=[
-            pl.BlockSpec(memory_space=pltpu.SMEM),
-            pl.BlockSpec(memory_space=pltpu.SMEM),
-            vmem_spec(),
-            pl.BlockSpec((width, chunk), lambda f: (0, f)),
-            vmem_spec(),
-            any_spec(),
-            vmem_spec(),
-        ],
-        out_specs=(
-            pl.BlockSpec((length, chunk), lambda f: (0, f)),
-            vmem_spec(),
-            vmem_spec(),
-            vmem_spec(),
-        ),
-        scratch_shapes=[
-            VMEM((1, units), F32),
-            VMEM((units, width), BF),
-            VMEM((4, 1, width), F32),
-            pltpu.SemaphoreType.DMA((6,)),
-            pltpu.SemaphoreType.DMA((3,)),
-            pltpu.SemaphoreType.DMA((3,)),
-        ]
-        + RingGather.scratch(),
-        compiler_params=pltpu.CompilerParams(
-            collective_id=ident, has_side_effects=True, vmem_limit_bytes=BIG
-        ),
-        name="classify",
-    )(lengths, bins_at, normed, up, base, down, head)
-
-
 class Fold:
     def __init__(self, at, src, held, acc, last, sems, base, rows, x_first):
         self.at, self.src, self.held, self.acc, self.last = at, src, held, acc, last
@@ -1601,10 +1459,28 @@
         add_tiles(self.far.shape[1], self.tile, body)
 
 
-def backward_body(
-    chunk, length_ref, qkv_ref, lse_ref, small_ref, g_second_in, out_in, up_in, ctx_in, normed_in,
-    qkv_out, out_out, up_out, small_out,
-    g_second, outs, up_term, ctx, normed, loads,
+def stack_rows(rows):
+    rows = list(rows)
+    zero = jnp.zeros(rows[0].shape, F32)
+    while len(rows) * rows[0].shape[0] % 16:
+        rows.append(zero)
+    return jnp.concatenate(rows, axis=0).astype(BF)
+
+
+def split_three(values):
+    high = values.astype(BF).astype(F32)
+    middle = (values - high).astype(BF).astype(F32)
+    return high, middle, values - high - middle
+
+
+def finish_body(
+    chunk, length_ref, bin_ref, top_ref, lse_ref,
+    first_in, ctx_in, out_in, up_in, down_in, qkv_in, normed_in,
+    qkv_out, out_out, up_out, down_out, top_out, loss_out,
+    first, ctx, outs, up_full, down_full, qkv_ref, normed, loads, down_loads,
+    work, second, normed_two, turned, slope, sums, base, up_base, parts, p_send, p_recv, token, small_ref,
+    d_send, d_recv, d_local_sem,
+    g_second, up_term,
     spread, g_ctx, s_held, s_acc, s_last, s_send, s_recv,
     out_term, o_pair, out_sum, o_held, o_acc, o_last, o_send, o_recv,
     o_own, o_far, o_sem0, o_sem1, o_sem2, o_sem3,
@@ -1613,22 +1489,204 @@
     smalls, m_send, m_recv,
 ):
     at = Place()
-    head = pl.program_id(0)
-    heads = lse_ref.shape[0] * q_term.shape[0]
+    peers = at.peers(True)
+    at.signal(peers)
+    heads = lse_ref.shape[0]
     end = heads - 1
     e_local = g_ctx.shape[0]
     d_local = q_term.shape[3]
     groups = q_term.shape[1]
+    span, width = first.shape
+    units = slope.shape[1]
+    bins = top_ref.shape[1]
     half = HEAD_WIDTH // 2
     length = length_ref[0]
     scale = HEAD_WIDTH ** (-0.5)
-    span = qkv_ref.shape[2]
+    local = span // 4
+
+    pairs = (
+        (ctx_in, ctx), (out_in, outs), (first_in, first), (up_in, up_full), (qkv_in, qkv_ref), (normed_in, normed)
+    )
 
     def load(index):
-        pairs = (
-            (g_second_in, g_second), (out_in, outs), (up_in, up_term), (ctx_in, ctx), (normed_in, normed)
-        )
         return pltpu.make_async_copy(*pairs[index], loads.at[index])
+
+    slot = columns_of(down_full, d_local)
+    source = columns_of(down_in, d_local)
+    downs = RingGather(
+        at, slot(at.group, None), lambda part: slot(at.group, part), slot, (d_send, d_recv, d_local_sem)
+    )
+
+    def load_down(index):
+        block = (at.same(at.turn(1)), at.same(at.turn(3)), at.group)[index % 3]
+        if index > 2:
+            block = block + 1 - 2 * at.core
+        return pltpu.make_async_copy(source(block, None), slot(block, None), down_loads.at[index])
+
+    load(0).start()
+    load(1).start()
+    for index in range(2):
+        load_down(index).start()
+    load(2).start()
+    load(3).start()
+    for index in range(2, 6):
+        load_down(index).start()
+    load(4).start()
+    load(5).start()
+    base[...] = jnp.zeros(base.shape, F32)
+    load(0).wait()
+    load(1).wait()
+    load(2).wait()
+
+    def project_tile(tile, carry):
+        start = pl.multiple_of(tile * local, local)
+        work[...] = contract(ctx[:, pl.ds(start, local)], outs[...], (0, 0))
+
+        def body(rows):
+            here = pl.ds(pl.multiple_of(start + rows.start, 32), rows.size)
+            value = (first[here].astype(F32) + work[rows]).astype(BF)
+            second[here] = value
+            value = value.astype(F32)
+            normed_two[here] = normalize(value).astype(BF)
+            live = lax.broadcasted_iota(jnp.int32, value.shape, 0) + here.start < length
+            base[...] += jnp.sum(jnp.where(live, value, 0.0), axis=0, keepdims=True)
+
+        add_tiles(local, 32, body)
+        turned[:, pl.ds(start, local)] = normed_two[pl.ds(start, local)].T
+        return carry
+
+    lax.fori_loop(0, 1, project_tile, 0)
+    load_down(0).wait()
+    load_down(1).wait()
+    at.ready(peers)
+    downs.pass_on()
+    lax.fori_loop(1, 4, project_tile, 0)
+    load(3).wait()
+
+    def hidden_chunk(step, carry):
+        lanes = pl.ds(pl.multiple_of(step * chunk, chunk), chunk)
+        pre = jnp.dot(normed_two[...], up_full[:, lanes], preferred_element_type=F32)
+        live = lax.broadcasted_iota(jnp.int32, pre.shape, 0) < length
+        square = pre * pre
+        bend = jnp.tanh(0.7978845608028654 * (pre * (1.0 + 0.044715 * square)))
+        part = 0.5 * (1.0 + bend)
+        act = (pre * part).astype(BF).astype(F32)
+        sums[:, lanes] = jnp.sum(jnp.where(live, act, 0.0), axis=0, keepdims=True)
+        inner = 0.7978845608028654 * (1.0 + 3 * 0.044715 * square)
+        value = part + 0.5 * pre * (1.0 - bend * bend) * inner
+        slope[:, lanes] = jnp.where(live, value, 0.0).astype(BF)
+        return carry
+
+    lax.fori_loop(0, units // chunk, hidden_chunk, 0)
+    downs.far()
+    for index in range(2, 6):
+        load_down(index).wait()
+    downs.close_far()
+    hidden_sum = sums[...]
+    parts[at.rank] = exact_dot(hidden_sum, down_full[...], (1, 0))
+    part_copies = [
+        remote(parts.at[at.rank], parts.at[at.rank], (p_send, p_recv), index, peer)
+        for index, peer in enumerate(peers[:3])
+    ]
+    for copy in part_copies:
+        copy.start()
+
+    def base_chunk(step, carry):
+        lanes = pl.ds(pl.multiple_of(step * chunk, chunk), chunk)
+        up_base[:, lanes] = jnp.dot(turned[...], slope[:, lanes], preferred_element_type=F32)
+        return carry
+
+    lax.fori_loop(0, units // chunk, base_chunk, 0)
+    for copy in part_copies:
+        copy.wait()
+    count = jnp.full((1, 1), length, jnp.int32).astype(F32)
+    total = base[...]
+    for index in range(4):
+        total = total + parts[index]
+    pooled = total / count
+    mean = jnp.mean(pooled, axis=-1, keepdims=True)
+    centered = pooled - mean
+    norm_scale = lax.rsqrt(jnp.mean(centered * centered, axis=-1, keepdims=True) + EPS)
+    final = centered * norm_scale
+    logits = exact_dot(final, top_ref[...], (1, 0))
+    highest = jnp.max(logits, axis=-1, keepdims=True)
+    total_exp = jnp.log(jnp.sum(jnp.exp(logits - highest), axis=-1, keepdims=True)) + highest
+    labels = (lax.broadcasted_iota(jnp.int32, logits.shape, 1) == bin_ref[0]).astype(F32)
+    loss = total_exp - jnp.sum(logits * labels, axis=-1, keepdims=True)
+    g_logits = (jnp.exp(logits - total_exp) - labels) / 8.0
+    g_final = exact_dot(g_logits, top_ref[...], (1, 1))
+    g_pooled = norm_scale * (
+        g_final
+        - jnp.mean(g_final, axis=-1, keepdims=True)
+        - final * jnp.mean(g_final * final, axis=-1, keepdims=True)
+    )
+    per_token = g_pooled / count
+    rounded = per_token.astype(BF).astype(F32)
+    token[...] = per_token / 4.0
+    sums[...] = contract(
+        jnp.broadcast_to(rounded, (8, width)).astype(BF), down_full[...], (1, 1)
+    )[:1]
+    small_ref[:, :units] = hidden_sum
+    small_ref[:, units : units + width] = rounded
+    small_ref[:, units + width : units + 2 * width] = final
+    small_ref[:, units + 2 * width : units + 2 * width + bins] = g_logits
+    small_ref[:, units + 2 * width + bins :] = jnp.broadcast_to(loss, (1, 128))
+
+    def scale_group(group, carry):
+        def body(rows):
+            here = pl.ds(pl.multiple_of(group * d_local + rows.start, 32), rows.size)
+            up_term[group, rows] = (up_base[here] * sums[...]).astype(BF)
+
+        add_tiles(d_local, 32, body)
+        return carry
+
+    lax.fori_loop(0, groups, scale_group, 0)
+    up_sum = GroupSum(up_term, up_out, u_pair, u_own, u_far, (u_sem0, u_sem1, u_sem2, u_sem3))
+    up_sum.start()
+
+    def small_copies():
+        return [
+            remote(
+                small_ref, smalls.at[at.group], (m_send, m_recv), step - 1,
+                {"dp": lax.rem(at.group + step, groups)},
+            )
+            for step in range(1, groups)
+        ]
+
+    for copy in small_copies():
+        copy.start()
+    smalls[at.group] = small_ref[...]
+
+    def back_tile(tile, carry):
+        start = pl.multiple_of(tile * local, local)
+
+        def pre(rows):
+            here = pl.ds(pl.multiple_of(start + rows.start, 32), rows.size)
+            slope[here] = (slope[here].astype(F32) * sums[...]).astype(BF)
+
+        add_tiles(local, 32, pre)
+        work[...] = contract(slope[pl.ds(start, local)], up_full[...], (1, 1))
+
+        def body(rows):
+            here = pl.ds(pl.multiple_of(start + rows.start, 32), rows.size)
+            value = second[here].astype(F32)
+            grad = work[rows]
+            away = value - jnp.mean(value, axis=-1, keepdims=True)
+            inverse = lax.rsqrt(jnp.mean(away * away, axis=-1, keepdims=True) + EPS)
+            unit = away * inverse
+            back = inverse * (
+                grad
+                - jnp.mean(grad, axis=-1, keepdims=True)
+                - unit * jnp.mean(grad * unit, axis=-1, keepdims=True)
+            )
+            live = lax.broadcasted_iota(jnp.int32, value.shape, 0) + here.start < length
+            g_second[here] = (back + jnp.where(live, token[...], 0.0)).astype(BF)
+
+        add_tiles(local, 32, body)
+        return carry
+
+    lax.fori_loop(0, 4, back_tile, 0)
+    up_sum.middle()
 
     def folds(one):
         return [
@@ -1646,7 +1704,6 @@
         )
         for part in range(2)
     ]
-    up_sum = GroupSum(up_term, up_out, u_pair, u_own, u_far, (u_sem0, u_sem1, u_sem2, u_sem3))
     out_group = DirectSum(out_term, o_pair, o_own, o_far, (o_sem0, o_sem1, o_sem2, o_sem3), 64)
 
     def qkv_sum(one):
@@ -1654,15 +1711,6 @@
             q_term.at[one], q_pair.at[one], q_own.at[one], q_far.at[one],
             (q_sem0.at[one], q_sem1.at[one], q_sem2.at[one], q_sem3.at[one]), q_term.shape[2],
         )
-
-    def small_copies():
-        return [
-            remote(
-                small_ref, smalls.at[at.group], (m_send, m_recv), step - 1,
-                {"dp": lax.rem(at.group + step, groups)},
-            )
-            for step in range(1, groups)
-        ]
 
     def put_context(here, total):
         g_ctx[here] = total.astype(BF)
@@ -1690,180 +1738,201 @@
 
         lax.fori_loop(0, 4, block, 0)
 
-    @pl.when(head == 0)
-    def _():
-        at.signal(at.peers(True))
-        for index in range(5):
-            load(index).start()
-        load(2).wait()
-        at.ready(at.peers(True))
-        up_sum.start()
-        for copy in small_copies():
-            copy.start()
-        smalls[at.group] = small_ref[...]
-        load(0).wait()
-        load(1).wait()
-
-        def spread_head(one, carry):
-            left = jnp.concatenate(
-                [
-                    outs[pl.ds(pl.multiple_of(part * e_local + one * HEAD_WIDTH, HEAD_WIDTH), HEAD_WIDTH)]
-                    for part in range(4)
-                ],
-                axis=0,
-            )
-            result = contract(left, g_second[...], (1, 1)).astype(BF)
-            for part in range(4):
-                spread[part, pl.ds(pl.multiple_of(one * HEAD_WIDTH, HEAD_WIDTH), HEAD_WIDTH)] = result[
-                    part * HEAD_WIDTH : (part + 1) * HEAD_WIDTH
+    def spread_head(one, carry):
+        left = jnp.concatenate(
+            [
+                outs[pl.ds(pl.multiple_of(part * e_local + one * HEAD_WIDTH, HEAD_WIDTH), HEAD_WIDTH)]
+                for part in range(4)
+            ],
+            axis=0,
+        )
+        result = contract(left, g_second[...], (1, 1)).astype(BF)
+        for part in range(4):
+            spread[part, pl.ds(pl.multiple_of(one * HEAD_WIDTH, HEAD_WIDTH), HEAD_WIDTH)] = result[
+                part * HEAD_WIDTH : (part + 1) * HEAD_WIDTH
+            ]
+        for fold in folds(one):
+            fold.start()
+        return carry
+
+    lax.fori_loop(0, 2, spread_head, 0)
+    for fold in folds(0):
+        fold.second()
+    lax.fori_loop(2, heads, spread_head, 0)
+    for fold in folds(1):
+        fold.second()
+
+    def out_block(one, carry):
+        rows = pl.ds(pl.multiple_of(one * e_local, e_local), e_local)
+        result = jnp.dot(ctx[rows], g_second[...], preferred_element_type=F32)
+        for group in range(groups):
+            out_term[group, rows] = result[:, group * d_local : (group + 1) * d_local].astype(BF)
+        return carry
+
+    lax.fori_loop(0, 4, out_block, 0)
+    out_group.start()
+    load(4).wait()
+    load(5).wait()
+
+    def back_head(head, carry):
+        for fold in folds(head):
+            fold.third(put_context)
+
+        mine = pl.ds(pl.multiple_of(head * HEAD_WIDTH, HEAD_WIDTH), HEAD_WIDTH)
+        keys, vals = qkv_ref[1, mine], qkv_ref[2, mine]
+        g_keys = jnp.zeros((HEAD_WIDTH, span), F32)
+        g_vals = jnp.zeros((HEAD_WIDTH, span), F32)
+        for index, start in enumerate(range(0, span, local)):
+            here = slice(start, start + local)
+            query = (qkv_ref[0, mine, here].astype(F32) * scale).astype(BF)
+            grad = g_ctx[mine, here]
+            probs = jnp.exp(masked_scores(keys, query, length) - lse_ref[head, :, here])
+            g_probs = contract(vals, grad, (0, 0))
+            weighted = probs * g_probs
+            inner = jnp.sum(weighted, axis=0, keepdims=True)
+            g_scores = (weighted - probs * inner).astype(BF)
+            g_qkv[:HEAD_WIDTH, here] = (contract(keys, g_scores, (1, 0)) * scale).astype(BF)
+            g_keys += contract(query, g_scores, (1, 1))
+            g_vals += contract(grad, probs.astype(BF), (1, 1))
+            if index == 1:
+
+                @pl.when(head > 0)
+                def _():
+                    qkv_sum(head - 1).middle()
+
+                @pl.when(head == 1)
+                def _():
+                    for fold in out_folds:
+                        fold.second()
+
+                @pl.when(head == 2)
+                def _():
+                    for fold in out_folds:
+                        fold.third(put_out)
+                    for copy in out_group.far_copies():
+                        copy.start()
+
+        g_qkv[HEAD_WIDTH : 2 * HEAD_WIDTH] = g_keys.astype(BF)
+        g_qkv[2 * HEAD_WIDTH :] = g_vals.astype(BF)
+        result = jnp.dot(g_qkv[...], normed[...], preferred_element_type=F32)
+        for group in range(groups):
+            q_term[head, group] = result[:, group * d_local : (group + 1) * d_local].astype(BF)
+        qkv_sum(head).start()
+
+        @pl.when(head == 0)
+        def _():
+            def second(one, carry):
+                for fold in folds(one):
+                    fold.second()
+                return carry
+
+            lax.fori_loop(2, heads, second, 0)
+            pair_out()
+            for fold in out_folds:
+                fold.start()
+            up_sum.relay()
+        return carry
+
+    lax.fori_loop(0, heads, back_head, 0)
+    qkv_sum(end).middle()
+    up_sum.finish()
+    for copy in small_copies():
+        copy.wait()
+
+    def lines(start, size):
+        return [smalls[group, :, pl.ds(start, size)] for group in range(groups)]
+
+    mine_d = pl.multiple_of(at.group * d_local, d_local)
+    units_all = split_three(jnp.concatenate(lines(0, units), axis=0))
+    tokens_all = jnp.concatenate(lines(units + mine_d, d_local), axis=0)
+    down_out[...] = contract(stack_rows(units_all), stack_rows([tokens_all] * 3), (0, 0))
+    finals = split_three(jnp.concatenate(lines(units + width + mine_d, d_local), axis=0))
+    errors = split_three(jnp.concatenate(lines(units + 2 * width, bins), axis=0))
+    order = [(i, j) for i in range(3) for j in range(3) if i + j < 4]
+    top_out[...] = contract(
+        stack_rows([finals[i] for i, _ in order]), stack_rows([errors[j] for _, j in order]), (0, 0)
+    )
+    losses = jnp.concatenate(lines(units + 2 * width + bins, 128), axis=0)
+    loss_out[...] = jnp.sum(losses, axis=0, keepdims=True) / 8.0
+
+    def drain(one, carry):
+        for fold in folds(one):
+            fold.finish()
+        return carry
+
+    lax.fori_loop(0, heads, drain, 0)
+    for fold in out_folds:
+        fold.finish()
+
+    def put_final(here, total):
+        out_out[here] = total
+
+    out_group.finish(put_final)
+
+    def store(one, carry):
+        def put(here, total):
+            for kind in range(3):
+                qkv_out[kind, pl.ds(pl.multiple_of(one * HEAD_WIDTH, HEAD_WIDTH), HEAD_WIDTH)] = total[
+                    kind * HEAD_WIDTH : (kind + 1) * HEAD_WIDTH
                 ]
-            for fold in folds(one):
-                fold.start()
-            return carry
-
-        lax.fori_loop(0, 2, spread_head, 0)
-        up_sum.middle()
-        for fold in folds(0):
-            fold.second()
-        lax.fori_loop(2, heads, spread_head, 0)
-        for fold in folds(1):
-            fold.second()
-        load(3).wait()
-
-        def out_block(one, carry):
-            rows = pl.ds(pl.multiple_of(one * e_local, e_local), e_local)
-            result = jnp.dot(ctx[rows], g_second[...], preferred_element_type=F32)
-            for group in range(groups):
-                out_term[group, rows] = result[:, group * d_local : (group + 1) * d_local].astype(BF)
-            return carry
-
-        lax.fori_loop(0, 4, out_block, 0)
-        out_group.start()
-        load(4).wait()
-
-    for fold in folds(head):
-        fold.third(put_context)
-
-    keys, vals = qkv_ref[1], qkv_ref[2]
-    g_keys = jnp.zeros((HEAD_WIDTH, span), F32)
-    g_vals = jnp.zeros((HEAD_WIDTH, span), F32)
-    mine = pl.ds(pl.multiple_of(head * HEAD_WIDTH, HEAD_WIDTH), HEAD_WIDTH)
-    for index, start in enumerate(range(0, span, chunk)):
-        here = slice(start, start + chunk)
-        query = (qkv_ref[0, :, here].astype(F32) * scale).astype(BF)
-        grad = g_ctx[mine, here]
-        probs = jnp.exp(masked_scores(keys, query, length) - lse_ref[0, :, here])
-        g_probs = contract(vals, grad, (0, 0))
-        weighted = probs * g_probs
-        inner = jnp.sum(weighted, axis=0, keepdims=True)
-        g_scores = (weighted - probs * inner).astype(BF)
-        g_qkv[:HEAD_WIDTH, here] = (contract(keys, g_scores, (1, 0)) * scale).astype(BF)
-        g_keys += contract(query, g_scores, (1, 1))
-        g_vals += contract(grad, probs.astype(BF), (1, 1))
-        if index == 1:
-
-            @pl.when(head > 0)
-            def _():
-                qkv_sum(head - 1).middle()
-
-            @pl.when(head == 1)
-            def _():
-                for fold in out_folds:
-                    fold.second()
-
-            @pl.when(head == 2)
-            def _():
-                for fold in out_folds:
-                    fold.third(put_out)
-                for copy in out_group.far_copies():
-                    copy.start()
-
-    g_qkv[HEAD_WIDTH : 2 * HEAD_WIDTH] = g_keys.astype(BF)
-    g_qkv[2 * HEAD_WIDTH :] = g_vals.astype(BF)
-    result = jnp.dot(g_qkv[...], normed[...], preferred_element_type=F32)
-    for group in range(groups):
-        q_term[head, group] = result[:, group * d_local : (group + 1) * d_local].astype(BF)
-    qkv_sum(head).start()
-
-    @pl.when(head == 0)
-    def _():
-        def second(one, carry):
-            for fold in folds(one):
-                fold.second()
-            return carry
-
-        lax.fori_loop(2, heads, second, 0)
-        pair_out()
-        for fold in out_folds:
-            fold.start()
-        up_sum.relay()
-
-    @pl.when(head == end)
-    def _():
-        qkv_sum(head).middle()
-        up_sum.finish()
-        for copy in small_copies():
-            copy.wait()
-        small_out[...] = smalls[...]
-
-        def drain(one, carry):
-            for fold in folds(one):
-                fold.finish()
-            return carry
-
-        lax.fori_loop(0, heads, drain, 0)
-        for fold in out_folds:
-            fold.finish()
-
-        def put_final(here, total):
-            out_out[here] = total
-
-        out_group.finish(put_final)
-
-        def store(one, carry):
-            def put(here, total):
-                for kind in range(3):
-                    qkv_out[kind, pl.ds(pl.multiple_of(one * HEAD_WIDTH, HEAD_WIDTH), HEAD_WIDTH)] = total[
-                        kind * HEAD_WIDTH : (kind + 1) * HEAD_WIDTH
-                    ]
-
-            qkv_sum(one).finish(put)
-            return carry
-
-        lax.fori_loop(0, heads, store, 0)
-
-
-def backward(qkv, lengths, lse, small, g_second, out_full, up_term, context, normed, chunk, ident):
+
+        qkv_sum(one).finish(put)
+        return carry
+
+    lax.fori_loop(0, heads, store, 0)
+
+
+def finish(lengths, bins_at, top, lse, first, context, out_full, up, down, qkv, normed, chunk, ident):
     _, width, length = qkv.shape
+    full, units = up.shape
     heads = width // HEAD_WIDTH
-    groups, d_local, f_local = up_term.shape
-    full = out_full.shape[1]
+    groups = lax.axis_size("dp")
+    d_local = full // groups
+    bins = top.shape[1]
     rows = 3 * HEAD_WIDTH
+    small = units + 2 * full + bins + 128
     dma = pltpu.SemaphoreType.DMA
+    smem = pl.BlockSpec(memory_space=pltpu.SMEM)
     return pl.pallas_call(
-        functools.partial(backward_body, chunk),
-        grid=(heads,),
+        functools.partial(finish_body, chunk),
         out_shape=(
             jax.ShapeDtypeStruct((3, width, d_local), F32),
             jax.ShapeDtypeStruct((width, d_local), F32),
-            jax.ShapeDtypeStruct((d_local, f_local), F32),
-            jax.ShapeDtypeStruct((groups,) + small.shape, F32),
+            jax.ShapeDtypeStruct((d_local, units), F32),
+            jax.ShapeDtypeStruct((units, d_local), F32),
+            jax.ShapeDtypeStruct((d_local, bins), F32),
+            jax.ShapeDtypeStruct((1, 128), F32),
         ),
-        in_specs=[
-            pl.BlockSpec(memory_space=pltpu.SMEM),
-            pl.BlockSpec((3, HEAD_WIDTH, length), lambda h: (0, h, 0)),
-            pl.BlockSpec((1, 1, length), lambda h: (h, 0, 0)),
-            vmem_spec(),
+        in_specs=[smem, smem, vmem_spec(), vmem_spec()] + [any_spec()] * 7,
+        out_specs=(vmem_spec(),) * 6,
+        scratch_shapes=[
+            VMEM((length, full), BF),
+            VMEM(context.shape, BF),
+            VMEM(out_full.shape, BF),
+            VMEM(up.shape, BF),
+            VMEM(down.shape, BF),
+            VMEM(qkv.shape, BF),
+            VMEM(normed.shape, BF),
+            dma((6,)),
+            dma((6,)),
+            VMEM((length // 4, full), F32),
+            VMEM((length, full), BF),
+            VMEM((length, full), BF),
+            VMEM((full, length), BF),
+            VMEM((length, units), BF),
+            VMEM((1, units), F32),
+            VMEM((1, full), F32),
+            VMEM((full, units), F32),
+            VMEM((4, 1, full), F32),
+            dma((3,)),
+            dma((3,)),
+            VMEM((1, full), F32),
+            VMEM((1, small), F32),
         ]
-        + [any_spec()] * 5,
-        out_specs=(vmem_spec(),) * 4,
-        scratch_shapes=[
-            VMEM(g_second.shape, BF),
-            VMEM(out_full.shape, BF),
-            VMEM(up_term.shape, BF),
-            VMEM(context.shape, BF),
-            VMEM(normed.shape, BF),
-            dma((5,)),
+        + RingGather.scratch()
+        + [
+            VMEM((length, full), BF),
+            VMEM((groups, d_local, units), BF),
             VMEM((4, width, length), BF),
             VMEM((width, length), BF),
             VMEM((2, width, length), BF),
@@ -1886,7 +1955,7 @@
             dma((3,)),
             dma((3,)),
         ]
-        + GroupSum.scratch(up_term.shape, BF)
+        + GroupSum.scratch((groups, d_local, units), BF)
         + [
             VMEM((rows, length), BF),
             VMEM((heads, groups, rows, d_local), BF),
@@ -1897,15 +1966,15 @@
             dma((heads, 4)),
             dma((heads, 3)),
             dma((heads, 3)),
-            VMEM((groups,) + small.shape, F32),
+            VMEM((groups, 1, small), F32),
             dma((groups - 1,)),
             dma((groups - 1,)),
         ],
         compiler_params=pltpu.CompilerParams(
             collective_id=ident, has_side_effects=True, vmem_limit_bytes=BIG
         ),
-        name="backward",
-    )(lengths, qkv, lse, small, g_second, out_full, up_term, context, normed)
+        name="finish",
+    )(lengths, bins_at, top, lse, first, context, out_full, up, down, qkv, normed)
 
 
 def per_device_block(
@@ -1920,17 +1989,13 @@
     w_head,
 ):
     ranks = lax.axis_size("tensor")
-    groups = lax.axis_size("dp")
     rank = lax.axis_index("tensor")
-    group = lax.axis_index("dp")
     assert token_ids.shape[0] == 1
     local_len = token_ids.shape[1]
     span = local_len * ranks
     vocab_local, width = embed_table.shape
-    d_local, _, e_local = query_key_value_matrix.shape
+    _, _, e_local = query_key_value_matrix.shape
     f_local = up_matrix.shape[1]
-    bins = w_head.shape[1]
-    exact = lax.Precision.HIGHEST
 
     all_ids = share_ids(token_ids, 11)
     all_ids = all_ids.reshape(ranks, local_len)
@@ -1952,52 +2017,18 @@
     first = first.reshape(span, width)
     normed_one = normed_one.reshape(span, width)
     context_all = context.reshape(ranks * e_local, span)
-    attn = lax.dot_general(
-        context_all, out_full, (((0,), (0,)), ((), ())), preferred_element_type=F32
-    )
-    second = (first.astype(F32) + attn).astype(BF)
-    normed_f, norm_back = jax.vjp(normalize, second.astype(F32))
-    normed_two = normed_f.astype(BF)
-    live = (jnp.arange(span, dtype=jnp.int32) < lengths[0]).astype(F32)
-    second_sum = jnp.sum(second.astype(F32) * live[:, None], axis=0, keepdims=True)
-    slope, packed, g_hidden, per_token = classify(
-        normed_two, up_full, second_sum, down_part, head_full, lengths, teacher_bins,
-        min(256, f_local), 14,
-    )
-
-    over_seqs = (((0,), (0,)), ((), ()))
-    up_base = lax.dot_general(normed_two, slope, over_seqs, preferred_element_type=F32)
-    up_term = (up_base * g_hidden).astype(BF).reshape(groups, d_local, f_local)
-    g_pre = (slope.astype(F32) * g_hidden).astype(BF)
-    g_normed = lax.dot_general(
-        g_pre, up_full, (((1,), (1,)), ((), ())), preferred_element_type=F32
-    )
-    g_second = (
-        norm_back(g_normed)[0] + live[:, None] * (per_token / ranks)
-    ).astype(BF)
-    qkv_gradient, output_weight_gradient, up_weight_gradient, every = backward(
-        qkv, lengths, lse, packed, g_second, out_full, up_term, context_all, normed_one, chunk, 15
-    )
-    every = every[:, 0]
-    hidden_every = every[:, :f_local]
-    rounded_every = every[:, f_local : f_local + width]
-    final_every = every[:, f_local + width : f_local + 2 * width]
-    rest = every[:, f_local + 2 * width :]
-    loss = jnp.sum(rest[:, bins]) / groups
-    mine = group * d_local
-    down_weight_gradient = lax.dot_general(
-        hidden_every,
-        lax.dynamic_slice_in_dim(rounded_every, mine, d_local, axis=1),
-        over_seqs,
-        precision=exact,
-    )
-    grad_head = lax.dot_general(
-        lax.dynamic_slice_in_dim(final_every, mine, d_local, axis=1),
-        rest[:, :bins],
-        over_seqs,
-        precision=exact,
-    )
-
+    (
+        qkv_gradient,
+        output_weight_gradient,
+        up_weight_gradient,
+        down_weight_gradient,
+        grad_head,
+        losses,
+    ) = finish(
+        lengths, teacher_bins, head_full, lse, first, context_all, out_full, up_full, down_part,
+        qkv, normed_one, min(256, f_local), 15,
+    )
+    loss = losses[0, 0]
     query_key_value_gradient = qkv_gradient.transpose(2, 0, 1)
     return (
         loss,

time: 204 us -> 197 us (0.966)
  Pallas kernels: 154 us -> 171 us
  matrix products: 16.8 us -> 0 us
  other arithmetic: 10.7 us -> 2.3 us
    dot_general x5 -> x0, matrix products: 16.8 us -> none  [the longest x1 6.16 us: per_device_block(): lax.dot_general(normed_two, slope, over_seqs, preferred_element_type=F32)]
    pallas_call x2 -> x1, Pallas kernels: 73.7 us -> 90.5 us  [finish(): pl.pallas_call(functools.partial(finish_body, chunk), out_shape=(jax.Shap...]
    reduce_sum x3 -> x0, other arithmetic: 3.91 us -> none  [the longest x1 1.69 us: per_device_block(): jnp.sum(second.astype(F32) * live[:, None], axis=0, keepdims=True)]
    convert_element_type x3 -> x0, other arithmetic: 3.83 us -> none  [the longest x1 1.91 us: per_device_block(): normed_two = normed_f.astype(BF)]
    unnamed x15 -> x12, local copies, waits for them, and re-layouts: 5.26 us -> 6.86 us
where the time goes in v3:
time: 197 us
  Pallas kernels  171 us (87%)
  local copies, waits for them, and re-layouts  19.5 us (10%)
  between operations  3.8 us (2%)
  other arithmetic  2.3 us (1%)
    pallas_call x1, Pallas kernels, finish(): pl.pallas_call(functools.partial(finish_body, chunk), out_shape=(jax.Shap...  90.5 us
    pallas_call x1, Pallas kernels, front(): pl.pallas_call(functools.partial(front_body, chunk), out_shape=(jax.Shape...  73.3 us
    gather x1, local copies, waits for them, and re-layouts, per_device_block(): rows = jnp.take(embed_table, jnp.clip(shifted, 0, vocab_local - 1), axis=0)  12.6 us
    pallas_call x1, Pallas kernels, share_ids(): pl.pallas_call(ids_body, out_shape=jax.ShapeDtypeStruct((4,) + ids.shape,...  7.38 us
    unnamed x12, local copies, waits for them, and re-layouts  6.86 us

profile of v3, /device:TPU:0, one launch (start us, length us, event | category | flops | bytes accessed | tf_op | source)
XLA Modules:
  0.0 196.8 jit_solution(17663293671387129570)
XLA Ops:
  0.6 7.4 %share_ids.1 = s32[4,1,256]{2,1,0:T(1,128)} custom-call(s32[1,256]{1,0:T(1,128)} %ids_ref.1), custom_call_target="tpu_custom_call" | custom-call | tf_op jit(solution)/shard_map/share_ids/pallas_call | solution.py:1006
  8.0 0.7 compare_select_fusion
  8.7 0.0 copy-start.2
  8.8 12.6 %gather_fusion = bf16[1024,1024]{1,0:T(8,128)(2,1)S(1)} fusion(bf16[7632,1024]{1,0:T(8,128)(2,1)} %param.12, s32[1024]{0:T(1024)S(1)} %broadcast_clamp_fusion), kind=kCustom, calls=%fused_computation | custom fusion | bytes 4198400 | tf_op jit(solution)/shard_map/jit(_take)/gather | solution.py:2004
  21.4 0.0 copy-done.2
  21.4 1.6 select_select_fusion.x_in
  23.7 73.3 %front.1 = (bf16[4,256,1024]{2,1,0:T(8,128)(2,1)}, bf16[4,256,1024]{2,1,0:T(8,128)(2,1)}, bf16[3,256,1024]{2,1,0:T(8,128)(2,1)}, bf16[4,256,1024]{2,1,0:T(8,128)...) custom-call(s32[1]{0:T(128)S(6)} %copy.29.length_ref, ...), custom_call_target="tpu_custom_call" | custom-call | tf_op jit(solution)/shard_map/front/pallas_call | solution.py:1310
  97.7 90.5 %finish.1 = (f32[3,256,128]{2,1,0:T(8,128)}, f32[256,128]{1,0:T(8,128)}, f32[128,1024]{1,0:T(8,128)}, f32[1024,128]{1,0:T(8,128)}, f32[128,128]{1,0:T(8,128)}, /*index=5*/f32[1,128]{1,0:T(1,128)}) custom-call(s32[1]{0:T(128)S(6)} %copy.29.length_ref, s32[1]{0:T(128)S(6)} %copy.30.bin_ref, bf16[1024,128]{1,0:T(8,128)(2,1)} %get-tuple-element.21.top_ref, ...), custom_call_target="tpu_custom_call" | custom-call | tf_op jit(solution)/shard_map/finish/pallas_call | solution.py:1896
  188.2 0.0 copy-start
  188.2 0.0 copy-start.1
  188.2 2.0 %copy.16 = f32[128,3,256]{2,0,1:T(8,128)} copy(f32[128,3,256]{0,2,1:T(8,128)} %bitcast.22) | data formatting | bytes 786432
  190.8 1.6 copy.32
  192.4 1.9 copy.33
  194.3 0.0 copy-done
  194.3 0.8 copy.34
  195.1 0.0 copy-done.1
  195.1 0.6 copy.35
  (4 shorter events, 0.0 us)
Async XLA Ops:
  8.7 12.6 %copy-start.2 = (s32[4,1,256]{2,1,0:T(1,128)S(1)}, s32[4,1,256]{2,1,0:T(1,128)}, u32[]{:S(2)}) copy-start(s32[4,1,256]{2,1,0:T(1,128)} %share_ids.1) | copy-start | bytes 12292
  188.2 6.1 %copy-start = (f32[1024,128]{1,0:T(8,128)S(1)}, f32[1024,128]{1,0:T(8,128)}, u32[]{:S(2)}) copy-start(f32[1024,128]{1,0:T(8,128)} %get-tuple-element.60) | copy-start | bytes 1572868
  188.2 6.9 %copy-start.1 = (f32[128,128]{1,0:T(8,128)S(1)}, f32[128,128]{1,0:T(8,128)}, u32[]{:S(2)}) copy-start(f32[128,128]{1,0:T(8,128)} %get-tuple-element.61) | copy-start | bytes 196612

commit v4 on v3

--- a/solution.py
+++ b/solution.py
@@ -926,27 +926,29 @@
             copy.wait_send()
         self.keep().wait()
 
+    def start_half(self):
+        copies = self.copies()
+        for index in (0, 1, 6):
+            copies[index].start()
+        self.keep().start()
+
+    def close_half(self):
+        copies = self.copies()
+        for index in (0, 1, 6):
+            copies[index].wait()
+        self.keep().wait()
+
+    def start_rest(self):
+        copies = self.copies()
+        for index in (2, 3, 4, 5):
+            copies[index].start()
+
     def near(self):
         copies = self.copies()
-        for index in (0, 2):
-            copies[index].wait_recv()
+        copies[2].wait_recv()
         copies[7].start()
-        for index in (1, 3):
-            copies[index].wait_recv()
+        copies[3].wait_recv()
         copies[8].start()
-
-    def close_near(self):
-        copies = self.copies()
-        for index in (6, 7, 8):
-            copies[index].wait_recv()
-        for index in (0, 1, 2, 3, 6, 7, 8):
-            copies[index].wait_send()
-        self.keep().wait()
-
-    def pass_on(self):
-        copies = self.copies()
-        copies[4].start()
-        copies[5].start()
 
     def far(self):
         copies = self.copies()
@@ -954,10 +956,11 @@
         copies[5].wait_recv()
         copies[9].start()
 
-    def close_far(self):
+    def close_rest(self):
         copies = self.copies()
-        copies[9].wait_recv()
-        for index in (4, 5, 9):
+        for index in (7, 8, 9):
+            copies[index].wait_recv()
+        for index in (2, 3, 4, 5, 7, 8, 9):
             copies[index].wait_send()
 
 
@@ -1187,18 +1190,18 @@
         one.relay()
     ups.relay()
     tops.relay()
-    downs.start()
     for one in streams:
         one.beside()
+    own_columns.wait()
+    for copy in column_copies:
+        copy.wait()
+    outs.start()
+    downs.start_half()
     project(at.across, 1)
     project(at.over, 2)
     for one in streams:
         one.opposite()
     project(at.diag, 3)
-    own_columns.wait()
-    for copy in column_copies:
-        copy.wait()
-    outs.start()
 
     def copies(one):
         def copy(index, block, half, peer):
@@ -1261,18 +1264,18 @@
             ups.spread()
             tops.spread()
 
-        @pl.when(head == 1)
+        @pl.when(head == 2)
         def _():
-            downs.near()
+            outs.relay()
 
         return carry
 
     lax.fori_loop(0, heads, attend_head, 0)
-    outs.relay()
     relay(heads - 1)
+    outs.spread()
     ups.finish()
     tops.finish()
-    downs.close_near()
+    downs.close_half()
     for one in streams:
         one.finish()
 
@@ -1286,7 +1289,6 @@
         return carry
 
     lax.fori_loop(0, heads, drain, 0)
-    outs.spread()
     for slot, block in enumerate((at.rank, at.across, at.over, at.diag)):
         for copy in saves(slot, block):
             copy.wait()
@@ -1305,7 +1307,7 @@
     f_local = up.shape[1]
     heads = e_local // HEAD_WIDTH
     span = ranks * local
-    assert heads > 1
+    assert heads > 2
     dma = pltpu.SemaphoreType.DMA
     return pl.pallas_call(
         functools.partial(front_body, chunk),
@@ -1477,7 +1479,7 @@
     chunk, length_ref, bin_ref, top_ref, lse_ref,
     first_in, ctx_in, out_in, up_in, down_in, qkv_in, normed_in,
     qkv_out, out_out, up_out, down_out, top_out, loss_out,
-    first, ctx, outs, up_full, down_full, qkv_ref, normed, loads, down_loads,
+    first, ctx, outs, up_full, down_full, qkv_ref, normed, loads, tile_loads, down_loads, stats,
     work, second, normed_two, turned, slope, sums, base, up_base, parts, p_send, p_recv, token, small_ref,
     d_send, d_recv, d_local_sem,
     g_second, up_term,
@@ -1486,7 +1488,7 @@
     o_own, o_far, o_sem0, o_sem1, o_sem2, o_sem3,
     u_pair, u_own, u_far, u_sem0, u_sem1, u_sem2, u_sem3,
     g_qkv, q_term, q_pair, q_own, q_far, q_sem0, q_sem1, q_sem2, q_sem3,
-    smalls, m_send, m_recv,
+    smalls, m_send, m_recv, q_all,
 ):
     at = Place()
     peers = at.peers(True)
@@ -1504,12 +1506,17 @@
     scale = HEAD_WIDTH ** (-0.5)
     local = span // 4
 
-    pairs = (
-        (ctx_in, ctx), (out_in, outs), (first_in, first), (up_in, up_full), (qkv_in, qkv_ref), (normed_in, normed)
-    )
+    pairs = ((out_in, outs), (up_in, up_full), (qkv_in, qkv_ref), (normed_in, normed))
 
     def load(index):
         return pltpu.make_async_copy(*pairs[index], loads.at[index])
+
+    def load_tile(tile):
+        here = pl.ds(pl.multiple_of(tile * local, local), local)
+        return (
+            pltpu.make_async_copy(ctx_in.at[:, here], ctx.at[:, here], tile_loads.at[tile, 0]),
+            pltpu.make_async_copy(first_in.at[here], first.at[here], tile_loads.at[tile, 1]),
+        )
 
     slot = columns_of(down_full, d_local)
     source = columns_of(down_in, d_local)
@@ -1518,50 +1525,60 @@
     )
 
     def load_down(index):
-        block = (at.same(at.turn(1)), at.same(at.turn(3)), at.group)[index % 3]
-        if index > 2:
-            block = block + 1 - 2 * at.core
-        return pltpu.make_async_copy(source(block, None), slot(block, None), down_loads.at[index])
+        other = at.group + 1 - 2 * at.core
+        ends = ((at.same(at.turn(3)), 0), (at.same(at.turn(1)), 1), (at.group, None), (other, None))
+        return pltpu.make_async_copy(
+            source(*ends[index]), slot(*ends[index]), down_loads.at[index]
+        )
 
     load(0).start()
+    for copy in load_tile(0):
+        copy.start()
+    for index in range(3):
+        load_down(index).start()
+    for tile in range(1, 4):
+        for copy in load_tile(tile):
+            copy.start()
     load(1).start()
-    for index in range(2):
-        load_down(index).start()
+    load_down(3).start()
     load(2).start()
     load(3).start()
-    for index in range(2, 6):
-        load_down(index).start()
-    load(4).start()
-    load(5).start()
     base[...] = jnp.zeros(base.shape, F32)
     load(0).wait()
-    load(1).wait()
-    load(2).wait()
 
     def project_tile(tile, carry):
+        for copy in load_tile(tile):
+            copy.wait()
         start = pl.multiple_of(tile * local, local)
         work[...] = contract(ctx[:, pl.ds(start, local)], outs[...], (0, 0))
 
         def body(rows):
-            here = pl.ds(pl.multiple_of(start + rows.start, 32), rows.size)
+            here = pl.ds(pl.multiple_of(start + rows.start, 64), rows.size)
             value = (first[here].astype(F32) + work[rows]).astype(BF)
             second[here] = value
             value = value.astype(F32)
-            normed_two[here] = normalize(value).astype(BF)
+            mean = jnp.mean(value, axis=-1, keepdims=True)
+            away = value - mean
+            inverse = lax.rsqrt(jnp.mean(away * away, axis=-1, keepdims=True) + EPS)
+            normed_two[here] = (away * inverse).astype(BF)
+            stats[0, here] = jnp.broadcast_to(mean, (rows.size, 128))
+            stats[1, here] = jnp.broadcast_to(inverse, (rows.size, 128))
             live = lax.broadcasted_iota(jnp.int32, value.shape, 0) + here.start < length
-            base[...] += jnp.sum(jnp.where(live, value, 0.0), axis=0, keepdims=True)
-
-        add_tiles(local, 32, body)
+            base[...] += jnp.sum(
+                jnp.where(live, value, 0.0).reshape(rows.size // 8, 8, width), axis=0
+            )
+
+        add_tiles(local, 64, body)
         turned[:, pl.ds(start, local)] = normed_two[pl.ds(start, local)].T
         return carry
 
     lax.fori_loop(0, 1, project_tile, 0)
-    load_down(0).wait()
-    load_down(1).wait()
+    for index in range(3):
+        load_down(index).wait()
     at.ready(peers)
-    downs.pass_on()
+    downs.start_rest()
     lax.fori_loop(1, 4, project_tile, 0)
-    load(3).wait()
+    load(1).wait()
 
     def hidden_chunk(step, carry):
         lanes = pl.ds(pl.multiple_of(step * chunk, chunk), chunk)
@@ -1578,10 +1595,10 @@
         return carry
 
     lax.fori_loop(0, units // chunk, hidden_chunk, 0)
+    load_down(3).wait()
+    downs.near()
     downs.far()
-    for index in range(2, 6):
-        load_down(index).wait()
-    downs.close_far()
+    downs.close_rest()
     hidden_sum = sums[...]
     parts[at.rank] = exact_dot(hidden_sum, down_full[...], (1, 0))
     part_copies = [
@@ -1600,7 +1617,7 @@
     for copy in part_copies:
         copy.wait()
     count = jnp.full((1, 1), length, jnp.int32).astype(F32)
-    total = base[...]
+    total = jnp.sum(base[...], axis=0, keepdims=True)
     for index in range(4):
         total = total + parts[index]
     pooled = total / count
@@ -1661,32 +1678,31 @@
         start = pl.multiple_of(tile * local, local)
 
         def pre(rows):
-            here = pl.ds(pl.multiple_of(start + rows.start, 32), rows.size)
+            here = pl.ds(pl.multiple_of(start + rows.start, 64), rows.size)
             slope[here] = (slope[here].astype(F32) * sums[...]).astype(BF)
 
-        add_tiles(local, 32, pre)
+        add_tiles(local, 64, pre)
         work[...] = contract(slope[pl.ds(start, local)], up_full[...], (1, 1))
 
         def body(rows):
-            here = pl.ds(pl.multiple_of(start + rows.start, 32), rows.size)
-            value = second[here].astype(F32)
+            here = pl.ds(pl.multiple_of(start + rows.start, 64), rows.size)
             grad = work[rows]
-            away = value - jnp.mean(value, axis=-1, keepdims=True)
-            inverse = lax.rsqrt(jnp.mean(away * away, axis=-1, keepdims=True) + EPS)
-            unit = away * inverse
+            inverse = stats[1, here, :1]
+            unit = (second[here].astype(F32) - stats[0, here, :1]) * inverse
             back = inverse * (
                 grad
                 - jnp.mean(grad, axis=-1, keepdims=True)
                 - unit * jnp.mean(grad * unit, axis=-1, keepdims=True)
             )
-            live = lax.broadcasted_iota(jnp.int32, value.shape, 0) + here.start < length
+            live = lax.broadcasted_iota(jnp.int32, grad.shape, 0) + here.start < length
             g_second[here] = (back + jnp.where(live, token[...], 0.0)).astype(BF)
 
-        add_tiles(local, 32, body)
+        add_tiles(local, 64, body)
         return carry
 
-    lax.fori_loop(0, 4, back_tile, 0)
+    lax.fori_loop(0, 1, back_tile, 0)
     up_sum.middle()
+    lax.fori_loop(1, 4, back_tile, 0)
 
     def folds(one):
         return [
@@ -1755,13 +1771,6 @@
             fold.start()
         return carry
 
-    lax.fori_loop(0, 2, spread_head, 0)
-    for fold in folds(0):
-        fold.second()
-    lax.fori_loop(2, heads, spread_head, 0)
-    for fold in folds(1):
-        fold.second()
-
     def out_block(one, carry):
         rows = pl.ds(pl.multiple_of(one * e_local, e_local), e_local)
         result = jnp.dot(ctx[rows], g_second[...], preferred_element_type=F32)
@@ -1769,10 +1778,18 @@
             out_term[group, rows] = result[:, group * d_local : (group + 1) * d_local].astype(BF)
         return carry
 
-    lax.fori_loop(0, 4, out_block, 0)
+    lax.fori_loop(0, 2, spread_head, 0)
+    lax.fori_loop(0, 2, out_block, 0)
+    for fold in folds(0):
+        fold.second()
+    lax.fori_loop(2, heads, spread_head, 0)
+    for fold in folds(1):
+        fold.second()
+    lax.fori_loop(2, 4, out_block, 0)
     out_group.start()
-    load(4).wait()
-    load(5).wait()
+    up_sum.relay()
+    load(2).wait()
+    load(3).wait()
 
     def back_head(head, carry):
         for fold in folds(head):
@@ -1800,6 +1817,8 @@
                 def _():
                     qkv_sum(head - 1).middle()
 
+            if index == 3:
+
                 @pl.when(head == 1)
                 def _():
                     for fold in out_folds:
@@ -1830,7 +1849,6 @@
             pair_out()
             for fold in out_folds:
                 fold.start()
-            up_sum.relay()
         return carry
 
     lax.fori_loop(0, heads, back_head, 0)
@@ -1872,7 +1890,7 @@
     def store(one, carry):
         def put(here, total):
             for kind in range(3):
-                qkv_out[kind, pl.ds(pl.multiple_of(one * HEAD_WIDTH, HEAD_WIDTH), HEAD_WIDTH)] = total[
+                q_all[kind, pl.ds(pl.multiple_of(one * HEAD_WIDTH, HEAD_WIDTH), HEAD_WIDTH)] = total[
                     kind * HEAD_WIDTH : (kind + 1) * HEAD_WIDTH
                 ]
 
@@ -1880,6 +1898,8 @@
         return carry
 
     lax.fori_loop(0, heads, store, 0)
+    for kind in range(3):
+        qkv_out[kind] = q_all[kind].T
 
 
 def finish(lengths, bins_at, top, lse, first, context, out_full, up, down, qkv, normed, chunk, ident):
@@ -1896,7 +1916,7 @@
     return pl.pallas_call(
         functools.partial(finish_body, chunk),
         out_shape=(
-            jax.ShapeDtypeStruct((3, width, d_local), F32),
+            jax.ShapeDtypeStruct((3, d_local, width), F32),
             jax.ShapeDtypeStruct((width, d_local), F32),
             jax.ShapeDtypeStruct((d_local, units), F32),
             jax.ShapeDtypeStruct((units, d_local), F32),
@@ -1913,15 +1933,17 @@
             VMEM(down.shape, BF),
             VMEM(qkv.shape, BF),
             VMEM(normed.shape, BF),
-            dma((6,)),
-            dma((6,)),
+            dma((4,)),
+            dma((4, 2)),
+            dma((4,)),
+            VMEM((2, length, 128), F32),
             VMEM((length // 4, full), F32),
             VMEM((length, full), BF),
             VMEM((length, full), BF),
             VMEM((full, length), BF),
             VMEM((length, units), BF),
             VMEM((1, units), F32),
-            VMEM((1, full), F32),
+            VMEM((8, full), F32),
             VMEM((full, units), F32),
             VMEM((4, 1, full), F32),
             dma((3,)),
@@ -1969,6 +1991,7 @@
             VMEM((groups, 1, small), F32),
             dma((groups - 1,)),
             dma((groups - 1,)),
+            VMEM((3, width, d_local), F32),
         ],
         compiler_params=pltpu.CompilerParams(
             collective_id=ident, has_side_effects=True, vmem_limit_bytes=BIG
@@ -2029,7 +2052,7 @@
         qkv, normed_one, min(256, f_local), 15,
     )
     loss = losses[0, 0]
-    query_key_value_gradient = qkv_gradient.transpose(2, 0, 1)
+    query_key_value_gradient = qkv_gradient.transpose(1, 0, 2)
     return (
         loss,
         query_key_value_gradient,

time: 197 us -> 185 us (0.939)
  Pallas kernels: 171 us -> 159 us
    pallas_call x1, Pallas kernels: 90.5 us -> 80.7 us  [finish(): pl.pallas_call(functools.partial(finish_body, chunk), out_shape=(jax.Shap...]
    pallas_call x1, Pallas kernels: 73.3 us -> 70.7 us  [front(): pl.pallas_call(functools.partial(front_body, chunk), out_shape=(jax.Shape...]
where the time goes in v4:
time: 185 us; the launch traced here: 184 us
  Pallas kernels  159 us (86%)
  local copies, waits for them, and re-layouts  19.3 us (10%)
  between operations  3.85 us (2%)
  other arithmetic  2.3 us (1%)
    pallas_call x1, Pallas kernels, finish(): pl.pallas_call(functools.partial(finish_body, chunk), out_shape=(jax.Shap...  80.7 us
    pallas_call x1, Pallas kernels, front(): pl.pallas_call(functools.partial(front_body, chunk), out_shape=(jax.Shape...  70.7 us
    gather x1, local copies, waits for them, and re-layouts, per_device_block(): rows = jnp.take(embed_table, jnp.clip(shifted, 0, vocab_local - 1), axis=0)  12.6 us
    pallas_call x1, Pallas kernels, share_ids(): pl.pallas_call(ids_body, out_shape=jax.ShapeDtypeStruct((4,) + ids.shape,...  7.38 us
    unnamed x12, local copies, waits for them, and re-layouts  6.66 us

profile of v4, /device:TPU:0, one launch (start us, length us, event | category | flops | bytes accessed | tf_op | source)
XLA Modules:
  0.0 184.2 jit_solution(1823384154862570829)
XLA Ops:
  0.6 7.4 %share_ids.1 = s32[4,1,256]{2,1,0:T(1,128)} custom-call(s32[1,256]{1,0:T(1,128)} %ids_ref.1), custom_call_target="tpu_custom_call" | custom-call | tf_op jit(solution)/shard_map/share_ids/pallas_call | solution.py:1009
  8.0 0.7 compare_select_fusion
  8.7 0.0 copy-start.2
  8.8 12.6 %gather_fusion = bf16[1024,1024]{1,0:T(8,128)(2,1)S(1)} fusion(bf16[7632,1024]{1,0:T(8,128)(2,1)} %param.12, s32[1024]{0:T(1024)S(1)} %broadcast_clamp_fusion), kind=kCustom, calls=%fused_computation | custom fusion | bytes 4198400 | tf_op jit(solution)/shard_map/jit(_take)/gather | solution.py:2027
  21.4 0.0 copy-done.2
  21.4 1.6 select_select_fusion.x_in
  23.7 70.7 %front.1 = (bf16[4,256,1024]{2,1,0:T(8,128)(2,1)}, bf16[4,256,1024]{2,1,0:T(8,128)(2,1)}, bf16[3,256,1024]{2,1,0:T(8,128)(2,1)}, bf16[4,256,1024]{2,1,0:T(8,128)...) custom-call(s32[1]{0:T(128)S(6)} %copy.28.length_ref, ...), custom_call_target="tpu_custom_call" | custom-call | tf_op jit(solution)/shard_map/front/pallas_call | solution.py:1312
  95.0 80.7 %finish.1 = (f32[3,128,256]{2,1,0:T(8,128)}, f32[256,128]{1,0:T(8,128)}, f32[128,1024]{1,0:T(8,128)}, f32[1024,128]{1,0:T(8,128)}, f32[128,128]{1,0:T(8,128)}, /*index=5*/f32[1,128]{1,0:T(1,128)}) custom-call(s32[1]{0:T(128)S(6)} %copy.28.length_ref, s32[1]{0:T(128)S(6)} %copy.29.bin_ref, bf16[1024,128]{1,0:T(8,128)(2,1)} %get-tuple-element.21.top_ref, ...), custom_call_target="tpu_custom_call" | custom-call | tf_op jit(solution)/shard_map/finish/pallas_call | solution.py:1916
  175.7 0.0 copy-start
  175.7 0.0 copy-start.1
  176.4 1.8 copy.31
  178.1 1.6 copy.32
  179.7 1.9 %copy.33 = f32[128,1024]{1,0:T(8,128)} copy(f32[128,1024]{1,0:T(8,128)} %get-tuple-element.47) | data formatting | bytes 1048576
  181.6 0.0 copy-done
  181.6 0.8 copy.34
  182.4 0.0 copy-done.1
  182.4 0.6 copy.35
  (4 shorter events, 0.0 us)
Async XLA Ops:
  8.7 12.6 %copy-start.2 = (s32[4,1,256]{2,1,0:T(1,128)S(1)}, s32[4,1,256]{2,1,0:T(1,128)}, u32[]{:S(2)}) copy-start(s32[4,1,256]{2,1,0:T(1,128)} %share_ids.1) | copy-start | bytes 12292
  175.7 5.9 %copy-start = (f32[1024,128]{1,0:T(8,128)S(1)}, f32[1024,128]{1,0:T(8,128)}, u32[]{:S(2)}) copy-start(f32[1024,128]{1,0:T(8,128)} %get-tuple-element.48) | copy-start | bytes 1572868
  175.7 6.7 %copy-start.1 = (f32[128,128]{1,0:T(8,128)S(1)}, f32[128,128]{1,0:T(8,128)}, u32[]{:S(2)}) copy-start(f32[128,128]{1,0:T(8,128)} %get-tuple-element.49) | copy-start | bytes 196612

commit v5 on v4

--- a/solution.py
+++ b/solution.py
@@ -1087,9 +1087,9 @@
 
 
 def front_body(
-    chunk, length_ref, x_in, w_ref, up_ref, down_ref, head_ref, out_ref,
+    chunk, vocab, length_ref, ids_ref, x_in, w_ref, up_ref, down_ref, head_ref, out_ref,
     first_out, normed_out, qkv_out, ctx_out, lse_ref, up_out, out_full, down_out, head_out,
-    x_ref, acc, held, last, whole, normed, qkv_ref, w_full, w_turn, ctx_ref, cols,
+    x_ref, mask, acc, held, last, whole, normed, qkv_ref, w_full, w_turn, ctx_ref, cols,
     load, saved, send, recv, col_send, col_recv, ctx_send, ctx_recv, ctx_saved, *rest,
 ):
     at = Place()
@@ -1129,9 +1129,22 @@
         for index, peer in enumerate(peers[:3])
     ]
 
+    entry.wait()
+    lines = mask.shape[1]
+    for block in range(4):
+        shifted = ids_ref[block] - at.rank * vocab
+        inside = ((shifted >= 0) & (shifted < vocab)).astype(F32)
+        mask[...] = jnp.broadcast_to(inside, (lines, local)).T
+
+        def keep(rows, block=block):
+            here = mask[rows]
+            for start in range(0, x_ref.shape[2], lines):
+                cut = slice(start, start + lines)
+                x_ref[block, rows, cut] = (x_ref[block, rows, cut].astype(F32) * here).astype(BF)
+
+        add_tiles(local, 64, keep)
     at.ready(peers)
     weights.start()
-    entry.wait()
     part = local // 4
     streams = [
         Stream(
@@ -1170,7 +1183,7 @@
         def tile(here):
             normed[block, here] = normalize(whole[block, here].astype(F32)).astype(BF)
 
-        add_tiles(local, 32, tile)
+        add_tiles(local, 64, tile)
         base = pl.multiple_of(block * local, local)
 
         def matrix(index, carry):
@@ -1301,7 +1314,7 @@
     outs.finish()
 
 
-def front(x, w, up, down, top, out, lengths, chunk, ident):
+def front(ids, x, w, up, down, top, out, lengths, vocab, chunk, ident):
     ranks, local, width = x.shape
     kinds, d_local, e_local = w.shape
     f_local = up.shape[1]
@@ -1310,7 +1323,7 @@
     assert heads > 2
     dma = pltpu.SemaphoreType.DMA
     return pl.pallas_call(
-        functools.partial(front_body, chunk),
+        functools.partial(front_body, chunk, vocab),
         out_shape=(
             jax.ShapeDtypeStruct(x.shape, BF),
             jax.ShapeDtypeStruct(x.shape, BF),
@@ -1322,10 +1335,11 @@
             jax.ShapeDtypeStruct((f_local, width), BF),
             jax.ShapeDtypeStruct((width, top.shape[1]), BF),
         ),
-        in_specs=[pl.BlockSpec(memory_space=pltpu.SMEM), any_spec()] + [vmem_spec()] * 5,
+        in_specs=[pl.BlockSpec(memory_space=pltpu.SMEM), vmem_spec(), any_spec()] + [vmem_spec()] * 5,
         out_specs=(any_spec(),) * 4 + (vmem_spec(),) + (any_spec(),) * 4,
         scratch_shapes=[
             VMEM(x.shape, BF),
+            VMEM((local, 128), F32),
             VMEM((local, width), BF),
             VMEM((2, local, width), BF),
             VMEM((local, width), BF),
@@ -1351,7 +1365,7 @@
             collective_id=ident, has_side_effects=True, vmem_limit_bytes=BIG
         ),
         name="front",
-    )(lengths, x, w, up, down, top, out)
+    )(lengths, ids, x, w, up, down, top, out)
 
 
 def exact_dot(row, matrix, dims):
@@ -1445,20 +1459,45 @@
                 ).astype(BF)
 
             add_tiles(self.rows, self.tile, body)
+        self.send()
+
+    def send(self):
         for copy in self.far_copies():
             copy.start()
 
-    def finish(self, put):
+    def settle(self):
         for copy in self.far_copies():
             copy.wait()
+        return self.chips - 1
+
+    def finish(self, put):
+        steps = self.settle()
 
         def body(at):
             total = self.mine[self.chip, at].astype(F32)
-            for step in range(self.chips - 1):
+            for step in range(steps):
                 total = total + self.far[step, at].astype(F32)
             put(at, total)
 
         add_tiles(self.far.shape[1], self.tile, body)
+
+
+class RelaySum(DirectSum):
+    def __init__(self, *args):
+        super().__init__(*args)
+        self.rows = self.far.shape[1]
+
+    def send(self):
+        for copy in self.ring_copies()[:4]:
+            copy.start()
+
+    def settle(self):
+        copies = self.ring_copies()
+        for copy in copies[2:]:
+            copy.wait()
+        for copy in copies[:2]:
+            copy.wait_send()
+        return 2
 
 
 def stack_rows(rows):
@@ -1720,10 +1759,10 @@
         )
         for part in range(2)
     ]
-    out_group = DirectSum(out_term, o_pair, o_own, o_far, (o_sem0, o_sem1, o_sem2, o_sem3), 64)
-
-    def qkv_sum(one):
-        return DirectSum(
+    out_group = RelaySum(out_term, o_pair, o_own, o_far, (o_sem0, o_sem1, o_sem2, o_sem3), 64)
+
+    def qkv_sum(one, kind=RelaySum):
+        return kind(
             q_term.at[one], q_pair.at[one], q_own.at[one], q_far.at[one],
             (q_sem0.at[one], q_sem1.at[one], q_sem2.at[one], q_sem3.at[one]), q_term.shape[2],
         )
@@ -1811,13 +1850,21 @@
             g_qkv[:HEAD_WIDTH, here] = (contract(keys, g_scores, (1, 0)) * scale).astype(BF)
             g_keys += contract(query, g_scores, (1, 1))
             g_vals += contract(grad, probs.astype(BF), (1, 1))
-            if index == 1:
+            if index == 0:
 
                 @pl.when(head > 0)
                 def _():
                     qkv_sum(head - 1).middle()
 
             if index == 3:
+
+                @pl.when(head > 0)
+                def _():
+                    qkv_sum(head - 1).relay()
+
+                @pl.when(head == end)
+                def _():
+                    out_group.relay()
 
                 @pl.when(head == 1)
                 def _():
@@ -1828,8 +1875,7 @@
                 def _():
                     for fold in out_folds:
                         fold.third(put_out)
-                    for copy in out_group.far_copies():
-                        copy.start()
+                    out_group.send()
 
         g_qkv[HEAD_WIDTH : 2 * HEAD_WIDTH] = g_keys.astype(BF)
         g_qkv[2 * HEAD_WIDTH :] = g_vals.astype(BF)
@@ -1852,7 +1898,7 @@
         return carry
 
     lax.fori_loop(0, heads, back_head, 0)
-    qkv_sum(end).middle()
+    qkv_sum(end, DirectSum).middle()
     up_sum.finish()
     for copy in small_copies():
         copy.wait()
@@ -1887,17 +1933,18 @@
 
     out_group.finish(put_final)
 
-    def store(one, carry):
+    def store(one, kind):
         def put(here, total):
             for kind in range(3):
                 q_all[kind, pl.ds(pl.multiple_of(one * HEAD_WIDTH, HEAD_WIDTH), HEAD_WIDTH)] = total[
                     kind * HEAD_WIDTH : (kind + 1) * HEAD_WIDTH
                 ]
 
-        qkv_sum(one).finish(put)
-        return carry
-
-    lax.fori_loop(0, heads, store, 0)
+        qkv_sum(one, kind).finish(put)
+
+    for one in range(end):
+        store(one, RelaySum)
+    store(end, DirectSum)
     for kind in range(3):
         qkv_out[kind] = q_all[kind].T
 
@@ -1974,8 +2021,8 @@
             VMEM((3, width, d_local), BF),
             dma((4,)),
             dma((4,)),
-            dma((3,)),
-            dma((3,)),
+            dma((6,)),
+            dma((6,)),
         ]
         + GroupSum.scratch((groups, d_local, units), BF)
         + [
@@ -1986,8 +2033,8 @@
             VMEM((heads, 3, rows, d_local), BF),
             dma((heads, 4)),
             dma((heads, 4)),
-            dma((heads, 3)),
-            dma((heads, 3)),
+            dma((heads, 6)),
+            dma((heads, 6)),
             VMEM((groups, 1, small), F32),
             dma((groups - 1,)),
             dma((groups - 1,)),
@@ -1998,6 +2045,22 @@
         ),
         name="finish",
     )(lengths, bins_at, top, lse, first, context, out_full, up, down, qkv, normed)
+
+
+def hand_over_body(*refs):
+    half = len(refs) // 2
+    for source, target in zip(refs[:half], refs[half:]):
+        target[...] = source[...]
+
+
+def hand_over(*arrays):
+    return pl.pallas_call(
+        hand_over_body,
+        out_shape=tuple(jax.ShapeDtypeStruct(one.shape, one.dtype) for one in arrays),
+        in_specs=[vmem_spec()] * len(arrays),
+        out_specs=(vmem_spec(),) * len(arrays),
+        name="hand_over",
+    )(*arrays)
 
 
 def per_device_block(
@@ -2021,19 +2084,19 @@
     f_local = up_matrix.shape[1]
 
     all_ids = share_ids(token_ids, 11)
-    all_ids = all_ids.reshape(ranks, local_len)
-    shifted = all_ids - rank * vocab_local
-    inside = (shifted >= 0) & (shifted < vocab_local)
-    rows = jnp.take(embed_table, jnp.clip(shifted, 0, vocab_local - 1), axis=0)
+    shifted = all_ids.reshape(span) - rank * vocab_local
+    rows = embed_table.at[jnp.clip(shifted, 0, vocab_local - 1)].get(mode="promise_in_bounds")
     chunk = min(256, span)
     first, normed_one, qkv, context, lse, up_full, out_full, down_part, head_full = front(
-        jnp.where(inside[..., None], rows, jnp.zeros((), BF)),
+        all_ids,
+        rows.reshape(ranks, local_len, width),
         query_key_value_matrix.transpose(1, 0, 2),
         up_matrix,
         down_matrix,
         w_head,
         output_matrix,
         lengths,
+        vocab_local,
         chunk,
         12,
     )
@@ -2051,6 +2114,21 @@
         lengths, teacher_bins, head_full, lse, first, context_all, out_full, up_full, down_part,
         qkv, normed_one, min(256, f_local), 15,
     )
+    (
+        qkv_gradient,
+        output_weight_gradient,
+        up_weight_gradient,
+        down_weight_gradient,
+        grad_head,
+        losses,
+    ) = hand_over(
+        qkv_gradient,
+        output_weight_gradient,
+        up_weight_gradient,
+        down_weight_gradient,
+        grad_head,
+        losses,
+    )
     loss = losses[0, 0]
     query_key_value_gradient = qkv_gradient.transpose(1, 0, 2)
     return (

time: 185 us -> 176 us (0.951)
  local copies, waits for them, and re-layouts: 19.3 us -> 13.7 us
  between operations: 3.85 us -> 1.96 us
    unnamed x12 -> x0, local copies, waits for them, and re-layouts: 6.66 us -> none
    select_n x2 -> x1, other arithmetic: 2.27 us -> 0.01 us  [per_device_block(): embed_table.at[jnp.clip(shifted, 0, vocab_local - 1)]]
    pallas_call x1 -> x2, Pallas kernels: 70.7 us -> 72.3 us  [the longest x1 69.7 us: front(): pl.pallas_call(functools.partial(front_body, chunk, vocab), out_shape=(ja...]
where the time goes in v5:
time: 176 us
  Pallas kernels  160 us (91%)
  local copies, waits for them, and re-layouts  13.7 us (8%)
  between operations  1.96 us (1%)
    pallas_call x1, Pallas kernels, finish(): pl.pallas_call(functools.partial(finish_body, chunk), out_shape=(jax.Shap...  79.8 us
    pallas_call x1, Pallas kernels, front(): pl.pallas_call(functools.partial(front_body, chunk, vocab), out_shape=(ja...  69.7 us
    gather x1, local copies, waits for them, and re-layouts, per_device_block(): embed_table.at[jnp.clip(shifted, 0, vocab_local - 1)]  13.7 us
    pallas_call x1, Pallas kernels, share_ids(): pl.pallas_call(ids_body, out_shape=jax.ShapeDtypeStruct((4,) + ids.shape,...  7.38 us

profile of v5, /device:TPU:0, one launch (start us, length us, event | category | flops | bytes accessed | tf_op | source)
XLA Modules:
  0.0 175.8 jit_solution(12320816737499635514)
XLA Ops:
  0.6 7.4 %share_ids.1.ids_ref = s32[4,1,256]{2,1,0:T(1,128)} custom-call(s32[1,256]{1,0:T(1,128)} %ids_ref.1), custom_call_target="tpu_custom_call" | custom-call | tf_op jit(solution)/shard_map/share_ids/pallas_call | solution.py:1009
  8.0 0.7 subtract_clamp_fusion
  8.7 13.7 %gather_fusion = bf16[1024,1024]{1,0:T(8,128)(2,1)} fusion(bf16[7632,1024]{1,0:T(8,128)(2,1)} %param.12, s32[1024]{0:T(1024)S(1)} %broadcast_clamp_fusion), kind=kCustom, calls=%fused_computation | custom fusion | bytes 4198400 | tf_op jit(solution)/shard_map/gather | solution.py:2088
  23.1 69.7 %front.1 = (bf16[4,256,1024]{2,1,0:T(8,128)(2,1)}, bf16[4,256,1024]{2,1,0:T(8,128)(2,1)}, bf16[3,256,1024]{2,1,0:T(8,128)(2,1)}, bf16[4,256,1024]{2,1,0:T(8,128)...) custom-call(s32[1]{0:T(128)S(6)} %copy.15.length_ref, ...), custom_call_target="tpu_custom_call" | custom-call | tf_op jit(solution)/shard_map/front/pallas_call | solution.py:1325
  93.4 79.8 %finish.1 = (f32[3,128,256]{2,1,0:T(8,128)}, f32[256,128]{1,0:T(8,128)}, f32[128,1024]{1,0:T(8,128)}, f32[1024,128]{1,0:T(8,128)}, f32[128,128]{1,0:T(8,128)}, /*index=5*/f32[1,128]{1,0:T(1,128)}) custom-call(s32[1]{0:T(128)S(6)} %copy.15.length_ref, s32[1]{0:T(128)S(6)} %copy.16.bin_ref, bf16[1024,128]{1,0:T(8,128)(2,1)} %get-tuple-element.27.top_ref, ...), custom_call_target="tpu_custom_call" | custom-call | tf_op jit(solution)/shard_map/finish/pallas_call | solution.py:1963
  173.3 2.6 %hand_over.1 = (f32[3,128,256]{2,1,0:T(8,128)}, f32[256,128]{1,0:T(8,128)}, f32[128,1024]{1,0:T(8,128)}, f32[1024,128]{1,0:T(8,128)}, f32[128,128]{1,0:T(8,128)}, /*index=5*/f32[1,128]{1,0:T(1,128)}) custom-call(f32[3,128,256]{2,1,0:T(8,128)} %get-tuple-element.36.refs_0_, f32[256,128]{1,0:T(8,128)} %get-tuple-element.37.refs_1_, ...), custom_call_target="tpu_custom_call" | custom-call | tf_op jit(solution)/shard_map/hand_over/pallas_call | solution.py:2057
  (2 shorter events, 0.0 us)
